TPU v7x, 16 devices: a whole 2x2x2 slice. The times are simulated.
16 devices in a mesh: dp: 16 (over z, y, x, core).
Axes of the slice: x: 2, y: 2, z: 2, core: 2. Of those that a mesh axis runs over, the one named last changes fastest.
Arguments:
- tokens: bfloat16 [4096, 128], P('dp')
- w_one: bfloat16 [128, 512], replicated
- w_two: bfloat16 [512, 128], replicated
- wi_one: bfloat16 [128, 512], replicated
- wi_two: bfloat16 [512, 128], replicated
- item_table: bfloat16 [524288, 128], P('dp')
- cand_ids: int32 [16384], replicated
- log_q: float32 [16384], replicated
- targets: int32 [4096], P('dp')
Outputs:
- output 1: float32 [], replicated
- output 2: float32 [524288, 128], P('dp')
- output 3: float32 [128, 512], replicated
- output 4: float32 [512, 128], replicated
- output 5: float32 [128, 512], replicated
- output 6: float32 [512, 128], replicated
All inputs are finite; a program needn't handle non-finite values.
Results may differ from a plain program's by a relative error of at most 0.011364.
Values are sent between devices in bfloat16 or wider.
A program may use at most 1 GiB of HBM per device.

v0:
```python
import math
import jax
import jax.numpy as jnp
from jax import lax
from jax.sharding import PartitionSpec as P

SCORE_GAIN = 3.0
HIT_VALUE = -1e9


def tower_fwd(row_block, w_in, w_out):
    pre_act = jnp.dot(row_block, w_in, preferred_element_type=jnp.float32)
    hidden = jax.nn.gelu(pre_act).astype(jnp.bfloat16)
    tower_out = jnp.dot(hidden, w_out, preferred_element_type=jnp.float32).astype(jnp.bfloat16)
    return pre_act, hidden, tower_out


def tower_back(row_block, w_out, pre_act, hidden, grad_out):
    dw_out = jnp.einsum("nf,nd->fd", hidden, grad_out, preferred_element_type=jnp.float32)
    grad_hidden = jnp.einsum("nd,fd->nf", grad_out, w_out, preferred_element_type=jnp.float32)
    gelu_back = jax.vjp(jax.nn.gelu, pre_act)[1]
    grad_pre = gelu_back(grad_hidden)[0].astype(jnp.bfloat16)
    dw_in = jnp.einsum("ne,nf->ef", row_block, grad_pre, preferred_element_type=jnp.float32)
    return grad_pre, dw_in, dw_out


def owned_rows(table_loc, row_ids, row_base):
    local_ids = row_ids - row_base
    num_rows = table_loc.shape[0]
    is_owned = (local_ids >= 0) & (local_ids < num_rows)
    picked = jnp.take(table_loc, jnp.clip(local_ids, 0, num_rows - 1), axis=0)
    return jnp.where(is_owned[:, None], picked, 0)


def loss_grads(query, targ_vec, cand_vec, log_q, targ_ids, cand_ids, tok_total):
    logit_scale = SCORE_GAIN / math.sqrt(query.shape[1])
    z_targ = jnp.einsum("td,td->t", query, targ_vec, preferred_element_type=jnp.float32) * logit_scale
    z_cand = jnp.einsum("td,sd->ts", query, cand_vec, preferred_element_type=jnp.float32) * logit_scale - log_q[None, :]
    z_cand = jnp.where(targ_ids[:, None] == cand_ids[None, :], HIT_VALUE, z_cand)
    row_max = jnp.maximum(z_targ, jnp.max(z_cand, axis=1))
    e_targ = jnp.exp(z_targ - row_max)
    e_cand = jnp.exp(z_cand - row_max[:, None])
    denom_sum = e_targ + jnp.sum(e_cand, axis=1)
    loss_sum = jnp.sum(jnp.log(denom_sum) + row_max - z_targ)
    dz_targ = ((e_targ / denom_sum - 1.0) / tok_total).astype(jnp.bfloat16).astype(jnp.float32)
    dz_cand = (e_cand / denom_sum[:, None] / tok_total).astype(jnp.bfloat16)
    d_query = ((dz_targ[:, None] * targ_vec.astype(jnp.float32) + jnp.einsum("ts,sd->td", dz_cand, cand_vec, preferred_element_type=jnp.float32)) * logit_scale).astype(jnp.bfloat16)
    d_targ_vec = (logit_scale * dz_targ[:, None] * query.astype(jnp.float32)).astype(jnp.bfloat16)
    return loss_sum, d_query, d_targ_vec, dz_cand, logit_scale


def solution(mesh):
    num_dev = mesh.shape["dp"]

    def local_step(tokens, w_one, w_two, wi_one, wi_two, table_loc, cand_ids, log_q, targ_loc):
        my_index = lax.axis_index("dp")
        rows_loc = table_loc.shape[0]
        row_base = my_index * rows_loc
        tok_total = tokens.shape[0] * num_dev
        cand_mine = lax.psum_scatter(owned_rows(table_loc, cand_ids, row_base), "dp", scatter_dimension=0, tiled=True)
        c_pre, c_hidden, cand_vec_mine = tower_fwd(cand_mine, wi_one, wi_two)
        cand_vec = lax.all_gather(cand_vec_mine, "dp", axis=0, tiled=True)
        targ_all = lax.all_gather(targ_loc, "dp", axis=0, tiled=True)
        targ_raw = lax.psum_scatter(owned_rows(table_loc, targ_all, row_base), "dp", scatter_dimension=0, tiled=True)
        t_pre, t_hidden, targ_vec = tower_fwd(targ_raw, wi_one, wi_two)
        q_pre, q_hidden, query = tower_fwd(tokens, w_one, w_two)
        loss_sum, d_query, d_targ_vec, dz_cand, logit_scale = loss_grads(query, targ_vec, cand_vec, log_q, targ_loc, cand_ids, tok_total)
        d_cand_part = jnp.einsum("ts,td->sd", dz_cand, query, preferred_element_type=jnp.float32)
        d_cand_vec = (lax.psum_scatter(d_cand_part, "dp", scatter_dimension=0, tiled=True) * logit_scale).astype(jnp.bfloat16)
        dw_one, dw_two = tower_back(tokens, w_two, q_pre, q_hidden, d_query)[1:]
        t_grad_pre, dwi_one_t, dwi_two_t = tower_back(targ_raw, wi_two, t_pre, t_hidden, d_targ_vec)
        c_grad_pre, dwi_one_c, dwi_two_c = tower_back(cand_mine, wi_two, c_pre, c_hidden, d_cand_vec)
        d_targ_raw = jnp.einsum("nf,df->nd", t_grad_pre, wi_one, preferred_element_type=jnp.float32).astype(jnp.bfloat16)
        d_cand_raw = jnp.einsum("nf,df->nd", c_grad_pre, wi_one, preferred_element_type=jnp.float32).astype(jnp.bfloat16)
        weight_grads = lax.psum((dw_one, dw_two, dwi_one_t + dwi_one_c, dwi_two_t + dwi_two_c), "dp")
        back_cand = lax.all_gather(d_cand_raw, "dp", axis=0, tiled=True)
        back_targ = lax.all_gather(d_targ_raw, "dp", axis=0, tiled=True)
        local_ids = jnp.concatenate([cand_ids, targ_all]) - row_base
        local_ids = jnp.where((local_ids >= 0) & (local_ids < rows_loc), local_ids, rows_loc)
        d_table = jax.ops.segment_sum(jnp.concatenate([back_cand, back_targ]).astype(jnp.float32), local_ids, num_segments=rows_loc)
        loss = lax.psum(loss_sum, "dp") / tok_total
        return (loss, d_table) + tuple(weight_grads)

    return jax.shard_map(local_step, mesh=mesh, in_specs=(P("dp", None), P(), P(), P(), P(), P("dp", None), P(), P(), P("dp")), out_specs=(P(), P("dp", None), P(), P(), P(), P()), check_vma=False)
```

profile of v0, /device:TPU:0, one launch (start us, length us, event | category | flops | bytes accessed | tf_op | source)
XLA Modules:
  0.0 639.8 jit_solution(11846216420025807794)
XLA Ops:
  7.2 0.0 copy-start
  7.2 0.0 reduce-scatter.6.cloned.1.call-start
  7.2 0.9 compare_and_fusion.1
  8.2 0.9 fusion.45
  9.0 60.1 %gather_fusion.1 = bf16[16384,128]{1,0:T(8,128)(2,1)} fusion(bf16[32768,128]{1,0:T(8,128)(2,1)} %param.14, s32[16384]{0:T(1024)S(1)} %fusion.45), kind=kCustom, calls=%fused_computation.1 | custom fusion | bytes 8454144 | tf_op jit(solution)/shard_map/jit(_take)/gather | solution.py:31
  69.2 13.9 %select_select_fusion = bf16[16384,128]{1,0:T(8,128)(2,1)} fusion(bf16[16384,128]{1,0:T(8,128)(2,1)} %gather_fusion.1, pred[16384]{0:T(1024)(128)(4,1)S(1)} %get-tuple-element.31, pred[16384]{0:T(1024)(128)(4,1)S(1)} %get-tuple-element.30), kind=kLoop, calls=%fused_computation.15 | loop fusion | flops 4194304 | bytes 8421376 | tf_op jit(solution)/shard_map/jit(_where)/select_n | solution.py:32
  83.1 0.0 reduce-scatter.6.cloned.1.call-update
  83.1 0.0 reduce-scatter.4.cloned.1.call-start
  83.2 0.6 copy-done.10
  83.8 15.0 %all-gather = s32[16,1,256]{2,1,0:T(1,128)S(1)} all-gather(s32[1,1,256]{2,1,0:T(1,128)S(1)} %bitcast.45), channel_id=1, replica_groups=mesh['dp'=16] {'dp'}, dimensions={0}, use_global_device_ids=true | all-gather | bytes 17408 | tf_op jit(solution)/shard_map/all_gather | solution.py:63
  98.8 15.5 %gather_fusion = bf16[4096,128]{1,0:T(8,128)(2,1)S(1)} fusion(bf16[32768,128]{1,0:T(8,128)(2,1)} %param.14, s32[4096]{0:T(1024)S(1)} %fusion.48), kind=kCustom, calls=%fused_computation | custom fusion | bytes 2113536 | tf_op jit(solution)/shard_map/jit(_take)/gather | solution.py:31
  114.3 0.1 and_reduce_fusion
  114.4 0.0 copy-start.9
  114.4 2.5 select_select_fusion.1
  116.9 0.0 reduce-scatter.4.cloned.1.call-update
  116.9 0.0 copy-start.8
  116.9 0.0 all-gather.5.cloned.1.call-start
  117.0 32.8 %reduce-scatter.6.cloned.1.call-done = bf16[1024,128]{1,0:T(8,128)(2,1)} async-done(((bf16[16384,128]{1,0:T(8,128)(2,1)}), bf16[1024,128]{1,0:T(8,128)(2,1)}) %reduce-scatter.6.cloned.1.call-update) | async-done | bytes 262160 | tf_op jit(solution)/shard_map/reduce_scatter | solution.py:60
  149.8 3.0 multiply_convert_fusion.1
  152.8 1.1 convolution_convert_fusion.1
  153.9 0.0 all-gather.5.cloned.1.call-update
  153.9 0.2 reduce-scatter.8.cloned.1.call-start
  154.2 0.3 multiply_convert_fusion.4
  154.5 0.2 convolution_convert_fusion.4
  154.7 52.0 %reduce-scatter.4.cloned.1.call-done = bf16[256,128]{1,0:T(8,128)(2,1)} async-done(((bf16[4096,128]{1,0:T(8,128)(2,1)}), bf16[256,128]{1,0:T(8,128)(2,1)}) %reduce-scatter.4.cloned.1.call-update) | async-done | bytes 65552 | tf_op jit(solution)/shard_map/reduce_scatter | solution.py:64
  206.7 1.0 fusion.61
  207.7 0.4 fusion.42
  208.1 34.9 %all-gather.5.cloned.1.call-done = bf16[16384,128]{1,0:T(8,128)(2,1)} async-done(((bf16[1024,128]{1,0:T(8,128)(2,1)}), bf16[16384,128]{1,0:T(8,128)(2,1)}) %all-gather.5.cloned.1.call-update) | async-done | bytes 4194320 | tf_op jit(solution)/shard_map/all_gather | solution.py:62
  243.0 0.0 copy-done.12
  243.0 10.4 %fusion.60 = (f32[256]{0:T(256)S(1)}, f32[256,16384]{1,0:T(8,128)}) fusion(f32[16384]{0:T(1024)S(1)} %copy-done.12, bf16[256,128]{1,0:T(8,128)(2,1)S(1)} %convolution_convert_fusion.4, bf16[16384,128]{1,0:T(8,128)(2,1)} %all-gather.5.cloned.1.call-done, s32[16384]{0:T(1024)S(1)} %copy-done.2, s32[256]{0:T(256)S(1)} %copy-done.10), kind=kOutput, calls=%fused_computation.99 | convolution fusion | flops 1094713088 | bytes 21170176 | tf_op jit(solution)/shard_map/td,sd->ts/dot_general | solution.py:38
  253.5 8.1 %fusion.2 = f32[256]{0:T(256)S(1)} fusion(f32[256,16384]{1,0:T(8,128)} %get-tuple-element.41, f32[256]{0:T(256)S(1)} %multiply_maximum_fusion), kind=kLoop, calls=%fused_computation.8 | loop fusion | flops 8388352 | bytes 16779264 | tf_op jit(solution)/shard_map/reduce_sum | solution.py:43
  261.6 0.6 fusion.58
  262.2 7.6 %multiply_convert_fusion = bf16[256,16384]{1,0:T(8,128)(2,1)S(1)} fusion(f32[256,16384]{1,0:T(8,128)} %get-tuple-element.41, f32[256]{0:T(256)S(1)} %get-tuple-element.32, f32[256]{0:T(256)S(1)} %multiply_maximum_fusion), kind=kLoop, calls=%fused_computation.6 | loop fusion | flops 16777216 | bytes 25167872 | tf_op jit(solution)/shard_map/convert_element_type | solution.py:46
  269.8 3.2 copy-done.1
  273.0 5.8 fusion.62
  278.8 0.0 reduce-scatter.8.cloned.1.call-update
  278.9 0.3 all-reduce.3.cloned.1.call-start
  279.1 6.9 %fusion.17 = bf16[256,128]{1,0:T(8,128)(2,1)S(1)} fusion(bf16[256,16384]{1,0:T(8,128)(2,1)} %copy-done.1, bf16[16384,128]{1,0:T(8,128)(2,1)} %all-gather.5.cloned.1.call-done, f32[256,128]{1,0:T(8,128)S(1)} %get-tuple-element.43, f32[256]{0:T(256)S(1)} %get-tuple-element.35), kind=kOutput, calls=%fused_computation.33 | convolution fusion | flops 1073872896 | bytes 12780544 | tf_op jit(solution)/shard_map/ts,sd->td/dot_general | solution.py:47
  286.1 1.0 fusion.63
  287.0 0.5 fusion.32
  287.5 1.4 convolution_bitcast_fusion
  288.9 82.9 %reduce-scatter.8.cloned.1.call-done = f32[1024,128]{1,0:T(8,128)} async-done(((f32[16384,128]{1,0:T(8,128)}), f32[1024,128]{1,0:T(8,128)}) %reduce-scatter.8.cloned.1.call-update) | async-done | bytes 524304 | tf_op jit(solution)/shard_map/reduce_scatter | solution.py:69
  371.8 1.5 fusion.44
  373.3 1.1 convolution_add_fusion
  374.4 3.3 fusion.15
  377.7 0.3 fusion.64
  378.1 0.9 convolution_add_fusion.1
  379.0 0.0 all-reduce.3.cloned.1.call-update
  379.0 0.0 all-gather.9.cloned.1.call-start
  379.1 0.9 convolution_convert_fusion.2
  379.9 0.0 all-gather.9.cloned.1.call-update
  380.0 0.0 all-gather.7.cloned.1.call-start
  380.0 1.1 convolution_convert_fusion
  381.1 0.0 all-gather.7.cloned.1.call-update
  381.2 0.1 and_select_fusion
  381.3 31.2 %psum.35 = f32[]{:T(128)} all-reduce(f32[]{:T(128)} %get-tuple-element.33), channel_id=1, replica_groups=mesh['dp'=16] {'dp'}, use_global_device_ids=true, to_apply=%region_5.6 | all-reduce | flops 1 | bytes 8 | tf_op jit(solution)/shard_map/psum | solution.py:81
  413.1 32.8 %all-reduce.3.cloned.1.call-done = (f32[128,512]{0,1:T(8,128)}, f32[512,128]{1,0:T(8,128)}, f32[128,512]{1,0:T(8,128)}, f32[512,128]{1,0:T(8,128)}) async-done(((f32[128,512]{0,1:T(8,128)}, f32[512,128]{1,0:T(8,128)}, f32[128,512]{1,0:T(8,128)}, f32[512,128]{1,0:T(8,128)}), (f32[128,512]{0,1:T(8,128)}, f32[512,128]{1,0:T(8,128)}, f32[128,512]{1,0:T(8,128)}, ...) | async-done | bytes 1048592 | tf_op jit(solution)/shard_map/psum | solution.py:75
  445.9 1.8 copy.18
  447.7 24.2 %all-gather.9.cloned.1.call-done = bf16[4096,128]{1,0:T(8,128)(2,1)} async-done(((bf16[256,128]{1,0:T(8,128)(2,1)}), bf16[4096,128]{1,0:T(8,128)(2,1)}) %all-gather.9.cloned.1.call-update) | async-done | bytes 1048592 | tf_op jit(solution)/shard_map/all_gather | solution.py:77
  471.9 37.9 %all-gather.7.cloned.1.call-done = bf16[16384,128]{1,0:T(8,128)(2,1)} async-done(((bf16[1024,128]{1,0:T(8,128)(2,1)}), bf16[16384,128]{1,0:T(8,128)(2,1)}) %all-gather.7.cloned.1.call-update) | async-done | bytes 4194320 | tf_op jit(solution)/shard_map/all_gather | solution.py:76
  509.8 119.9 %scatter_custom_fusion = f32[32768,128]{1,0:T(8,128)} fusion(s32[20480]{0:T(1024)S(1)} %bitcast.44, f32[]{:T(128)} %constant.34.clone.1, bf16[4096,128]{1,0:T(8,128)(2,1)} %all-gather.9.cloned.1.call-done, bf16[]{:T(256)} %constant.47, bf16[16384,128]{1,0:T(8,128)(2,1)} %all-gather.7.cloned.1.call-done), kind=kCustom, calls=%fused_computation.9 | custom fusion | flops 13107200 | bytes 22020102 | tf_op jit(solution)/shard_map/scatter-add | solution.py:80
  629.7 0.7 copy.28
  630.4 0.7 copy.29
  631.1 0.7 copy.30
  (27 shorter events, 0.1 us)
Async XLA Ops:
  7.2 142.6 %copy-start = (bf16[128,512]{1,0:T(8,128)(2,1)S(1)}, bf16[128,512]{1,0:T(8,128)(2,1)}, u32[]{:S(2)}) copy-start(bf16[128,512]{1,0:T(8,128)(2,1)} %param.12) | copy-start | bytes 393220
  7.2 142.6 %reduce-scatter.6.cloned.1.call-start = ((), (), s32[]{:S(2)}) async-start(), calls=%async_computation.4 | async-start | bytes 4456448 | tf_op jit(solution)/shard_map/reduce_scatter | solution.py:60
  83.1 0.7 copy-start.10
  83.1 123.6 %reduce-scatter.4.cloned.1.call-start = ((), (), s32[]{:S(2)}) async-start(), calls=%async_computation.3 | async-start | bytes 1114112 | tf_op jit(solution)/shard_map/reduce_scatter | solution.py:64
  114.4 38.4 %copy-start.9 = (bf16[512,128]{1,0:T(8,128)(2,1)S(1)}, bf16[512,128]{1,0:T(8,128)(2,1)}, u32[]{:S(2)}) copy-start(bf16[512,128]{1,0:T(8,128)(2,1)} %param.13) | copy-start | bytes 393220
  116.9 37.3 %copy-start.11 = (bf16[128,512]{1,0:T(8,128)(2,1)S(1)}, bf16[128,512]{1,0:T(8,128)(2,1)}, u32[]{:S(2)}) copy-start(bf16[128,512]{1,0:T(8,128)(2,1)} %param.10) | copy-start | bytes 393220
  116.9 37.3 %copy-start.13 = (bf16[256,128]{1,0:T(8,128)(2,1)S(1)}, bf16[256,128]{1,0:T(8,128)(2,1)}, u32[]{:S(2)}) copy-start(bf16[256,128]{1,0:T(8,128)(2,1)} %param.9) | copy-start | bytes 196612
  116.9 37.6 %copy-start.8 = (bf16[512,128]{1,0:T(8,128)(2,1)S(1)}, bf16[512,128]{1,0:T(8,128)(2,1)}, u32[]{:S(2)}) copy-start(bf16[512,128]{1,0:T(8,128)(2,1)} %param.11) | copy-start | bytes 393220
  116.9 126.1 %all-gather.5.cloned.1.call-start = ((), (), s32[]{:S(2)}) async-start(), calls=%async_computation.5 | async-start | bytes 4456448 | tf_op jit(solution)/shard_map/all_gather | solution.py:62
  152.8 90.3 %copy-start.2 = (s32[16384]{0:T(1024)S(1)}, s32[16384]{0:T(1024)}, u32[]{:S(2)}) copy-start(s32[16384]{0:T(1024)} %param.15) | copy-start | bytes 196612
  152.8 90.3 %copy-start.12 = (f32[16384]{0:T(1024)S(1)}, f32[16384]{0:T(1024)}, u32[]{:S(2)}) copy-start(f32[16384]{0:T(1024)} %param.16) | copy-start | bytes 196612
  153.9 217.8 %reduce-scatter.8.cloned.1.call-start = ((), (), s32[]{:S(2)}) async-start(), calls=%async_computation.6 | async-start | bytes 8912896 | tf_op jit(solution)/shard_map/reduce_scatter | solution.py:69
  269.8 3.2 copy-start.1
  278.9 167.1 %all-reduce.3.cloned.1.call-start = ((), (), s32[]{:S(2)}) async-start(), calls=%async_computation.9 | async-start | bytes 2097152 | tf_op jit(solution)/shard_map/psum | solution.py:75
  374.4 3.4 copy-start.6
  374.4 3.7 copy-start.7
  379.0 92.9 %all-gather.9.cloned.1.call-start = ((), (), s32[]{:S(2)}) async-start(), calls=%async_computation.8 | async-start | bytes 1114112 | tf_op jit(solution)/shard_map/all_gather | solution.py:77
  380.0 129.8 %all-gather.7.cloned.1.call-start = ((), (), s32[]{:S(2)}) async-start(), calls=%async_computation.7 | async-start | bytes 4456448 | tf_op jit(solution)/shard_map/all_gather | solution.py:76
  509.8 119.9 %copy-start.5 = (f32[512,128]{1,0:T(8,128)S(1)}, f32[512,128]{1,0:T(8,128)}, u32[]{:S(2)}) copy-start(f32[512,128]{1,0:T(8,128)} %get-tuple-element.47) | copy-start | bytes 786436
  509.8 120.6 %copy-start.4 = (f32[128,512]{1,0:T(8,128)S(1)}, f32[128,512]{1,0:T(8,128)}, u32[]{:S(2)}) copy-start(f32[128,512]{1,0:T(8,128)} %get-tuple-element.48) | copy-start | bytes 786436
  509.8 121.3 %copy-start.3 = (f32[512,128]{1,0:T(8,128)S(1)}, f32[512,128]{1,0:T(8,128)}, u32[]{:S(2)}) copy-start(f32[512,128]{1,0:T(8,128)} %get-tuple-element.49) | copy-start | bytes 786436
Sparse Core Ops, SparseCore 0:
  83.2 66.5 reduce-scatter.5
  152.0 54.6 reduce-scatter.3
  209.5 33.4 all-gather.4
  279.0 92.7 reduce-scatter.7
  379.1 66.7 all-reduce.2
  448.0 23.8 all-gather.8
  474.7 35.0 all-gather.6
where the time goes:
time: 640 us
  waiting for transfers between devices  298 us (47%)
  other arithmetic  155 us (24%)
  local copies, waits for them, and re-layouts  83.4 us (13%)
  blocking collectives  46.2 us (7%)
  matrix products  41.2 us (6%)
  between operations  16.1 us (3%)
    scatter-add x1, other arithmetic, local_step(): jax.ops.segment_sum(jnp.concatenate([back_cand, back_targ]).astype(jnp.fl...  120 us
    reduce_scatter x1, waiting for transfers between devices, local_step(): lax.psum_scatter(d_cand_part, 'dp', scatter_dimension=0, tiled=True)  82.9 us
    gather x2, local copies, waits for them, and re-layouts, owned_rows(): picked = jnp.take(table_loc, jnp.clip(local_ids, 0, num_rows - 1), axis=0)  75.6 us
    reduce_scatter x1, waiting for transfers between devices, local_step(): lax.psum_scatter(owned_rows(table_loc, targ_all, row_base), 'dp', scatter...  52 us
    all_gather x1, waiting for transfers between devices, local_step(): back_cand = lax.all_gather(d_cand_raw, 'dp', axis=0, tiled=True)  37.9 us
    all_gather x1, waiting for transfers between devices, local_step(): cand_vec = lax.all_gather(cand_vec_mine, 'dp', axis=0, tiled=True)  34.9 us
    psum x1, waiting for transfers between devices, local_step(): lax.psum((dw_one, dw_two, dwi_one_t + dwi_one_c, dwi_two_t + dwi_two_c),...  32.8 us
    reduce_scatter x1, waiting for transfers between devices, local_step(): lax.psum_scatter(owned_rows(table_loc, cand_ids, row_base), 'dp', scatter...  32.8 us
  transfers between devices with their start and end apart: 7, of which 7 were waited for; matrix products, arithmetic and copies ran while one was open for 6% of the time, Pallas kernels for 0%

commit v1 on v0

v1 whole, which is shorter than its diff:
```python
import functools
import math
import jax
import jax.numpy as jnp
from jax import lax
from jax.experimental import pallas as pl
from jax.experimental.pallas import tpu as pltpu
from jax.sharding import PartitionSpec as P

SCORE_GAIN = 3.0
HIT_VALUE = -1e9
LANES = 128
VMEM_CAP = 60 * 1024 * 1024
BF = jnp.bfloat16
F32 = jnp.float32
I32 = jnp.int32
VM = pl.BlockSpec(memory_space=pltpu.VMEM)
SM = pl.BlockSpec(memory_space=pltpu.SMEM)
HB = pl.BlockSpec(memory_space=pl.ANY)
BLK = 256


def compact(loc, num_rows):
    nr = loc.shape[0]
    own = jnp.where((loc >= 0) & (loc < num_rows), 1.0, 0.0)
    own16 = own.astype(BF)
    tri = jnp.where(lax.broadcasted_iota(I32, (LANES, LANES), 0) < lax.broadcasted_iota(I32, (LANES, LANES), 1), 1.0, 0.0).astype(BF)
    within = jnp.dot(own16, tri, preferred_element_type=F32)
    low = jnp.where(lax.broadcasted_iota(I32, (nr, nr), 1) < lax.broadcasted_iota(I32, (nr, nr), 0), 1.0, 0.0).astype(BF)
    before = jnp.sum(jnp.dot(low, own16, preferred_element_type=F32), axis=1, keepdims=True)
    lane = lax.broadcasted_iota(I32, (nr, LANES), 1)
    flat = lax.broadcasted_iota(I32, (nr, LANES), 0) * LANES + lane
    disp = flat - (within + before).astype(I32)
    val = jnp.where(own > 0, flat * 32768 + loc, -1)
    total = jnp.sum(own).astype(I32)

    def back(x, s):
        if s >= LANES:
            return pltpu.roll(x, nr - s // LANES, axis=0)
        here = pltpu.roll(x, LANES - s, axis=1)
        return jnp.where(lane < LANES - s, here, pltpu.roll(here, nr - 1, axis=0))

    bit = 0
    while (1 << bit) < nr * LANES:
        val_b, disp_b = back(val, 1 << bit), back(disp, 1 << bit)
        take = (val_b >= 0) & (((disp_b >> bit) & 1) == 1)
        stay = ((disp >> bit) & 1) == 0
        val = jnp.where(take, val_b, jnp.where(stay, val, -1))
        disp = jnp.where(take, disp_b, disp)
        bit += 1
    return jnp.where(flat < total, val, nr * LANES * 32768), own, total


def gather_kernel(chunks, head, base_ref, ids_ref, table_ref, out_ref, list_ref, cnt_ref, stage, tab, dense, plist, sem, psem):
    rows = tab.shape[0]
    npos = out_ref.shape[0]
    cr = rows // chunks

    def load(c):
        return pltpu.make_async_copy(table_ref.at[pl.ds(c * cr, cr), :], stage.at[pl.ds(c * cr, cr), :], sem.at[c])

    for c in range(chunks):
        load(c).start()
    packed, own, total = compact(ids_ref[...] - base_ref[0], rows)
    list_ref[...] = packed
    cnt_ref[0] = jnp.sum(own[:head // LANES]).astype(I32)
    cnt_ref[1] = total
    to_smem = pltpu.make_async_copy(list_ref, plist, psem)
    to_smem.start()

    def zero(i, _):
        dense[pl.ds(pl.multiple_of(i * BLK, BLK), BLK), :] = jnp.zeros((BLK, LANES), F32)
        return 0

    lax.fori_loop(0, npos // BLK, zero, 0)
    for c in range(chunks):
        load(c).wait()

        def conv(i, _, c=c):
            s = pl.ds(pl.multiple_of(c * cr + i * BLK, BLK), BLK)
            tab[s, :] = stage[s, :].astype(F32)
            return 0

        lax.fori_loop(0, cr // BLK, conv, 0)
    to_smem.wait()

    def pick(i, _):
        vals = []
        for u in range(LANES):
            w = plist[i, u]
            vals.append((w >> 15, tab[pl.ds(w & 32767, 1), :]))
        for p, v in vals:
            dense[pl.ds(p, 1), :] = v
        return 0

    lax.fori_loop(0, (total + LANES - 1) // LANES, pick, 0)

    def pack(i, _):
        s = pl.ds(pl.multiple_of(i * BLK, BLK), BLK)
        out_ref[s, :] = dense[s, :].astype(BF)
        return 0

    lax.fori_loop(0, npos // BLK, pack, 0)


def gather(table, ids, base, head):
    rows = table.shape[0]
    nr = ids.shape[0]
    npos = nr * LANES
    chunks = 8
    return pl.pallas_call(
        functools.partial(gather_kernel, chunks, head),
        out_shape=(jax.ShapeDtypeStruct((npos, LANES), BF), jax.ShapeDtypeStruct((nr, LANES), I32), jax.ShapeDtypeStruct((2,), I32)),
        in_specs=[SM, VM, HB],
        out_specs=(VM, VM, SM),
        scratch_shapes=[pltpu.VMEM((rows, LANES), BF), pltpu.VMEM((rows, LANES), F32), pltpu.VMEM((npos + 8, LANES), F32), pltpu.SMEM((nr, LANES), I32), pltpu.SemaphoreType.DMA((chunks,)), pltpu.SemaphoreType.DMA],
        compiler_params=pltpu.CompilerParams(vmem_limit_bytes=VMEM_CAP),
        name="gather_rows",
    )(base, ids, table)


ADDS = 4


def scatter_kernel(chunks, cnt_ref, list_ref, grad_ref, out_ref, acc, grad, plist, sem, psem):
    rows = out_ref.shape[0]
    npos = grad_ref.shape[0]
    to_smem = pltpu.make_async_copy(list_ref, plist, psem)
    to_smem.start()

    def zero(i, _):
        acc[pl.ds(pl.multiple_of(i * BLK, BLK), BLK), :] = jnp.zeros((BLK, LANES), F32)
        return 0

    lax.fori_loop(0, rows // BLK, zero, 0)

    def conv(i, _):
        s = pl.ds(pl.multiple_of(i * BLK, BLK), BLK)
        grad[s, :] = grad_ref[s, :].astype(F32)
        return 0

    lax.fori_loop(0, npos // BLK, conv, 0)
    grad[npos:, :] = jnp.zeros((8, LANES), F32)
    to_smem.wait()
    nhead = cnt_ref[0]
    total = cnt_ref[1]

    def put(i, _):
        vals = []
        for u in range(LANES):
            w = plist[i, u]
            vals.append((w & 32767, grad[pl.ds(w >> 15, 1), :]))
        for r, v in vals:
            acc[pl.ds(r, 1), :] = v
        return 0

    lax.fori_loop(0, nhead // LANES, put, 0)

    def add_one(i, _):
        w = plist[i >> 7, i & 127]
        r = pl.ds(w & 32767, 1)
        acc[r, :] = acc[r, :] + grad[pl.ds(w >> 15, 1), :]
        return 0

    def add_row(i, _):
        for j in range(0, LANES, ADDS):
            words = [plist[i, j + u] for u in range(ADDS)]
            rs = [w & 32767 for w in words]
            gs = [grad[pl.ds(w >> 15, 1), :] for w in words]
            outs = []
            for u in range(ADDS):
                v = acc[pl.ds(rs[u], 1), :] + gs[u]
                for t in range(u):
                    v = v + jnp.where(rs[t] == rs[u], gs[t], 0.0)
                outs.append(v)
            for u in range(ADDS):
                acc[pl.ds(rs[u], 1), :] = outs[u]
        return 0

    begin = nhead // LANES * LANES
    split = jnp.minimum((nhead + LANES - 1) // LANES * LANES, total)
    lax.fori_loop(begin, split, add_one, 0)
    lax.fori_loop((split + LANES - 1) // LANES, (total + LANES - 1) // LANES, add_row, 0)
    cr = rows // chunks

    def store(c):
        return pltpu.make_async_copy(acc.at[pl.ds(c * cr, cr), :], out_ref.at[pl.ds(c * cr, cr), :], sem.at[c])

    for c in range(chunks):
        store(c).start()
    for c in range(chunks):
        store(c).wait()


def scatter(grads, plist, counts, rows):
    nr = plist.shape[0]
    npos = nr * LANES
    chunks = 8
    return pl.pallas_call(
        functools.partial(scatter_kernel, chunks),
        out_shape=jax.ShapeDtypeStruct((rows, LANES), F32),
        in_specs=[SM, HB, VM],
        out_specs=HB,
        scratch_shapes=[pltpu.VMEM((rows, LANES), F32), pltpu.VMEM((npos + 8, LANES), F32), pltpu.SMEM((nr, LANES), I32), pltpu.SemaphoreType.DMA((chunks,)), pltpu.SemaphoreType.DMA],
        compiler_params=pltpu.CompilerParams(vmem_limit_bytes=VMEM_CAP),
        name="scatter_rows",
    )(counts, plist, grads)


MESHID = pl.DeviceIdType.MESH
CHIP_DIMS = (1, 2, 4)
SLOTS = tuple(range(8))


def place():
    me = lax.axis_index("dp")
    core = lax.rem(me, 2)
    chip = me // 2
    sign = {d: 1 - 2 * lax.rem(chip // d, 2) for d in CHIP_DIMS}
    return me, core, chip, sign


def chip_at(chip, sign, s):
    for d in CHIP_DIMS:
        if s & d:
            chip = chip + d * sign[d]
    return chip


def enter():
    me, core, chip, sign = place()
    barrier = pltpu.get_barrier_semaphore()
    peers = [me + 1 - 2 * core] + [2 * chip_at(chip, sign, d) + core for d in CHIP_DIMS]
    for peer in peers:
        pl.semaphore_signal(barrier, inc=1, device_id=(peer,), device_id_type=MESHID)
    pl.semaphore_wait(barrier, len(peers))


def order_of(k):
    return tuple(CHIP_DIMS[(k + i) % 3] for i in range(3))


def pieces_of(rows, unit):
    base = rows // unit
    cuts = [(base * i // 3) * unit for i in range(4)]
    return [(cuts[i], cuts[i + 1] - cuts[i]) for i in range(3)]


def remote(src, dst, send, recv, peer):
    return pltpu.make_async_remote_copy(src_ref=src, dst_ref=dst, send_sem=send, recv_sem=recv, device_id=(peer,), device_id_type=MESHID)


CORE_ORDER = (7, 3, 5, 6, 1, 2, 4, 0)


def stage_slots(k, t):
    dims = order_of(k)
    live = [s for s in SLOTS if all(not s & d for d in dims[:t])]
    return [(s, s ^ dims[t]) for s in live if s & dims[t]]


RS_BASE = (0, 4, 6)


def rs_scratch(rows, dtype):
    return [
        pltpu.VMEM((8, rows, LANES), dtype),
        pltpu.VMEM((8, rows, LANES), dtype),
        pltpu.VMEM((7, rows, LANES), dtype),
        pltpu.SemaphoreType.DMA((8,)),
        pltpu.SemaphoreType.DMA((8,)),
        pltpu.SemaphoreType.DMA((3, 7)),
        pltpu.SemaphoreType.DMA((3, 7)),
    ]


def reduce_scatter_steps(get, pieces, scratch):
    crecv, acc, recv, csend_s, crecv_s, send_s, recv_s = scratch
    me, core, chip, sign = place()
    other = me + 1 - 2 * core
    num = len(pieces)
    started = []

    def core_copy(s):
        return remote(get(2 * chip_at(chip, sign, s) + 1 - core), crecv.at[s], csend_s.at[s], crecv_s.at[s], other)

    def ici_copy(k, t, i, s):
        off, ln = pieces[k]
        slot = RS_BASE[t] + i
        peer = 2 * chip_at(chip, sign, order_of(k)[t]) + core
        return remote(acc.at[s, pl.ds(off, ln), :], recv.at[slot, pl.ds(off, ln), :], send_s.at[k, slot], recv_s.at[k, slot], peer)

    for s in CORE_ORDER:
        c = core_copy(s)
        c.start()
        started.append(c)
    yield
    for s in CORE_ORDER:
        core_copy(s).wait_recv()
        mine = get(2 * chip_at(chip, sign, s) + core)
        acc[s] = mine[...] + crecv[s]
        for k in range(num):
            for i, (src, dst) in enumerate(stage_slots(k, 0)):
                if src == s:
                    c = ici_copy(k, 0, i, s)
                    c.start()
                    started.append(c)
    yield
    for t in range(3):
        for i in reversed(range(len(stage_slots(0, t)))):
            for k in range(num):
                off, ln = pieces[k]
                src, dst = stage_slots(k, t)[i]
                ici_copy(k, t, i, src).wait_recv()
                p = pl.ds(off, ln)
                acc[dst, p, :] = acc[dst, p, :] + recv[RS_BASE[t] + i, p, :]
                if t < 2:
                    for i2, (src2, dst2) in enumerate(stage_slots(k, t + 1)):
                        if src2 == dst:
                            c = ici_copy(k, t + 1, i2, dst)
                            c.start()
                            started.append(c)
        yield
    for c in started:
        c.wait_send()


def ag_scratch():
    return [pltpu.SemaphoreType.DMA((3, 8)), pltpu.SemaphoreType.DMA((3, 8)), pltpu.SemaphoreType.DMA((3, 8)), pltpu.SemaphoreType.DMA((3, 8))]


def all_gather_steps(own, out, pieces, scratch):
    csend_s, crecv_s, send_s, recv_s = scratch
    me, core, chip, sign = place()
    other = me + 1 - 2 * core
    num = len(pieces)
    started = []

    def ref(k, s):
        off, ln = pieces[k]
        return out(2 * chip_at(chip, sign, s) + core).at[pl.ds(off, ln), :]

    def source(k, s):
        off, ln = pieces[k]
        return own.at[pl.ds(off, ln), :] if s == 0 else ref(k, s)

    def core_copy(k, s):
        return remote(source(k, s), ref(k, s), csend_s.at[k, s], crecv_s.at[k, s], other)

    def core_wait(k, s):
        off, ln = pieces[k]
        there = out(2 * chip_at(chip, sign, s) + 1 - core).at[pl.ds(off, ln), :]
        remote(there, there, csend_s.at[k, s], crecv_s.at[k, s], other).wait_recv()

    def ici_copy(k, t, s):
        d = order_of(k)[t]
        peer = 2 * chip_at(chip, sign, d) + core
        return remote(source(k, s), ref(k, s), send_s.at[k, s ^ d], recv_s.at[k, s ^ d], peer)

    def ici_wait(k, s):
        remote(ref(k, s), ref(k, s), send_s.at[k, s], recv_s.at[k, s], other).wait_recv()

    def go(c):
        c.start()
        started.append(c)

    def live(k, t):
        dims = order_of(k)[:t]
        rest = order_of(k)[t:]
        return [s for s in SLOTS if all(not s & d for d in rest)]

    for t in range(3):
        for k in range(num):
            go(ici_copy(k, t, 0))
    for k in range(num):
        go(core_copy(k, 0))
    yield
    for t in range(3):
        for i in range(len(live(0, t))):
            for k in range(num):
                d = order_of(k)[t]
                s = live(k, t)[i] ^ d
                ici_wait(k, s)
                for t2 in range(t + 1, 3):
                    go(ici_copy(k, t2, s))
                go(core_copy(k, s))
        yield
    for k in range(num):
        for s in SLOTS:
            core_wait(k, s)
    for c in started:
        c.wait_send()


def rs_kernel(pieces, x_ref, out_ref, *scratch):
    enter()
    for _ in reduce_scatter_steps(lambda dev: x_ref.at[dev], pieces, scratch):
        pass
    out_ref[...] = scratch[1][0]


def ag_kernel(pieces, x_ref, out_ref, *scratch):
    enter()
    out_ref[lax.axis_index("dp")] = x_ref[...]
    for _ in all_gather_steps(x_ref, lambda dev: out_ref.at[dev], pieces, scratch):
        pass


def ar_kernel(pieces, x_ref, out_ref, *scratch):
    enter()
    n = len(rs_scratch(8, F32))
    for _ in reduce_scatter_steps(lambda dev: x_ref.at[dev], pieces, scratch[:n]):
        pass
    acc = scratch[1]
    out_ref[lax.axis_index("dp")] = acc[0]
    for _ in all_gather_steps(acc.at[0], lambda dev: out_ref.at[dev], pieces, scratch[n:]):
        pass


def stats_kernel(x_ref, out_ref, held, recv, send_s, recv_s):
    enter()
    me, core, chip, sign = place()
    peers = [me + 1 - 2 * core] + [2 * chip_at(chip, sign, d) + core for d in CHIP_DIMS]
    src = x_ref
    for t, peer in enumerate(peers):
        c = remote(src, recv.at[t], send_s.at[t], recv_s.at[t], peer)
        c.start()
        c.wait()
        top = jnp.maximum(src[0], recv[t, 0])
        den = src[1] * jnp.exp(src[0] - top) + recv[t, 1] * jnp.exp(recv[t, 0] - top)
        dst = held.at[t] if t < 3 else out_ref
        dst[0] = top
        dst[1] = den
        src = dst


def comm_call(body, name, cid, out_shape, scratch, *args):
    return pl.pallas_call(
        body,
        out_shape=out_shape,
        in_specs=[VM] * len(args),
        out_specs=jax.tree.map(lambda _: VM, out_shape),
        scratch_shapes=scratch,
        compiler_params=pltpu.CompilerParams(collective_id=cid, has_side_effects=True, vmem_limit_bytes=VMEM_CAP),
        name=name,
    )(*args)


def cut(x):
    rows = x.shape[-2]
    return pieces_of(rows, 16 if x.dtype == BF else 8) if rows >= 48 else [(0, rows)]


def rs(x, cid):
    n, rows, _ = x.shape
    return comm_call(functools.partial(rs_kernel, cut(x)), "sum_scatter", cid, jax.ShapeDtypeStruct((rows, LANES), x.dtype), rs_scratch(rows, x.dtype), x)


def ag(x, cid, n=16):
    rows = x.shape[0]
    return comm_call(functools.partial(ag_kernel, cut(x)), "all_rows", cid, jax.ShapeDtypeStruct((n, rows, LANES), x.dtype), ag_scratch(), x)


def ar(x, cid):
    n, rows, _ = x.shape
    return comm_call(functools.partial(ar_kernel, cut(x)), "sum_all", cid, jax.ShapeDtypeStruct((n, rows, LANES), F32), rs_scratch(rows, F32) + ag_scratch(), x)


def stats(x, cid):
    sems = pltpu.SemaphoreType.DMA((4,))
    return comm_call(stats_kernel, "soft_stats", cid, jax.ShapeDtypeStruct(x.shape, F32), [pltpu.VMEM((3,) + x.shape, F32), pltpu.VMEM((4,) + x.shape, F32), sems, sems], x)


def tower_fwd(row_block, w_in, w_out):
    pre_act = jnp.dot(row_block, w_in, preferred_element_type=F32)
    hidden = jax.nn.gelu(pre_act).astype(BF)
    return pre_act, hidden, jnp.dot(hidden, w_out, preferred_element_type=F32).astype(BF)


def tower_back(row_block, w_out, pre_act, hidden, grad_out):
    dw_out = jnp.einsum("nf,nd->fd", hidden, grad_out, preferred_element_type=F32)
    grad_hidden = jnp.einsum("nd,fd->nf", grad_out, w_out, preferred_element_type=F32)
    grad_pre = jax.vjp(jax.nn.gelu, pre_act)[1](grad_hidden)[0].astype(BF)
    dw_in = jnp.einsum("ne,nf->ef", row_block, grad_pre, preferred_element_type=F32)
    return grad_pre, dw_in, dw_out


def solution(mesh):
    num_dev = mesh.shape["dp"]

    def local_step(tokens, w_one, w_two, wi_one, wi_two, table_loc, cand_ids, log_q, targ_loc):
        my_index = lax.axis_index("dp")
        rows_loc = table_loc.shape[0]
        num_tok = tokens.shape[0]
        tok_total = num_tok * num_dev
        num_cand = cand_ids.shape[0]
        cand_loc = num_cand // num_dev
        dim = table_loc.shape[1]
        scale = SCORE_GAIN / math.sqrt(dim)
        targ_all = ag(targ_loc.reshape(-1, LANES), 1).reshape(-1)
        ids = jnp.concatenate([cand_ids, targ_all]).reshape(-1, LANES)
        base = (my_index * rows_loc).reshape(1).astype(I32)
        owned, plist, counts = gather(table_loc, ids, base, num_cand)
        raw_c = rs(owned[:num_cand].reshape(num_dev, cand_loc, dim), 2)
        raw_t = rs(owned[num_cand:].reshape(num_dev, num_tok, dim), 3)
        q_pre, q_hidden, query = tower_fwd(tokens, w_one, w_two)
        query_all = ag(query, 4).reshape(tok_total, dim)
        raw = jnp.concatenate([raw_c, raw_t])
        i_pre, i_hidden, vec = tower_fwd(raw, wi_one, wi_two)
        cand_vec, targ_vec = vec[:cand_loc], vec[cand_loc:]
        my_ids = lax.dynamic_slice_in_dim(cand_ids, my_index * cand_loc, cand_loc)
        my_logq = lax.dynamic_slice_in_dim(log_q, my_index * cand_loc, cand_loc)
        z = jnp.einsum("td,sd->ts", query_all, cand_vec, preferred_element_type=F32) * scale - my_logq[None, :]
        z = jnp.where(targ_all[:, None] == my_ids[None, :], HIT_VALUE, z)
        top = jnp.max(z, axis=1)
        e = jnp.exp(z - top[:, None])
        den = jnp.sum(e, axis=1)
        z_targ = jnp.einsum("td,td->t", query, targ_vec, preferred_element_type=F32) * scale
        mine = my_index * num_tok
        z_all = lax.dynamic_update_slice_in_dim(jnp.full((tok_total,), -jnp.inf, F32), z_targ, mine, 0)
        top_t = jnp.maximum(top, z_all)
        den_t = den * jnp.exp(top - top_t) + jnp.exp(z_all - top_t)
        st = stats(jnp.stack([top_t, den_t]).reshape(2, -1, LANES), 5).reshape(2, tok_total)
        factor = jnp.exp(top - st[0]) / st[1] / tok_total
        dz = (e * factor[:, None]).astype(BF)
        dh_part = jnp.einsum("ts,sd->td", dz, cand_vec, preferred_element_type=F32)
        d_cand = (jnp.einsum("ts,td->sd", dz, query_all, preferred_element_type=F32) * scale).astype(BF)
        my_top = lax.dynamic_slice_in_dim(st[0], mine, num_tok)
        my_den = lax.dynamic_slice_in_dim(st[1], mine, num_tok)
        loss_sum = jnp.sum(jnp.log(my_den) + my_top - z_targ)
        dz_targ = ((jnp.exp(z_targ - my_top) / my_den - 1.0) / tok_total).astype(BF).astype(F32)
        dh_cand = rs(dh_part.reshape(num_dev, num_tok, dim), 6)
        d_query = ((dz_targ[:, None] * targ_vec.astype(F32) + dh_cand) * scale).astype(BF)
        d_targ = (scale * dz_targ[:, None] * query.astype(F32)).astype(BF)
        dw_one, dw_two = tower_back(tokens, w_two, q_pre, q_hidden, d_query)[1:]
        i_grad_pre, dwi_one, dwi_two = tower_back(raw, wi_two, i_pre, i_hidden, jnp.concatenate([d_cand, d_targ]))
        d_raw = jnp.einsum("nf,df->nd", i_grad_pre, wi_one, preferred_element_type=F32).astype(BF)
        back_c = ag(d_raw[:cand_loc], 7).reshape(num_cand, dim)
        back_t = ag(d_raw[cand_loc:], 8).reshape(tok_total, dim)
        d_table = scatter(jnp.concatenate([back_c, back_t]), plist, counts, rows_loc)
        extra = jnp.zeros((num_dev * 8, LANES), F32).at[0, 0].set(loss_sum)
        parts = jnp.concatenate([w.reshape(-1, LANES) for w in (dw_one, dw_two, dwi_one, dwi_two)] + [extra])
        sums = ar(parts.reshape(num_dev, -1, LANES), 9).reshape(-1, LANES)
        n = dw_one.size // LANES
        outs = [sums[i * n:(i + 1) * n].reshape(w.shape) for i, w in enumerate((dw_one, dw_two, dwi_one, dwi_two))]
        return (sums[4 * n, 0] / tok_total, d_table) + tuple(outs)

    return jax.shard_map(local_step, mesh=mesh, in_specs=(P("dp", None), P(), P(), P(), P(), P("dp", None), P(), P(), P("dp")), out_specs=(P(), P("dp", None), P(), P(), P(), P()), check_vma=False)
```

time: 640 us -> 268 us (0.42)
  waiting for transfers between devices: 298 us -> 0 us
  Pallas kernels: 0 us -> 184 us
  other arithmetic: 155 us -> 33.5 us
  local copies, waits for them, and re-layouts: 83.4 us -> 18.9 us
  blocking collectives: 46.2 us -> 0 us
  matrix products: 41.2 us -> 27.5 us
  between operations: 16.1 us -> 2.75 us
    pallas_call x0 -> x11, Pallas kernels: none -> 184 us  [the longest x9 146 us: comm_call(): pl.pallas_call(body, out_shape=out_shape, in_specs=[VM] * len(args), out_...]
    reduce_scatter x3 -> x0, waiting for transfers between devices: 168 us -> none  [the longest x1 82.9 us: local_step(): lax.psum_scatter(d_cand_part, 'dp', scatter_dimension=0, tiled=True)]
    scatter-add x1 -> x0, other arithmetic: 120 us -> none  [local_step(): jax.ops.segment_sum(jnp.concatenate([back_cand, back_targ]).astype(jnp.fl...]
    all_gather x3 -> x0, waiting for transfers between devices: 97 us -> none  [the longest x1 37.9 us: local_step(): back_cand = lax.all_gather(d_cand_raw, 'dp', axis=0, tiled=True)]
    gather x2 -> x0, local copies, waits for them, and re-layouts: 75.6 us -> none  [owned_rows(): picked = jnp.take(table_loc, jnp.clip(local_ids, 0, num_rows - 1), axis=0)]
    psum x1 -> x0, waiting for transfers between devices: 32.8 us -> none  [local_step(): lax.psum((dw_one, dw_two, dwi_one_t + dwi_one_c, dwi_two_t + dwi_two_c),...]
    psum x1 -> x0, blocking collectives: 31.2 us -> none  [local_step(): loss = lax.psum(loss_sum, 'dp') / tok_total]
    select_n x3 -> x0, other arithmetic: 16.5 us -> none  [the longest x2 16.4 us: owned_rows(): return jnp.where(is_owned[:, None], picked, 0)]
  transfers between devices with their start and end apart: 7 -> 0, of which waited for: 7 -> 0; matrix products, arithmetic and copies ran while one was open for 6% -> 0% of each run, Pallas kernels for 0% -> 0%
where the time goes in v1:
time: 268 us; the launch traced here: 267 us
  Pallas kernels  184 us (69%)
  other arithmetic  33.5 us (12%)
  matrix products  27.5 us (10%)
  local copies, waits for them, and re-layouts  18.9 us (7%)
  between operations  2.75 us (1%)
    pallas_call x9, Pallas kernels, comm_call(): pl.pallas_call(body, out_shape=out_shape, in_specs=[VM] * len(args), out_...  146 us
    pallas_call x1, Pallas kernels, scatter(): pl.pallas_call(functools.partial(scatter_kernel, chunks), out_shape=jax.S...  21.2 us
    pallas_call x1, Pallas kernels, gather(): pl.pallas_call(functools.partial(gather_kernel, chunks, head), out_shape=...  16.3 us
    concatenate x1, other arithmetic, local_step(): jnp.concatenate([back_c, back_t])  14.2 us
    convert_element_type x1, other arithmetic, local_step(): dz = (e * factor[:, None]).astype(BF)  9.07 us
    reduce_sum x1, other arithmetic, local_step(): den = jnp.sum(e, axis=1)  5.48 us

profile of v1, /device:TPU:0, one launch (start us, length us, event | category | flops | bytes accessed | tf_op | source)
XLA Modules:
  0.0 266.5 jit_solution(15416644943038871720)
XLA Ops:
  0.6 0.0 copy-start
  0.7 0.7 dynamic_slice.13
  1.4 0.7 dynamic_slice.12
  2.1 14.5 %all_rows.4 = s32[16,2,128]{2,1,0:T(2,128)} custom-call(s32[2,128]{1,0:T(2,128)} %bitcast.59), custom_call_target="tpu_custom_call" | custom-call | tf_op jit(solution)/shard_map/all_rows/pallas_call | solution.py:438
  16.5 1.5 add_bitcast_fusion.ids_ref
  18.0 1.1 fusion.50
  19.2 0.0 copy-start.7
  19.2 16.3 %gather_rows.1 = (bf16[20480,128]{1,0:T(8,128)(2,1)}, s32[160,128]{1,0:T(8,128)}, s32[2]{0:T(128)}) custom-call(s32[1]{0:T(128)} %bitcast.base_ref, s32[160,128]{1,0:T(8,128)} %add_bitcast_fusion.ids_ref, bf16[32768,128]{1,0:T(8,128)(2,1)} %table_ref.1), custom_call_target="tpu_custom_call" | custom-call | tf_op jit(solution)/shard_map/gather_rows/pallas_call | solution.py:111
  35.5 2.3 slice.60
  37.8 3.7 %slice.59 = bf16[16384,128]{1,0:T(8,128)(2,1)} slice(bf16[20480,128]{1,0:T(8,128)(2,1)} %get-tuple-element.21), slice={[0:16384], [0:128]} | slice | bytes 8388608 | tf_op jit(solution)/shard_map/slice | solution.py:504
  41.4 21.3 %sum_scatter.3 = bf16[1024,128]{1,0:T(8,128)(2,1)} custom-call(bf16[16,1024,128]{2,1,0:T(8,128)(2,1)} %bitcast.47), custom_call_target="tpu_custom_call" | custom-call | tf_op jit(solution)/shard_map/sum_scatter/pallas_call | solution.py:438
  62.7 12.4 %sum_scatter.4 = bf16[256,128]{1,0:T(8,128)(2,1)} custom-call(bf16[16,256,128]{2,1,0:T(8,128)(2,1)} %bitcast.52), custom_call_target="tpu_custom_call" | custom-call | tf_op jit(solution)/shard_map/sum_scatter/pallas_call | solution.py:438
  75.2 0.0 copy-done.6
  75.2 1.5 fusion.31
  76.7 0.0 copy-done
  76.7 0.0 copy-start.11
  76.7 1.0 convolution_convert_fusion.1
  77.7 0.0 copy-done.11
  77.7 0.0 copy-start.9
  77.7 0.9 fusion.35
  78.6 0.2 multiply_dynamic-update-slice_fusion
  78.8 13.4 %all_rows.5 = bf16[16,256,128]{2,1,0:T(8,128)(2,1)} custom-call(bf16[256,128]{1,0:T(8,128)(2,1)} %get-tuple-element.38.x_ref), custom_call_target="tpu_custom_call" | custom-call | tf_op jit(solution)/shard_map/all_rows/pallas_call | solution.py:438
  92.2 0.0 copy-done.9
  92.2 4.7 %fusion.1 = (f32[4096]{0:T(1024)S(1)}, f32[4096,1024]{0,1:T(8,128)S(1)}) fusion(f32[1024]{0:T(1024)S(1)} %dynamic_slice.13, s32[4096]{0:T(1024)S(1)} %bitcast.56, s32[1024]{0:T(1024)S(1)} %dynamic_slice.12, bf16[4096,128]{1,0:T(8,128)(2,1)} %bitcast.53, bf16[1280,128]{1,0:T(8,128)(2,1)S(1)} %convolution_convert_fusion.1), kind=kOutput, calls=%fused_computation.4 | convolution fusion | flops 1094709248 | bytes 18128896 | tf_op jit(solution)/shard_map/td,sd->ts/dot_general | solution.py:513
  97.0 0.0 copy-start.1
  97.0 5.5 %fusion = f32[4096]{0:T(1024)S(1)} fusion(f32[4096,1024]{0,1:T(8,128)S(1)} %get-tuple-element.36, f32[4096]{0:T(1024)S(1)} %get-tuple-element.35, f32[1024]{0:T(1024)S(1)} %dynamic_slice.13, s32[4096]{0:T(1024)S(1)} %bitcast.57, s32[1024]{0:T(1024)S(1)} %dynamic_slice.12), kind=kLoop, calls=%fused_computation.3 | loop fusion | flops 25161728 | bytes 16834560 | tf_op jit(solution)/shard_map/reduce_sum | solution.py:517
  102.5 0.7 copy-done.1
  103.2 0.6 pad_maximum_fusion.7.x_ref
  103.8 12.1 %soft_stats.1 = f32[2,32,128]{2,1,0:T(8,128)} custom-call(f32[2,32,128]{2,1,0:T(8,128)} %pad_maximum_fusion.7.x_ref), custom_call_target="tpu_custom_call" | custom-call | tf_op jit(solution)/shard_map/soft_stats/pallas_call | solution.py:438
  115.9 0.7 divide_multiply_fusion
  116.6 0.0 copy-start.4
  116.6 9.1 %multiply_convert_fusion = bf16[4096,1024]{0,1:T(8,128)(2,1)S(1)} fusion(f32[4096,1024]{0,1:T(8,128)} %copy-done.1, f32[4096]{0:T(1024)S(1)} %divide_multiply_fusion, f32[4096]{0:T(1024)S(1)} %get-tuple-element.35, f32[1024]{0:T(1024)S(1)} %dynamic_slice.13, s32[4096]{0:T(1024)S(1)} %bitcast.58, s32[1024]{0:T(1024)S(1)} %dynamic_slice.12), kind=kLoop, calls=%fused_computation | loop fusion | flops 29360128 | bytes 25223168 | tf_op jit(solution)/shard_map/convert_element_type | solution.py:525
  125.7 0.0 copy-done.4
  125.7 3.0 %fusion.9 = bf16[1024,128]{1,0:T(8,128)(2,1)} fusion(bf16[4096,1024]{0,1:T(8,128)(2,1)S(1)} %multiply_convert_fusion, bf16[4096,128]{1,0:T(8,128)(2,1)S(1)} %bitcast.54), kind=kOutput, calls=%fused_computation.20 | convolution fusion | flops 1074003968 | bytes 9699328 | tf_op jit(solution)/shard_map/ts,td->sd/dot_general | solution.py:527
  128.8 3.7 %fusion.26 = f32[4096,128]{1,0:T(8,128)} fusion(bf16[4096,1024]{0,1:T(8,128)(2,1)S(1)} %multiply_convert_fusion, bf16[1280,128]{1,0:T(8,128)(2,1)S(1)} %convolution_convert_fusion.1), kind=kOutput, calls=%fused_computation.44 | convolution fusion | flops 1073741824 | bytes 10747904 | tf_op jit(solution)/shard_map/ts,sd->td/dot_general | solution.py:526
  132.5 14.4 %sum_scatter.5 = f32[256,128]{1,0:T(8,128)} custom-call(f32[16,256,128]{2,1,0:T(8,128)} %bitcast.48), custom_call_target="tpu_custom_call" | custom-call | tf_op jit(solution)/shard_map/sum_scatter/pallas_call | solution.py:438
  146.9 0.0 copy-done.8
  146.9 0.7 broadcast_multiply_fusion
  147.6 0.0 copy-done.10
  147.6 1.0 fusion.34
  148.6 0.0 copy-done.7
  148.6 2.3 convolution_bitcast_fusion
  150.9 1.1 copy.15
  152.0 0.7 constant_dynamic-update-slice_fusion.1
  152.7 2.1 convolution_dynamic-update-slice_fusion
  154.9 2.9 %fusion.8 = bf16[1280,512]{1,0:T(8,128)(2,1)S(1)} fusion(f32[1280,512]{1,0:T(8,128)S(1)} %fusion.31, bf16[512,128]{1,0:T(8,128)(2,1)S(1)} %copy-done, bf16[256,128]{1,0:T(8,128)(2,1)S(1)} %get-tuple-element.40, bf16[1024,128]{1,0:T(8,128)(2,1)} %fusion.9), kind=kOutput, calls=%fused_computation.14 | convolution fusion | flops 181534720 | bytes 4390912 | tf_op jit(solution)/shard_map/nd,fd->nf/dot_general | solution.py:482
  157.8 1.1 fusion.30
  158.9 0.5 convolution_convert_fusion
  159.4 1.0 reshape.134
  160.3 0.7 constant_dynamic-update-slice_fusion
  161.1 2.7 convolution_dynamic-update-slice_fusion.1
  163.7 1.3 pad_dynamic-update-slice_fusion
  165.0 23.6 %sum_all.1 = f32[16,136,128]{2,1,0:T(8,128)} custom-call(f32[16,136,128]{2,1,0:T(8,128)} %bitcast.14.x_ref), custom_call_target="tpu_custom_call" | custom-call | tf_op jit(solution)/shard_map/sum_all/pallas_call | solution.py:438
  188.6 1.2 slice.74
  190.4 2.0 fusion.49
  192.5 0.6 slice.76.x_ref
  193.1 0.7 slice.75.x_ref
  193.8 0.7 reshape.141
  194.6 0.7 reshape.140
  195.3 13.5 %all_rows.7 = bf16[16,256,128]{2,1,0:T(8,128)(2,1)} custom-call(bf16[256,128]{1,0:T(8,128)(2,1)} %slice.76.x_ref), custom_call_target="tpu_custom_call" | custom-call | tf_op jit(solution)/shard_map/all_rows/pallas_call | solution.py:438
  208.9 21.2 %all_rows.6 = bf16[16,1024,128]{2,1,0:T(8,128)(2,1)} custom-call(bf16[1024,128]{1,0:T(8,128)(2,1)} %slice.75.x_ref), custom_call_target="tpu_custom_call" | custom-call | tf_op jit(solution)/shard_map/all_rows/pallas_call | solution.py:438
  230.0 0.0 copy-done.2
  230.0 14.2 %pad_maximum_fusion.grad_ref = bf16[20480,128]{1,0:T(8,128)(2,1)} fusion(bf16[4096,128]{1,0:T(8,128)(2,1)S(1)} %bitcast.51, bf16[16384,128]{1,0:T(8,128)(2,1)} %bitcast.46), kind=kLoop, calls=%fused_computation.5 | loop fusion | flops 10485760 | bytes 10485760 | tf_op jit(solution)/shard_map/concatenate | solution.py:540
  244.2 21.2 %scatter_rows.1 = f32[32768,128]{1,0:T(8,128)} custom-call(s32[2]{0:T(128)} %get-tuple-element.22.cnt_ref, s32[160,128]{1,0:T(8,128)} %get-tuple-element.23.list_ref, bf16[20480,128]{1,0:T(8,128)(2,1)} %pad_maximum_fusion.grad_ref), custom_call_target="tpu_custom_call" | custom-call | tf_op jit(solution)/shard_map/scatter_rows/pallas_call | solution.py:199
  (12 shorter events, 0.1 us)
Async XLA Ops:
  0.6 76.0 %copy-start = (bf16[512,128]{1,0:T(8,128)(2,1)S(1)}, bf16[512,128]{1,0:T(8,128)(2,1)}, u32[]{:S(2)}) copy-start(bf16[512,128]{1,0:T(8,128)(2,1)} %param.15) | copy-start | bytes 393220
  19.2 129.4 %copy-start.7 = (f32[256,512]{1,0:T(8,128)}, f32[256,512]{1,0:T(8,128)S(1)}, u32[]{:S(2)}) copy-start(f32[256,512]{1,0:T(8,128)S(1)} %fusion.50) | copy-start | bytes 1572868
  41.4 33.7 %copy-start.6 = (bf16[128,512]{1,0:T(8,128)(2,1)S(1)}, bf16[128,512]{1,0:T(8,128)(2,1)}, u32[]{:S(2)}) copy-start(bf16[128,512]{1,0:T(8,128)(2,1)} %param.14) | copy-start | bytes 393220
  76.7 1.0 copy-start.11
  77.7 14.6 %copy-start.9 = (s32[16,2,128]{2,1,0:T(2,128)S(1)}, s32[16,2,128]{2,1,0:T(2,128)}, u32[]{:S(2)}) copy-start(s32[16,2,128]{2,1,0:T(2,128)} %all_rows.4) | copy-start | bytes 49156
  97.0 6.2 %copy-start.1 = (f32[4096,1024]{0,1:T(8,128)}, f32[4096,1024]{0,1:T(8,128)S(1)}, u32[]{:S(2)}) copy-start(f32[4096,1024]{0,1:T(8,128)S(1)} %get-tuple-element.36) | copy-start | bytes 50331652
  116.6 9.1 %copy-start.4 = (bf16[16,256,128]{2,1,0:T(8,128)(2,1)S(1)}, bf16[16,256,128]{2,1,0:T(8,128)(2,1)}, u32[]{:S(2)}) copy-start(bf16[16,256,128]{2,1,0:T(8,128)(2,1)} %all_rows.5) | copy-start | bytes 3145732
  128.7 18.1 %copy-start.8 = (f32[2,32,128]{2,1,0:T(8,128)S(1)}, f32[2,32,128]{2,1,0:T(8,128)}, u32[]{:S(2)}) copy-start(f32[2,32,128]{2,1,0:T(8,128)} %soft_stats.1) | copy-start | bytes 98308
  128.7 18.8 %copy-start.10 = (bf16[256,128]{1,0:T(8,128)(2,1)S(1)}, bf16[256,128]{1,0:T(8,128)(2,1)}, u32[]{:S(2)}) copy-start(bf16[256,128]{1,0:T(8,128)(2,1)} %get-tuple-element.38.x_ref) | copy-start | bytes 196612
  154.9 2.9 %copy-start.3 = (bf16[1024,128]{1,0:T(8,128)(2,1)S(1)}, bf16[1024,128]{1,0:T(8,128)(2,1)}, u32[]{:S(2)}) copy-start(bf16[1024,128]{1,0:T(8,128)(2,1)} %sum_scatter.3) | copy-start | bytes 786436
  154.9 2.9 %copy-start.5 = (bf16[256,128]{1,0:T(8,128)(2,1)S(1)}, bf16[256,128]{1,0:T(8,128)(2,1)}, u32[]{:S(2)}) copy-start(bf16[256,128]{1,0:T(8,128)(2,1)} %sum_scatter.4) | copy-start | bytes 196612
  208.8 21.2 %copy-start.2 = (bf16[16,256,128]{2,1,0:T(8,128)(2,1)S(1)}, bf16[16,256,128]{2,1,0:T(8,128)(2,1)}, u32[]{:S(2)}) copy-start(bf16[16,256,128]{2,1,0:T(8,128)(2,1)} %all_rows.7) | copy-start | bytes 3145732

commit v2 on v1

--- a/solution.py
+++ b/solution.py
@@ -20,7 +20,7 @@
 BLK = 256
 
 
-def compact(loc, num_rows):
+def compact(loc, num_rows, parts, head):
     nr = loc.shape[0]
     own = jnp.where((loc >= 0) & (loc < num_rows), 1.0, 0.0)
     own16 = own.astype(BF)
@@ -31,7 +31,10 @@
     lane = lax.broadcasted_iota(I32, (nr, LANES), 1)
     flat = lax.broadcasted_iota(I32, (nr, LANES), 0) * LANES + lane
     disp = flat - (within + before).astype(I32)
-    val = jnp.where(own > 0, flat * 32768 + loc, -1)
+    n_head, n_tail = head // parts, (nr * LANES - head) // parts
+    late = flat - head
+    pos = jnp.where(flat < head, flat + flat // n_head * n_tail, late + (late // n_tail + 1) * n_head)
+    val = jnp.where(own > 0, pos * 32768 + loc, -1)
     total = jnp.sum(own).astype(I32)
 
     def back(x, s):
@@ -51,7 +54,7 @@
     return jnp.where(flat < total, val, nr * LANES * 32768), own, total
 
 
-def gather_kernel(chunks, head, base_ref, ids_ref, table_ref, out_ref, list_ref, cnt_ref, stage, tab, dense, plist, sem, psem):
+def gather_kernel(chunks, head, parts, base_ref, ids_ref, table_ref, out_ref, list_ref, cnt_ref, stage, tab, dense, plist, sem, psem):
     rows = tab.shape[0]
     npos = out_ref.shape[0]
     cr = rows // chunks
@@ -61,7 +64,7 @@
 
     for c in range(chunks):
         load(c).start()
-    packed, own, total = compact(ids_ref[...] - base_ref[0], rows)
+    packed, own, total = compact(ids_ref[...] - base_ref[0], rows, parts, head)
     list_ref[...] = packed
     cnt_ref[0] = jnp.sum(own[:head // LANES]).astype(I32)
     cnt_ref[1] = total
@@ -103,13 +106,13 @@
     lax.fori_loop(0, npos // BLK, pack, 0)
 
 
-def gather(table, ids, base, head):
+def gather(table, ids, base, head, parts):
     rows = table.shape[0]
     nr = ids.shape[0]
     npos = nr * LANES
     chunks = 8
     return pl.pallas_call(
-        functools.partial(gather_kernel, chunks, head),
+        functools.partial(gather_kernel, chunks, head, parts),
         out_shape=(jax.ShapeDtypeStruct((npos, LANES), BF), jax.ShapeDtypeStruct((nr, LANES), I32), jax.ShapeDtypeStruct((2,), I32)),
         in_specs=[SM, VM, HB],
         out_specs=(VM, VM, SM),
@@ -262,11 +265,11 @@
 RS_BASE = (0, 4, 6)
 
 
-def rs_scratch(rows, dtype):
+def rs_scratch(rows, dtype, width=LANES):
     return [
-        pltpu.VMEM((8, rows, LANES), dtype),
-        pltpu.VMEM((8, rows, LANES), dtype),
-        pltpu.VMEM((7, rows, LANES), dtype),
+        pltpu.VMEM((8, rows, width), dtype),
+        pltpu.VMEM((8, rows, width), dtype),
+        pltpu.VMEM((7, rows, width), dtype),
         pltpu.SemaphoreType.DMA((8,)),
         pltpu.SemaphoreType.DMA((8,)),
         pltpu.SemaphoreType.DMA((3, 7)),
@@ -392,46 +395,11 @@
         c.wait_send()
 
 
-def rs_kernel(pieces, x_ref, out_ref, *scratch):
-    enter()
-    for _ in reduce_scatter_steps(lambda dev: x_ref.at[dev], pieces, scratch):
-        pass
-    out_ref[...] = scratch[1][0]
-
-
 def ag_kernel(pieces, x_ref, out_ref, *scratch):
     enter()
     out_ref[lax.axis_index("dp")] = x_ref[...]
     for _ in all_gather_steps(x_ref, lambda dev: out_ref.at[dev], pieces, scratch):
         pass
-
-
-def ar_kernel(pieces, x_ref, out_ref, *scratch):
-    enter()
-    n = len(rs_scratch(8, F32))
-    for _ in reduce_scatter_steps(lambda dev: x_ref.at[dev], pieces, scratch[:n]):
-        pass
-    acc = scratch[1]
-    out_ref[lax.axis_index("dp")] = acc[0]
-    for _ in all_gather_steps(acc.at[0], lambda dev: out_ref.at[dev], pieces, scratch[n:]):
-        pass
-
-
-def stats_kernel(x_ref, out_ref, held, recv, send_s, recv_s):
-    enter()
-    me, core, chip, sign = place()
-    peers = [me + 1 - 2 * core] + [2 * chip_at(chip, sign, d) + core for d in CHIP_DIMS]
-    src = x_ref
-    for t, peer in enumerate(peers):
-        c = remote(src, recv.at[t], send_s.at[t], recv_s.at[t], peer)
-        c.start()
-        c.wait()
-        top = jnp.maximum(src[0], recv[t, 0])
-        den = src[1] * jnp.exp(src[0] - top) + recv[t, 1] * jnp.exp(recv[t, 0] - top)
-        dst = held.at[t] if t < 3 else out_ref
-        dst[0] = top
-        dst[1] = den
-        src = dst
 
 
 def comm_call(body, name, cid, out_shape, scratch, *args):
@@ -451,38 +419,269 @@
     return pieces_of(rows, 16 if x.dtype == BF else 8) if rows >= 48 else [(0, rows)]
 
 
-def rs(x, cid):
-    n, rows, _ = x.shape
-    return comm_call(functools.partial(rs_kernel, cut(x)), "sum_scatter", cid, jax.ShapeDtypeStruct((rows, LANES), x.dtype), rs_scratch(rows, x.dtype), x)
-
-
 def ag(x, cid, n=16):
     rows = x.shape[0]
     return comm_call(functools.partial(ag_kernel, cut(x)), "all_rows", cid, jax.ShapeDtypeStruct((n, rows, LANES), x.dtype), ag_scratch(), x)
 
 
-def ar(x, cid):
-    n, rows, _ = x.shape
-    return comm_call(functools.partial(ar_kernel, cut(x)), "sum_all", cid, jax.ShapeDtypeStruct((n, rows, LANES), F32), rs_scratch(rows, F32) + ag_scratch(), x)
-
-
-def stats(x, cid):
-    sems = pltpu.SemaphoreType.DMA((4,))
-    return comm_call(stats_kernel, "soft_stats", cid, jax.ShapeDtypeStruct(x.shape, F32), [pltpu.VMEM((3,) + x.shape, F32), pltpu.VMEM((4,) + x.shape, F32), sems, sems], x)
-
-
-def tower_fwd(row_block, w_in, w_out):
-    pre_act = jnp.dot(row_block, w_in, preferred_element_type=F32)
-    hidden = jax.nn.gelu(pre_act).astype(BF)
-    return pre_act, hidden, jnp.dot(hidden, w_out, preferred_element_type=F32).astype(BF)
-
-
-def tower_back(row_block, w_out, pre_act, hidden, grad_out):
-    dw_out = jnp.einsum("nf,nd->fd", hidden, grad_out, preferred_element_type=F32)
-    grad_hidden = jnp.einsum("nd,fd->nf", grad_out, w_out, preferred_element_type=F32)
-    grad_pre = jax.vjp(jax.nn.gelu, pre_act)[1](grad_hidden)[0].astype(BF)
-    dw_in = jnp.einsum("ne,nf->ef", row_block, grad_pre, preferred_element_type=F32)
-    return grad_pre, dw_in, dw_out
+LOG2E = 1.4426950408889634
+GELU_C = math.sqrt(2.0 / math.pi)
+GELU_A = 0.044715
+ROW_BLK = 256
+
+
+def gelu_both(x):
+    x2 = x * x
+    t = jnp.tanh(GELU_C * (x + GELU_A * (x2 * x)))
+    half = 0.5 * (1.0 + t)
+    return x * half, half + (0.5 * GELU_C) * x * (1.0 - t * t) * (1.0 + (3.0 * GELU_A) * x2)
+
+
+def dot_nn(a, b):
+    return jnp.dot(a, b, preferred_element_type=F32)
+
+
+def dot_nt(a, b):
+    return lax.dot_general(a, b, (((1,), (1,)), ((), ())), preferred_element_type=F32)
+
+
+def turn(x):
+    return x.astype(F32).T.astype(BF)
+
+
+def tower_into(rows, load, w_in, w_out, slope_ref, hid_ref, out_ref):
+    def blk(i, _):
+        s = pl.ds(pl.multiple_of(i * ROW_BLK, ROW_BLK), ROW_BLK)
+        act, slope = gelu_both(dot_nn(load(s), w_in[...]))
+        slope_ref[s, :] = slope
+        hid_ref[s, :] = act.astype(BF)
+        out_ref[s, :] = dot_nn(hid_ref[s, :], w_out[...]).astype(BF)
+        return 0
+
+    lax.fori_loop(0, rows // ROW_BLK, blk, 0)
+
+
+def tower_pre_grad(rows, grad_ref, w_out, slope_ref, pre_ref):
+    def blk(i, _):
+        s = pl.ds(pl.multiple_of(i * ROW_BLK, ROW_BLK), ROW_BLK)
+        pre_ref[s, :] = (slope_ref[s, :] * dot_nt(grad_ref[s, :], w_out[...])).astype(BF)
+        return 0
+
+    lax.fori_loop(0, rows // ROW_BLK, blk, 0)
+
+
+def weight_grads(row_t, grad_t, pre_ref, hid_ref, sums_ref, parts, off):
+    d_in = dot_nn(row_t, pre_ref[...])
+    d_out = dot_nn(grad_t, hid_ref[...])
+    for which, w in enumerate((d_in, d_out)):
+        for c in range(4):
+            for h in range(2):
+                sums_ref[which * 8 + c * 2 + h, :64, :] = w[h * 64:(h + 1) * 64, c * LANES:(c + 1) * LANES]
+
+
+def step_kernel(shapes, names, x_ref, tok_ref, w1, w2, wi1, wi2, lq_ref, id_ref, targ_ref, rows_out, isum_out, qsum_out, *scratch):
+    n_cand, n_tok, parts = shapes
+    n_item = n_cand + n_tok
+    total = float(n_tok * parts)
+    scale = SCORE_GAIN / math.sqrt(LANES)
+    v = dict(zip(names, scratch))
+
+    def group(name):
+        return [v[k] for k in names if k.startswith(name + ".")]
+
+    enter()
+    me, core, chip, sign = place()
+    rs_rows = reduce_scatter_steps(lambda dev: x_ref.at[dev], pieces_of(n_item, 16), group("rs"))
+    next(rs_rows)
+    tower_into(n_tok, lambda s: tok_ref[s, :], w1, w2, v["q_slope"], v["q_hid"], v["q_vec"])
+    q_all = v["q_all"]
+    q_all[me] = v["q_vec"][...]
+    ag_q = all_gather_steps(v["q_vec"], lambda dev: q_all.at[dev], pieces_of(n_tok, 16), group("agq"))
+    next(ag_q)
+    next(rs_rows)
+    for _ in range(3):
+        next(rs_rows)
+        next(ag_q)
+    for g in (rs_rows, ag_q):
+        for _ in g:
+            pass
+    raw = v["rs.1"].at[0]
+    tower_into(n_item, lambda s: raw[s, :], wi1, wi2, v["i_slope"], v["i_hid"], v["i_vec"])
+    vec = v["i_vec"]
+    z_ref, top_ref, den_ref = v["z"], v["top"], v["den"]
+    jb = 128
+
+    def pass_one(t, _):
+        q_t = q_all[t]
+        targ = targ_ref[pl.ds(t, 1), :]
+        top8 = jnp.full((8, n_tok), -jnp.inf, F32)
+        for j in range(n_cand // jb):
+            s = pl.ds(j * jb, jb)
+            lq = jnp.concatenate([lq_ref[s, :]] * 2, axis=1)
+            ids = jnp.concatenate([id_ref[s, :]] * 2, axis=1)
+            z = dot_nt(vec[s, :], q_t) * (scale * LOG2E) - lq
+            z = jnp.where(ids == targ, HIT_VALUE * LOG2E, z)
+            z_ref[t, s, :] = z
+            top8 = jnp.maximum(top8, jnp.max(z.reshape(jb // 8, 8, n_tok), axis=0))
+        top = jnp.max(top8, axis=0, keepdims=True)
+        den8 = jnp.zeros((8, n_tok), F32)
+        for j in range(n_cand // jb):
+            e = jnp.exp2(z_ref[t, pl.ds(j * jb, jb), :] - top)
+            den8 = den8 + jnp.sum(e.reshape(jb // 8, 8, n_tok), axis=0)
+        top_ref[pl.ds(t, 1), :] = top
+        den_ref[pl.ds(t, 1), :] = jnp.sum(den8, axis=0, keepdims=True)
+        return 0
+
+    lax.fori_loop(0, parts, pass_one, 0)
+    own = pl.ds(me, 1)
+    targ_vec = vec[pl.ds(n_cand, n_tok), :]
+    q_own = v["q_vec"][...]
+    eye = lax.broadcasted_iota(I32, (n_tok, n_tok), 0) == lax.broadcasted_iota(I32, (n_tok, n_tok), 1)
+    z_own = jnp.sum(jnp.where(eye, dot_nt(targ_vec, q_own), 0.0), axis=0, keepdims=True) * (scale * LOG2E)
+    new_top = jnp.maximum(top_ref[own, :], z_own)
+    den_ref[own, :] = den_ref[own, :] * jnp.exp2(top_ref[own, :] - new_top) + jnp.exp2(z_own - new_top)
+    top_ref[own, :] = new_top
+
+    held, got, st_send, st_recv = group("st")
+    held[0, 0] = top_ref[...]
+    held[0, 1] = den_ref[...]
+    peers = [me + 1 - 2 * core] + [2 * chip_at(chip, sign, d) + core for d in CHIP_DIMS]
+    for i, peer in enumerate(peers):
+        c = remote(held.at[i], got.at[i], st_send.at[i], st_recv.at[i], peer)
+        c.start()
+        c.wait()
+        top = jnp.maximum(held[i, 0], got[i, 0])
+        den = held[i, 1] * jnp.exp2(held[i, 0] - top) + got[i, 1] * jnp.exp2(got[i, 0] - top)
+        held[i + 1, 0] = top
+        held[i + 1, 1] = den
+    last = len(peers)
+    norm = v["norm"]
+    norm[...] = held[last, 0] + jnp.log2(held[last, 1] * total)
+    top_ref[...] = held[last, 0]
+    den_ref[...] = held[last, 1]
+
+    lse = top_ref[own, :] + jnp.log2(den_ref[own, :])
+    loss = jnp.sum(lse - z_own, axis=1, keepdims=True) * (1.0 / LOG2E)
+    dz_row = ((jnp.exp2(z_own - top_ref[own, :]) / den_ref[own, :] - 1.0) * (1.0 / total)).astype(BF).astype(F32)
+    dz_col = jnp.sum(jnp.where(eye, dz_row, 0.0), axis=1, keepdims=True)
+    grad = v["i_grad"]
+    grad[pl.ds(n_cand, n_tok), :] = (scale * dz_col * q_own.astype(F32)).astype(BF)
+    vec_t = v["vec_t"]
+    vec_t[...] = turn(vec[:n_cand, :])
+    d_acc, dz_s, dh = v["d_acc"], v["dz"], v["dh"]
+    d_acc[...] = jnp.zeros_like(d_acc)
+
+    def pass_two(t, _):
+        shift = norm[pl.ds(t, 1), :]
+        for j in range(n_cand // jb):
+            s = pl.ds(j * jb, jb)
+            dz_s[s, :] = jnp.exp2(z_ref[t, s, :] - shift).astype(BF)
+        d_acc[...] += dot_nn(dz_s[...], q_all[t])
+        dh[t] = dot_nn(vec_t[...], dz_s[...])
+        return 0
+
+    lax.fori_loop(0, parts, pass_two, 0)
+    rs_dh = reduce_scatter_steps(lambda dev: dh.at[dev], pieces_of(LANES, 8), group("rsd"))
+    next(rs_dh)
+    grad[pl.ds(0, n_cand), :] = (d_acc[...] * scale).astype(BF)
+    tower_pre_grad(n_item, grad, wi2, v["i_slope"], v["i_pre"])
+    mine = rows_out.at[me]
+
+    def input_grad(i, _):
+        s = pl.ds(pl.multiple_of(i * ROW_BLK, ROW_BLK), ROW_BLK)
+        mine[s, :] = dot_nt(v["i_pre"][s, :], wi1[...]).astype(BF)
+        return 0
+
+    lax.fori_loop(0, n_item // ROW_BLK, input_grad, 0)
+    next(rs_dh)
+    ag_rows = all_gather_steps(mine, lambda dev: rows_out.at[dev], pieces_of(n_item, 16), group("agr"))
+    next(ag_rows)
+    isum, qsum = v["isum"], v["qsum"]
+    weight_grads(turn(raw[...]), turn(grad[...]), v["i_pre"], v["i_hid"], isum, parts, 0)
+    ars = []
+    for sums, out, name in ((isum, isum_out, "ai"), (qsum, qsum_out, "aq")):
+        refs = group(name)
+        n = len(refs) - 4
+        pieces = pieces_of(sums.shape[1], 8)
+        first = reduce_scatter_steps(lambda dev, sums=sums: sums.at[dev], pieces, refs[:n])
+        second = all_gather_steps(refs[1].at[0], lambda dev, out=out: out.at[dev], pieces, refs[n:])
+        ars.append((first, second, refs[1], out))
+    ar_i, ag_i, acc_i, _ = ars[0]
+    ar_q, ag_q2, acc_q, _ = ars[1]
+    next(rs_dh)
+    next(ar_i)
+    next(ag_rows)
+    next(rs_dh)
+    next(ar_i)
+    next(rs_dh)
+    next(ag_rows)
+    next(ar_i)
+    d_query = ((dz_col * targ_vec.astype(F32) + v["rsd.1"][0].T) * scale).astype(BF)
+    q_pre = v["q_pre"]
+    q_pre[...] = (v["q_slope"][...] * dot_nt(d_query, w2[...])).astype(BF)
+    weight_grads(turn(tok_ref[...]), turn(d_query), q_pre, v["q_hid"], qsum, parts, 0)
+    zero = jnp.zeros((8, LANES), F32)
+    for dev in range(parts):
+        qsum[dev, 64:, :] = zero + loss if dev == 0 else zero
+    next(ar_q)
+    next(ar_i)
+    next(ag_rows)
+    next(ar_q)
+    next(ar_i)
+    isum_out[me] = acc_i[0]
+    next(ag_i)
+    next(ar_q)
+    next(ag_i)
+    next(ar_q)
+    next(ag_i)
+    next(ar_q)
+    qsum_out[me] = acc_q[0]
+    next(ag_q2)
+    next(ag_i)
+    for g in (ag_rows, rs_dh, ar_i, ag_i, ar_q, ag_q2):
+        for _ in g:
+            pass
+
+
+def step(x, tokens, weights, lq, ids, targ, cid):
+    parts, n_item, _ = x.shape
+    n_tok = tokens.shape[0]
+    n_cand = n_item - n_tok
+    ff = weights[0].shape[1]
+    spec = []
+
+    def add(name, shape, dtype):
+        spec.append((name, pltpu.VMEM(shape, dtype)))
+
+    def add_group(name, items):
+        spec.extend((f"{name}.{i}", s) for i, s in enumerate(items))
+
+    add_group("rs", rs_scratch(n_item, BF))
+    add_group("agq", ag_scratch())
+    add_group("st", [pltpu.VMEM((5, 2, parts, n_tok), F32), pltpu.VMEM((4, 2, parts, n_tok), F32), pltpu.SemaphoreType.DMA((4,)), pltpu.SemaphoreType.DMA((4,))])
+    add_group("rsd", rs_scratch(LANES, F32, n_tok))
+    add_group("agr", ag_scratch())
+    add_group("ai", rs_scratch(64, F32) + ag_scratch())
+    add_group("aq", rs_scratch(72, F32) + ag_scratch())
+    for n, pre in ((n_tok, "q"), (n_item, "i")):
+        add(pre + "_slope", (n, ff), F32)
+        add(pre + "_hid", (n, ff), BF)
+        add(pre + "_pre", (n, ff), BF)
+        add(pre + "_vec", (n, LANES), BF)
+        add(pre + "_grad", (n, LANES), BF)
+    add("q_all", (parts, n_tok, LANES), BF)
+    add("z", (parts, n_cand, n_tok), F32)
+    for name in ("top", "den", "norm"):
+        add(name, (parts, n_tok), F32)
+    add("vec_t", (LANES, n_cand), BF)
+    add("d_acc", (n_cand, LANES), F32)
+    add("dz", (n_cand, n_tok), BF)
+    add("dh", (parts, LANES, n_tok), F32)
+    add("isum", (parts, 64, LANES), F32)
+    add("qsum", (parts, 72, LANES), F32)
+    names = tuple(n for n, _ in spec)
+    outs = (jax.ShapeDtypeStruct((parts, n_item, LANES), BF), jax.ShapeDtypeStruct((parts, 64, LANES), F32), jax.ShapeDtypeStruct((parts, 72, LANES), F32))
+    return comm_call(functools.partial(step_kernel, (n_cand, n_tok, parts), names), "softmax_step", cid, outs, [s for _, s in spec], x, tokens, *weights, lq, ids, targ)
 
 
 def solution(mesh):
@@ -490,59 +689,25 @@
 
     def local_step(tokens, w_one, w_two, wi_one, wi_two, table_loc, cand_ids, log_q, targ_loc):
         my_index = lax.axis_index("dp")
-        rows_loc = table_loc.shape[0]
+        rows_loc, dim = table_loc.shape
         num_tok = tokens.shape[0]
-        tok_total = num_tok * num_dev
         num_cand = cand_ids.shape[0]
         cand_loc = num_cand // num_dev
-        dim = table_loc.shape[1]
-        scale = SCORE_GAIN / math.sqrt(dim)
-        targ_all = ag(targ_loc.reshape(-1, LANES), 1).reshape(-1)
-        ids = jnp.concatenate([cand_ids, targ_all]).reshape(-1, LANES)
+        targ_all = ag(targ_loc.reshape(-1, LANES), 1)
+        ids = jnp.concatenate([cand_ids.reshape(-1, LANES), targ_all.reshape(-1, LANES)])
         base = (my_index * rows_loc).reshape(1).astype(I32)
-        owned, plist, counts = gather(table_loc, ids, base, num_cand)
-        raw_c = rs(owned[:num_cand].reshape(num_dev, cand_loc, dim), 2)
-        raw_t = rs(owned[num_cand:].reshape(num_dev, num_tok, dim), 3)
-        q_pre, q_hidden, query = tower_fwd(tokens, w_one, w_two)
-        query_all = ag(query, 4).reshape(tok_total, dim)
-        raw = jnp.concatenate([raw_c, raw_t])
-        i_pre, i_hidden, vec = tower_fwd(raw, wi_one, wi_two)
-        cand_vec, targ_vec = vec[:cand_loc], vec[cand_loc:]
+        owned, plist, counts = gather(table_loc, ids, base, num_cand, num_dev)
         my_ids = lax.dynamic_slice_in_dim(cand_ids, my_index * cand_loc, cand_loc)
         my_logq = lax.dynamic_slice_in_dim(log_q, my_index * cand_loc, cand_loc)
-        z = jnp.einsum("td,sd->ts", query_all, cand_vec, preferred_element_type=F32) * scale - my_logq[None, :]
-        z = jnp.where(targ_all[:, None] == my_ids[None, :], HIT_VALUE, z)
-        top = jnp.max(z, axis=1)
-        e = jnp.exp(z - top[:, None])
-        den = jnp.sum(e, axis=1)
-        z_targ = jnp.einsum("td,td->t", query, targ_vec, preferred_element_type=F32) * scale
-        mine = my_index * num_tok
-        z_all = lax.dynamic_update_slice_in_dim(jnp.full((tok_total,), -jnp.inf, F32), z_targ, mine, 0)
-        top_t = jnp.maximum(top, z_all)
-        den_t = den * jnp.exp(top - top_t) + jnp.exp(z_all - top_t)
-        st = stats(jnp.stack([top_t, den_t]).reshape(2, -1, LANES), 5).reshape(2, tok_total)
-        factor = jnp.exp(top - st[0]) / st[1] / tok_total
-        dz = (e * factor[:, None]).astype(BF)
-        dh_part = jnp.einsum("ts,sd->td", dz, cand_vec, preferred_element_type=F32)
-        d_cand = (jnp.einsum("ts,td->sd", dz, query_all, preferred_element_type=F32) * scale).astype(BF)
-        my_top = lax.dynamic_slice_in_dim(st[0], mine, num_tok)
-        my_den = lax.dynamic_slice_in_dim(st[1], mine, num_tok)
-        loss_sum = jnp.sum(jnp.log(my_den) + my_top - z_targ)
-        dz_targ = ((jnp.exp(z_targ - my_top) / my_den - 1.0) / tok_total).astype(BF).astype(F32)
-        dh_cand = rs(dh_part.reshape(num_dev, num_tok, dim), 6)
-        d_query = ((dz_targ[:, None] * targ_vec.astype(F32) + dh_cand) * scale).astype(BF)
-        d_targ = (scale * dz_targ[:, None] * query.astype(F32)).astype(BF)
-        dw_one, dw_two = tower_back(tokens, w_two, q_pre, q_hidden, d_query)[1:]
-        i_grad_pre, dwi_one, dwi_two = tower_back(raw, wi_two, i_pre, i_hidden, jnp.concatenate([d_cand, d_targ]))
-        d_raw = jnp.einsum("nf,df->nd", i_grad_pre, wi_one, preferred_element_type=F32).astype(BF)
-        back_c = ag(d_raw[:cand_loc], 7).reshape(num_cand, dim)
-        back_t = ag(d_raw[cand_loc:], 8).reshape(tok_total, dim)
-        d_table = scatter(jnp.concatenate([back_c, back_t]), plist, counts, rows_loc)
-        extra = jnp.zeros((num_dev * 8, LANES), F32).at[0, 0].set(loss_sum)
-        parts = jnp.concatenate([w.reshape(-1, LANES) for w in (dw_one, dw_two, dwi_one, dwi_two)] + [extra])
-        sums = ar(parts.reshape(num_dev, -1, LANES), 9).reshape(-1, LANES)
-        n = dw_one.size // LANES
-        outs = [sums[i * n:(i + 1) * n].reshape(w.shape) for i, w in enumerate((dw_one, dw_two, dwi_one, dwi_two))]
-        return (sums[4 * n, 0] / tok_total, d_table) + tuple(outs)
+        wide = (cand_loc, LANES)
+        back, isum, qsum = step(owned.reshape(num_dev, cand_loc + num_tok, dim), tokens, (w_one, w_two, wi_one, wi_two), jnp.broadcast_to((my_logq * LOG2E)[:, None], wide), jnp.broadcast_to(my_ids[:, None], wide), targ_all.reshape(num_dev, num_tok), 2)
+        d_table = scatter(back.reshape(-1, dim), plist, counts, rows_loc)
+
+        def grads(sums):
+            w = sums[:, :64].reshape(2, 4, 2, 64, LANES).transpose(0, 2, 3, 1, 4).reshape(2, LANES, 4 * LANES)
+            return w[0], w[1].T
+
+        loss = qsum[0, 64, 0] / (num_tok * num_dev)
+        return (loss, d_table) + grads(qsum) + grads(isum)
 
     return jax.shard_map(local_step, mesh=mesh, in_specs=(P("dp", None), P(), P(), P(), P(), P("dp", None), P(), P(), P("dp")), out_specs=(P(), P("dp", None), P(), P(), P(), P()), check_vma=False)

time: 268 us -> 177 us (0.66)
  other arithmetic: 33.5 us -> 2.19 us
  matrix products: 27.5 us -> 0 us
  Pallas kernels: 184 us -> 162 us
  local copies, waits for them, and re-layouts: 18.9 us -> 10.6 us
    dot_general x13 -> x0, matrix products: 27.5 us -> none  [the longest x2 4.76 us: tower_back(): jnp.einsum('nf,nd->fd', hidden, grad_out, preferred_element_type=F32)]
    pallas_call x9 -> x2, Pallas kernels: 146 us -> 124 us  [comm_call(): pl.pallas_call(body, out_shape=out_shape, in_specs=[VM] * len(args), out_...]
    concatenate x1, other arithmetic: 14.2 us -> 1.5 us  [local_step(): jnp.concatenate([cand_ids.reshape(-1, LANES), targ_all.reshape(-1, LANES)])]
    convert_element_type x2 -> x0, other arithmetic: 10.1 us -> none  [the longest x1 9.07 us: local_step(): dz = (e * factor[:, None]).astype(BF)]
    slice x6 -> x4, local copies, waits for them, and re-layouts: 10.5 us -> 2.34 us  [the longest x1 1.19 us: local_step(): loss = qsum[0, 64, 0] / (num_tok * num_dev)]
    reduce_sum x1 -> x0, other arithmetic: 5.48 us -> none  [local_step(): den = jnp.sum(e, axis=1)]
where the time goes in v2:
time: 177 us
  Pallas kernels  162 us (92%)
  local copies, waits for them, and re-layouts  10.6 us (6%)
  between operations  2.5 us (1%)
  other arithmetic  2.19 us (1%)
    pallas_call x2, Pallas kernels, comm_call(): pl.pallas_call(body, out_shape=out_shape, in_specs=[VM] * len(args), out_...  124 us
    pallas_call x1, Pallas kernels, scatter(): pl.pallas_call(functools.partial(scatter_kernel, chunks), out_shape=jax.S...  21.3 us
    pallas_call x1, Pallas kernels, gather(): pl.pallas_call(functools.partial(gather_kernel, chunks, head, parts), out...  16.2 us

profile of v2, /device:TPU:0, one launch (start us, length us, event | category | flops | bytes accessed | tf_op | source)
XLA Modules:
  0.0 176.9 jit_solution(18020191961032717437)
XLA Ops:
  0.6 0.7 dynamic-slice_multiply_fusion
  1.3 0.7 dynamic_slice.7
  2.0 14.5 %all_rows.1 = s32[16,2,128]{2,1,0:T(2,128)} custom-call(s32[2,128]{1,0:T(2,128)} %bitcast.59), custom_call_target="tpu_custom_call" | custom-call | tf_op jit(solution)/shard_map/all_rows/pallas_call | solution.py:406
  16.5 1.3 copy.39
  17.8 1.5 pad_add_fusion.ids_ref
  19.3 1.0 broadcast_in_dim.5.id_ref
  20.3 1.0 broadcast_in_dim.4.lq_ref
  21.3 16.2 %gather_rows.1 = (bf16[20480,128]{1,0:T(8,128)(2,1)}, s32[160,128]{1,0:T(8,128)}, s32[2]{0:T(128)}) custom-call(s32[1]{0:T(128)} %bitcast.base_ref, s32[160,128]{1,0:T(8,128)} %pad_add_fusion.ids_ref, bf16[32768,128]{1,0:T(8,128)(2,1)} %table_ref.1), custom_call_target="tpu_custom_call" | custom-call | tf_op jit(solution)/shard_map/gather_rows/pallas_call | solution.py:114
  37.5 109.5 %softmax_step.1 = (bf16[16,1280,128]{2,1,0:T(8,128)(2,1)}, f32[16,64,128]{2,1,0:T(8,128)}, f32[16,72,128]{2,1,0:T(8,128)}) custom-call(bf16[16,1280,128]{2,1,0:T(8,128)(2,1)} %bitcast.43, bf16[256,128]{1,0:T(8,128)(2,1)} %tok_ref.1, bf16[128,512]{1,0:T(8,128)(2,1)} %w1.1, bf16[512,128]{1,0:T(8,128)(2,1)} %w2.1, bf16[128,512]{1,0:T(8,128)(2,1)} %wi1.1, ...), custom_call_target="tpu_custom_call" | custom-call | tf_op jit(solution)/shard_map/softmax_step/pallas_call | solution.py:406
  147.1 1.2 slice.22
  148.9 1.4 copy.35
  150.4 0.8 copy.22
  151.2 1.1 slice.23
  152.3 0.3 copy.36
  152.7 0.8 copy.21
  153.6 0.8 copy_bitcast_fusion.2
  154.4 21.3 %scatter_rows.1 = f32[32768,128]{1,0:T(8,128)} custom-call(s32[2]{0:T(128)} %get-tuple-element.14.cnt_ref, s32[160,128]{1,0:T(8,128)} %get-tuple-element.15.list_ref, bf16[20480,128]{1,0:T(8,128)(2,1)} %bitcast.44), custom_call_target="tpu_custom_call" | custom-call | tf_op jit(solution)/shard_map/scatter_rows/pallas_call | solution.py:202
  (4 shorter events, 0.1 us)

commit v3 on v2

v3 whole, which is shorter than its diff:
```python
import functools
import math
import jax
import jax.numpy as jnp
from jax import lax
from jax.experimental import pallas as pl
from jax.experimental.pallas import tpu as pltpu
from jax.sharding import PartitionSpec as P

SCORE_GAIN = 3.0
HIT_VALUE = -1e9
LANES = 128
VMEM_CAP = 60 * 1024 * 1024
BF = jnp.bfloat16
F32 = jnp.float32
I32 = jnp.int32
VM = pl.BlockSpec(memory_space=pltpu.VMEM)
SM = pl.BlockSpec(memory_space=pltpu.SMEM)
HB = pl.BlockSpec(memory_space=pl.ANY)
BLK = 256


def compact(loc, num_rows, parts, head):
    nr = loc.shape[0]
    own = jnp.where((loc >= 0) & (loc < num_rows), 1.0, 0.0)
    own16 = own.astype(BF)
    tri = jnp.where(lax.broadcasted_iota(I32, (LANES, LANES), 0) < lax.broadcasted_iota(I32, (LANES, LANES), 1), 1.0, 0.0).astype(BF)
    within = jnp.dot(own16, tri, preferred_element_type=F32)
    low = jnp.where(lax.broadcasted_iota(I32, (nr, nr), 1) < lax.broadcasted_iota(I32, (nr, nr), 0), 1.0, 0.0).astype(BF)
    before = jnp.sum(jnp.dot(low, own16, preferred_element_type=F32), axis=1, keepdims=True)
    lane = lax.broadcasted_iota(I32, (nr, LANES), 1)
    flat = lax.broadcasted_iota(I32, (nr, LANES), 0) * LANES + lane
    disp = flat - (within + before).astype(I32)
    n_head, n_tail = head // parts, (nr * LANES - head) // parts
    late = flat - head
    pos = jnp.where(flat < head, flat + flat // n_head * n_tail, late + (late // n_tail + 1) * n_head)
    val = jnp.where(own > 0, pos * 32768 + loc, -1)
    total = jnp.sum(own).astype(I32)

    def back(x, s):
        if s >= LANES:
            return pltpu.roll(x, nr - s // LANES, axis=0)
        here = pltpu.roll(x, LANES - s, axis=1)
        return jnp.where(lane < LANES - s, here, pltpu.roll(here, nr - 1, axis=0))

    bit = 0
    while (1 << bit) < nr * LANES:
        val_b, disp_b = back(val, 1 << bit), back(disp, 1 << bit)
        take = (val_b >= 0) & (((disp_b >> bit) & 1) == 1)
        stay = ((disp >> bit) & 1) == 0
        val = jnp.where(take, val_b, jnp.where(stay, val, -1))
        disp = jnp.where(take, disp_b, disp)
        bit += 1
    return jnp.where(flat < total, val, nr * LANES * 32768), own, total


def gather_kernel(chunks, cand_ref, targ_ref, table_ref, out_ref, list_ref, cnt_ref, ids_ref, stage, tab, dense, plist, sem, psem):
    rows = tab.shape[0]
    npos = out_ref.shape[0]
    cr = rows // chunks

    def load(c):
        return pltpu.make_async_copy(table_ref.at[pl.ds(c * cr, cr), :], stage.at[pl.ds(c * cr, cr), :], sem.at[c])

    for c in range(chunks):
        load(c).start()
    parts, sub, _ = targ_ref.shape
    n_head = cand_ref.shape[0]
    head = n_head * LANES
    ids_ref[:n_head, :] = cand_ref[...]
    for d in range(parts):
        ids_ref[n_head + d * sub:n_head + (d + 1) * sub, :] = targ_ref[d]
    packed, own, total = compact(ids_ref[...] - lax.axis_index("dp") * rows, rows, parts, head)
    list_ref[...] = packed
    cnt_ref[0] = jnp.sum(own[:head // LANES]).astype(I32)
    cnt_ref[1] = total
    to_smem = pltpu.make_async_copy(list_ref, plist, psem)
    to_smem.start()

    def zero(i, _):
        dense[pl.ds(pl.multiple_of(i * BLK, BLK), BLK), :] = jnp.zeros((BLK, LANES), F32)
        return 0

    lax.fori_loop(0, npos // BLK, zero, 0)
    for c in range(chunks):
        load(c).wait()

        def conv(i, _, c=c):
            s = pl.ds(pl.multiple_of(c * cr + i * BLK, BLK), BLK)
            tab[s, :] = stage[s, :].astype(F32)
            return 0

        lax.fori_loop(0, cr // BLK, conv, 0)
    to_smem.wait()

    def pick(i, _):
        vals = []
        for u in range(LANES):
            w = plist[i, u]
            vals.append((w >> 15, tab[pl.ds(w & 32767, 1), :]))
        for p, v in vals:
            dense[pl.ds(p, 1), :] = v
        return 0

    lax.fori_loop(0, (total + LANES - 1) // LANES, pick, 0)

    def pack(i, _):
        s = pl.ds(pl.multiple_of(i * BLK, BLK), BLK)
        out_ref[s, :] = dense[s, :].astype(BF)
        return 0

    lax.fori_loop(0, npos // BLK, pack, 0)


def gather(table, cand, targ):
    rows = table.shape[0]
    nr = cand.shape[0] + targ.shape[0] * targ.shape[1]
    npos = nr * LANES
    chunks = 8
    return pl.pallas_call(
        functools.partial(gather_kernel, chunks),
        out_shape=(jax.ShapeDtypeStruct((npos, LANES), BF), jax.ShapeDtypeStruct((nr, LANES), I32), jax.ShapeDtypeStruct((2,), I32)),
        in_specs=[VM, VM, HB],
        out_specs=(VM, VM, SM),
        scratch_shapes=[pltpu.VMEM((nr, LANES), I32), pltpu.VMEM((rows, LANES), BF), pltpu.VMEM((rows, LANES), F32), pltpu.VMEM((npos + 8, LANES), F32), pltpu.SMEM((nr, LANES), I32), pltpu.SemaphoreType.DMA((chunks,)), pltpu.SemaphoreType.DMA],
        compiler_params=pltpu.CompilerParams(vmem_limit_bytes=VMEM_CAP),
        name="gather_rows",
    )(cand, targ, table)


ADDS = 4


def scatter_kernel(chunks, cnt_ref, list_ref, grad_ref, *refs):
    n = (len(refs) - 6) // 2
    passed, (out_ref, *kept, acc, grad, plist, sem, psem) = refs[:n], refs[n:]
    rows = out_ref.shape[0]
    npos = grad_ref.shape[0]
    to_smem = pltpu.make_async_copy(list_ref, plist, psem)
    to_smem.start()

    def zero(i, _):
        acc[pl.ds(pl.multiple_of(i * BLK, BLK), BLK), :] = jnp.zeros((BLK, LANES), F32)
        return 0

    lax.fori_loop(0, rows // BLK, zero, 0)

    def conv(i, _):
        s = pl.ds(pl.multiple_of(i * BLK, BLK), BLK)
        grad[s, :] = grad_ref[s, :].astype(F32)
        return 0

    lax.fori_loop(0, npos // BLK, conv, 0)
    grad[npos:, :] = jnp.zeros((8, LANES), F32)
    to_smem.wait()
    nhead = cnt_ref[0]
    total = cnt_ref[1]

    def put(i, _):
        vals = []
        for u in range(LANES):
            w = plist[i, u]
            vals.append((w & 32767, grad[pl.ds(w >> 15, 1), :]))
        for r, v in vals:
            acc[pl.ds(r, 1), :] = v
        return 0

    lax.fori_loop(0, nhead // LANES, put, 0)

    def add_one(i, _):
        w = plist[i >> 7, i & 127]
        r = pl.ds(w & 32767, 1)
        acc[r, :] = acc[r, :] + grad[pl.ds(w >> 15, 1), :]
        return 0

    def add_row(i, _):
        for j in range(0, LANES, ADDS):
            words = [plist[i, j + u] for u in range(ADDS)]
            rs = [w & 32767 for w in words]
            gs = [grad[pl.ds(w >> 15, 1), :] for w in words]
            outs = []
            for u in range(ADDS):
                v = acc[pl.ds(rs[u], 1), :] + gs[u]
                for t in range(u):
                    v = v + jnp.where(rs[t] == rs[u], gs[t], 0.0)
                outs.append(v)
            for u in range(ADDS):
                acc[pl.ds(rs[u], 1), :] = outs[u]
        return 0

    begin = nhead // LANES * LANES
    split = jnp.minimum((nhead + LANES - 1) // LANES * LANES, total)
    lax.fori_loop(begin, split, add_one, 0)
    lax.fori_loop((split + LANES - 1) // LANES, (total + LANES - 1) // LANES, add_row, 0)
    cr = rows // chunks

    def store(c):
        return pltpu.make_async_copy(acc.at[pl.ds(c * cr, cr), :], out_ref.at[pl.ds(c * cr, cr), :], sem.at[c])

    for c in range(chunks):
        store(c).start()
    for src, dst in zip(passed, kept):
        dst[...] = src[...]
    for c in range(chunks):
        store(c).wait()


def scatter(grads, plist, counts, rows, passed):
    nr = plist.shape[0]
    npos = nr * LANES
    chunks = 8
    return pl.pallas_call(
        functools.partial(scatter_kernel, chunks),
        out_shape=(jax.ShapeDtypeStruct((rows, LANES), F32),) + tuple(jax.ShapeDtypeStruct(p.shape, p.dtype) for p in passed),
        in_specs=[SM, HB, VM] + [VM] * len(passed),
        out_specs=(HB,) + (VM,) * len(passed),
        scratch_shapes=[pltpu.VMEM((rows, LANES), F32), pltpu.VMEM((npos + 8, LANES), F32), pltpu.SMEM((nr, LANES), I32), pltpu.SemaphoreType.DMA((chunks,)), pltpu.SemaphoreType.DMA],
        compiler_params=pltpu.CompilerParams(vmem_limit_bytes=VMEM_CAP),
        name="scatter_rows",
    )(counts, plist, grads, *passed)


MESHID = pl.DeviceIdType.MESH
CHIP_DIMS = (1, 2, 4)
SLOTS = tuple(range(8))
CORE_ORDER = (7, 3, 5, 6, 1, 2, 4, 0)
RS_BASE = (0, 4, 6)


def place():
    me = lax.axis_index("dp")
    core = lax.rem(me, 2)
    chip = me // 2
    sign = {d: 1 - 2 * lax.rem(chip // d, 2) for d in CHIP_DIMS}
    return me, core, chip, sign


def chip_at(chip, sign, s):
    for d in CHIP_DIMS:
        if s & d:
            chip = chip + d * sign[d]
    return chip


def enter(extra=()):
    me, core, chip, sign = place()
    barrier = pltpu.get_barrier_semaphore()
    peers = [me + 1 - 2 * core] + [2 * chip_at(chip, sign, d) + core for d in CHIP_DIMS] + list(extra)
    for peer in peers:
        pl.semaphore_signal(barrier, inc=1, device_id=(peer,), device_id_type=MESHID)
    pl.semaphore_wait(barrier, len(peers))


def order_of(k):
    return tuple(CHIP_DIMS[(k + i) % 3] for i in range(3))


def thirds(rows, unit, a=0):
    base = rows // unit
    cuts = [(base * i // 3) * unit for i in range(4)]
    return [(a, cuts[i], cuts[i + 1] - cuts[i], i) for i in range(3)]


def remote(src, dst, send, recv, peer):
    return pltpu.make_async_remote_copy(src_ref=src, dst_ref=dst, send_sem=send, recv_sem=recv, device_id=(peer,), device_id_type=MESHID)


def stage_slots(order, t):
    dims = order_of(order)
    live = [s for s in SLOTS if all(not s & d for d in dims[:t])]
    return [(s, s ^ dims[t]) for s in live if s & dims[t]]


def rs_scratch(arrays, num):
    out = []
    for rows, width, dtype in arrays:
        out += [pltpu.VMEM((8, rows, width), dtype), pltpu.VMEM((8, rows, width), dtype), pltpu.VMEM((7, rows, width), dtype)]
    n = len(arrays)
    dma = pltpu.SemaphoreType.DMA
    return out + [dma((n, 8)), dma((n, 8)), dma((num, 7)), dma((num, 7))]


def reduce_scatter_steps(get, pieces, scratch):
    csend_s, crecv_s, send_s, recv_s = scratch[-4:]
    me, core, chip, sign = place()
    other = me + 1 - 2 * core
    num = len(pieces)
    arrays = range((len(scratch) - 4) // 3)
    crecv, acc, recv = ([scratch[3 * a + i] for a in arrays] for i in range(3))
    started = []

    def core_copy(s, a):
        return remote(get(2 * chip_at(chip, sign, s) + 1 - core, a), crecv[a].at[s], csend_s.at[a, s], crecv_s.at[a, s], other)

    def ici_copy(k, t, i, s):
        a, off, ln, order = pieces[k]
        slot = RS_BASE[t] + i
        peer = 2 * chip_at(chip, sign, order_of(order)[t]) + core
        return remote(acc[a].at[s, pl.ds(off, ln), :], recv[a].at[slot, pl.ds(off, ln), :], send_s.at[k, slot], recv_s.at[k, slot], peer)

    def go(c):
        c.start()
        started.append(c)

    for s in CORE_ORDER:
        for a in arrays:
            go(core_copy(s, a))
    yield
    for s in CORE_ORDER:
        for a in arrays:
            core_copy(s, a).wait_recv()
            acc[a][s] = get(2 * chip_at(chip, sign, s) + core, a)[...] + crecv[a][s]
        for k in range(num):
            for i, (src, dst) in enumerate(stage_slots(pieces[k][3], 0)):
                if src == s:
                    go(ici_copy(k, 0, i, s))
    yield
    for t in range(3):
        for i in reversed(range(4 >> t)):
            for k in range(num):
                a, off, ln, order = pieces[k]
                src, dst = stage_slots(order, t)[i]
                ici_copy(k, t, i, src).wait_recv()
                p = pl.ds(off, ln)
                acc[a][dst, p, :] = acc[a][dst, p, :] + recv[a][RS_BASE[t] + i, p, :]
                if t < 2:
                    for i2, (src2, dst2) in enumerate(stage_slots(order, t + 1)):
                        if src2 == dst:
                            go(ici_copy(k, t + 1, i2, dst))
        yield
    for c in started:
        c.wait_send()


def ag_scratch(num):
    return [pltpu.SemaphoreType.DMA((num, 8))] * 4


def all_gather_steps(own, out, pieces, scratch):
    csend_s, crecv_s, send_s, recv_s = scratch
    me, core, chip, sign = place()
    other = me + 1 - 2 * core
    num = len(pieces)
    started = []

    def ref(k, s, c):
        a, off, ln, _ = pieces[k]
        return out(2 * chip_at(chip, sign, s) + c, a).at[pl.ds(off, ln), :]

    def source(k, s):
        a, off, ln, _ = pieces[k]
        return own(a).at[pl.ds(off, ln), :] if s == 0 else ref(k, s, core)

    def go(c):
        c.start()
        started.append(c)

    def core_send(k, s):
        go(remote(source(k, s), ref(k, s, core), csend_s.at[k, s], crecv_s.at[k, s], other))

    def send(k, t, s):
        d = order_of(pieces[k][3])[t]
        peer = 2 * chip_at(chip, sign, d) + core
        go(remote(source(k, s), ref(k, s, core), send_s.at[k, s ^ d], recv_s.at[k, s ^ d], peer))

    def arrive(k, s):
        there = ref(k, s, core)
        remote(there, there, send_s.at[k, s], recv_s.at[k, s], other).wait_recv()
        core_send(k, s)

    plan = (((), (0, 0)), ((), (1, 0)), ((1,), (1, 1)), ((), (2, 0)), ((), (2, 1)), ((2,), (2, 2)), ((3,), (2, 3)), ((4, 5, 6, 7), None))
    for i, (waits, sends) in enumerate(plan):
        for j in waits or (None,):
            for k in range(num):
                d = order_of(pieces[k][3])

                def slot(bits):
                    return sum(d[b] for b in range(3) if bits >> b & 1)

                if j is not None:
                    arrive(k, slot(j))
                if sends is not None:
                    send(k, sends[0], slot(sends[1]))
                if i == 0:
                    core_send(k, 0)
        yield
    for k in range(num):
        for s in SLOTS:
            there = ref(k, s, 1 - core)
            remote(there, there, csend_s.at[k, s], crecv_s.at[k, s], other).wait_recv()
    for c in started:
        c.wait_send()


def drain(*steps):
    live = list(steps)
    while live:
        live = [g for g in live if next(g, StopIteration) is not StopIteration]


def kernel_call(body, name, cid, out_shape, scratch, *args):
    names = tuple(n for n, _ in scratch)

    def kernel(*refs):
        n = len(args) + len(jax.tree.leaves(out_shape))
        body(*refs[:n], dict(zip(names, refs[n:])))

    return pl.pallas_call(
        kernel,
        out_shape=out_shape,
        in_specs=[VM] * len(args),
        out_specs=jax.tree.map(lambda _: VM, out_shape),
        scratch_shapes=[s for _, s in scratch],
        compiler_params=pltpu.CompilerParams(collective_id=cid, has_side_effects=True, vmem_limit_bytes=VMEM_CAP),
        name=name,
    )(*args)


def grouped(name, items):
    return [(f"{name}.{i}", s) for i, s in enumerate(items)]


def group(scratch, name):
    return [v for k, v in scratch.items() if k.startswith(name + ".")]
LOG2E = 1.4426950408889634
GELU_C = math.sqrt(2.0 / math.pi)
GELU_A = 0.044715
ROW_BLK = 256
COL_BLK = 128


def gelu_both(x):
    x2 = x * x
    t = jnp.tanh(GELU_C * (x + GELU_A * (x2 * x)))
    half = 0.5 * (1.0 + t)
    return x * half, half + (0.5 * GELU_C) * x * (1.0 - t * t) * (1.0 + (3.0 * GELU_A) * x2)


def dot_nn(a, b):
    return jnp.dot(a, b, preferred_element_type=F32)


def dot_nt(a, b):
    return lax.dot_general(a, b, (((1,), (1,)), ((), ())), preferred_element_type=F32)


def turn(x):
    return x.astype(F32).T.astype(BF)


def row_blocks(rows, body):
    def blk(i, _):
        body(pl.ds(pl.multiple_of(i * ROW_BLK, ROW_BLK), ROW_BLK))
        return 0

    lax.fori_loop(0, rows // ROW_BLK, blk, 0)


def tower_into(rows, load, w_in, w_out, slope_ref, hid_ref, out_ref):
    def blk(s):
        act, slope = gelu_both(dot_nn(load(s), w_in[...]))
        slope_ref[s, :] = slope
        hid_ref[s, :] = act.astype(BF)
        out_ref[s, :] = dot_nn(hid_ref[s, :], w_out[...]).astype(BF)

    row_blocks(rows, blk)


def start_kernel(tok_ref, w1, w2, targ_ref, targ_out, q_out, v):
    enter()
    me = lax.axis_index("dp")
    targ_out[me] = targ_ref[...]
    sub = targ_ref.shape[0]
    n_tok = tok_ref.shape[0]
    ag_t = all_gather_steps(lambda a: targ_ref, lambda dev, a: targ_out.at[dev], [(0, 0, sub, 0)], group(v, "agt"))
    next(ag_t)
    next(ag_t)
    tower_into(n_tok, lambda s: tok_ref[s, :], w1, w2, v["slope"], v["hid"], v["vec"])
    q_out[me] = v["vec"][...]
    ag_q = all_gather_steps(lambda a: v["vec"], lambda dev, a: q_out.at[dev], thirds(n_tok, 16), group(v, "agq"))
    drain(ag_t, ag_q)


def start(tokens, w_one, w_two, targ, parts, cid):
    n_tok = tokens.shape[0]
    ff = w_one.shape[1]
    scratch = grouped("agt", ag_scratch(1)) + grouped("agq", ag_scratch(3))
    scratch += [("slope", pltpu.VMEM((n_tok, ff), F32)), ("hid", pltpu.VMEM((n_tok, ff), BF)), ("vec", pltpu.VMEM((n_tok, LANES), BF))]
    outs = (jax.ShapeDtypeStruct((parts,) + targ.shape, I32), jax.ShapeDtypeStruct((parts, n_tok, LANES), BF))
    return kernel_call(start_kernel, "start_step", cid, outs, scratch, tokens, w_one, w_two, targ)


def weight_grads(row_t, grad_t, pre_ref, hid_ref, in_ref, out_ref):
    parts, n_in, _ = in_ref.shape
    n_out = out_ref.shape[1]
    d_in = dot_nn(row_t, pre_ref[...])
    d_out = dot_nn(grad_t, hid_ref[...]).T
    for dev in range(parts):
        in_ref[dev] = d_in[dev * n_in:(dev + 1) * n_in, :]
        out_ref[dev] = d_out[dev * n_out:(dev + 1) * n_out, :]


def step_kernel(x_ref, tok_ref, w1, w2, wi1, wi2, q_all, cand_ref, logq_ref, targ_ref, rows_out, di_in_out, di_out_out, dq_in_out, dq_out_out, loss_out, v):
    parts, n_item, _ = x_ref.shape
    n_tok = tok_ref.shape[0]
    n_cand = n_item - n_tok
    total = float(n_tok * parts)
    scale = SCORE_GAIN / math.sqrt(LANES)
    me, core, chip, sign = place()
    x_chip = 2 * chip_at(chip, sign, 1)
    diag = 2 * chip_at(chip, sign, 6) + core
    rounds = ((me + 1 - 2 * core, x_chip + core, x_chip + 1 - core), (2 * chip_at(chip, sign, 2) + core, 2 * chip_at(chip, sign, 4) + core, diag))
    enter((x_chip + 1 - core, diag))
    rs_rows = reduce_scatter_steps(lambda dev, a: x_ref.at[dev], thirds(n_item, 16), group(v, "rs"))
    next(rs_rows)
    tower_into(n_tok, lambda s: tok_ref[s, :], w1, w2, v["q_slope"], v["q_hid"], v["q_vec"])
    next(rs_rows)
    n_sub = n_cand // LANES
    for r in range(n_sub):
        s = pl.ds(r * LANES, LANES)
        row = pl.ds(me * n_sub + r, 1)
        v["lq"][s, :] = jnp.broadcast_to(logq_ref[row, :] * LOG2E, (LANES, LANES)).T
        v["ids"][s, :] = jnp.broadcast_to(cand_ref[row, :].astype(F32), (LANES, LANES)).T
    drain(rs_rows)
    raw = v["rs.1"].at[0]
    tower_into(n_item, lambda s: raw[s, :], wi1, wi2, v["i_slope"], v["i_hid"], v["i_vec"])
    vec = v["i_vec"]
    z_ref, top_ref, den_ref, own_ref = v["z"], v["top"], v["den"], v["own"]
    own = pl.ds(me, 1)
    targ_vec = vec[pl.ds(n_cand, n_tok), :]
    q_own = v["q_vec"][...]
    eye = lax.broadcasted_iota(I32, (n_tok, n_tok), 0) == lax.broadcasted_iota(I32, (n_tok, n_tok), 1)
    z_own = jnp.sum(jnp.where(eye, dot_nt(targ_vec, q_own), 0.0), axis=0, keepdims=True) * (scale * LOG2E)
    own_ref[...] = jnp.full(own_ref.shape, -jnp.inf, F32)
    own_ref[own, :] = z_own

    def pass_one(t, _):
        q_t = q_all[t]
        targ = jnp.concatenate([targ_ref[t, pl.ds(i, 1), :] for i in range(n_tok // LANES)], axis=1).astype(F32)
        z_t = own_ref[pl.ds(t, 1), :]
        top8 = jnp.broadcast_to(z_t, (8, n_tok))
        for j in range(n_cand // COL_BLK):
            s = pl.ds(j * COL_BLK, COL_BLK)
            lq = jnp.concatenate([v["lq"][s, :]] * (n_tok // LANES), axis=1)
            ids = jnp.concatenate([v["ids"][s, :]] * (n_tok // LANES), axis=1)
            z = dot_nt(vec[s, :], q_t) * (scale * LOG2E) - lq
            z = jnp.where(ids == targ, HIT_VALUE * LOG2E, z)
            z_ref[t, s, :] = z
            top8 = jnp.maximum(top8, jnp.max(z.reshape(COL_BLK // 8, 8, n_tok), axis=0))
        top = jnp.max(top8, axis=0, keepdims=True)
        den8 = jnp.zeros((8, n_tok), F32)
        for j in range(n_cand // COL_BLK):
            e = jnp.exp2(z_ref[t, pl.ds(j * COL_BLK, COL_BLK), :] - top)
            den8 = den8 + jnp.sum(e.reshape(COL_BLK // 8, 8, n_tok), axis=0)
        top_ref[pl.ds(t, 1), :] = top
        den_ref[pl.ds(t, 1), :] = jnp.sum(den8, axis=0, keepdims=True) + jnp.exp2(z_t - top)
        return 0

    lax.fori_loop(0, parts, pass_one, 0)
    held, got, st_send, st_recv = group(v, "st")
    held[0, 0] = top_ref[...]
    held[0, 1] = den_ref[...]
    for r, peers in enumerate(rounds):
        copies = [remote(held.at[r], got.at[r, i], st_send.at[r, i], st_recv.at[r, i], peer) for i, peer in enumerate(peers)]
        for c in copies:
            c.start()
        for c in copies:
            c.wait()
        tops = [held[r, 0]] + [got[r, i, 0] for i in range(3)]
        dens = [held[r, 1]] + [got[r, i, 1] for i in range(3)]
        top = jnp.maximum(jnp.maximum(tops[0], tops[1]), jnp.maximum(tops[2], tops[3]))
        held[r + 1, 0] = top
        held[r + 1, 1] = sum(d * jnp.exp2(m - top) for m, d in zip(tops, dens))
    norm = v["norm"]
    norm[...] = held[2, 0] + jnp.log2(held[2, 1] * total)
    top_ref[...] = held[2, 0]
    den_ref[...] = held[2, 1]
    lse = top_ref[own, :] + jnp.log2(den_ref[own, :])
    loss = jnp.sum(lse - z_own, axis=1, keepdims=True) * (1.0 / (LOG2E * total))
    dz_row = ((jnp.exp2(z_own - top_ref[own, :]) / den_ref[own, :] - 1.0) * (1.0 / total)).astype(BF).astype(F32)
    dz_col = jnp.sum(jnp.where(eye, dz_row, 0.0), axis=1, keepdims=True)
    grad = v["i_grad"]
    grad[pl.ds(n_cand, n_tok), :] = (scale * dz_col * q_own.astype(F32)).astype(BF)
    vec_t = v["vec_t"]
    vec_t[...] = turn(vec[:n_cand, :])
    d_acc, dz_s, dh = v["d_acc"], v["dz"], v["dh"]
    d_acc[...] = jnp.zeros_like(d_acc)

    def pass_two(t, _):
        shift = norm[pl.ds(t, 1), :]
        for j in range(n_cand // COL_BLK):
            s = pl.ds(j * COL_BLK, COL_BLK)
            dz_s[s, :] = jnp.exp2(z_ref[t, s, :] - shift).astype(BF)
        d_acc[...] += dot_nn(dz_s[...], q_all[t])
        dh[t] = dot_nn(vec_t[...], dz_s[...])
        return 0

    lax.fori_loop(0, parts, pass_two, 0)
    rs_dh = reduce_scatter_steps(lambda dev, a: dh.at[dev], thirds(LANES, 8), group(v, "rsd"))
    next(rs_dh)
    grad[pl.ds(0, n_cand), :] = (d_acc[...] * scale).astype(BF)
    i_pre, i_slope = v["i_pre"], v["i_slope"]

    def pre_grad(s):
        i_pre[s, :] = (i_slope[s, :] * dot_nt(grad[s, :], wi2[...])).astype(BF)

    row_blocks(n_item, pre_grad)
    next(rs_dh)
    mine = rows_out.at[me]

    def input_grad(s):
        mine[s, :] = dot_nt(i_pre[s, :], wi1[...]).astype(BF)

    row_blocks(n_item, input_grad)
    next(rs_dh)
    ag_rows = all_gather_steps(lambda a: mine, lambda dev, a: rows_out.at[dev], thirds(n_item, 16), group(v, "agr"))
    next(ag_rows)
    weight_grads(turn(raw[...]), turn(grad[...]), i_pre, v["i_hid"], v["di_in"], v["di_out"])
    next(rs_dh)
    next(ag_rows)

    def sum_all(name, parts_in, orders, outs):
        pieces = [(a, 0, r.shape[1], o) for a, (r, o) in enumerate(zip(parts_in, orders))]
        refs = group(v, name)
        sums = [refs[3 * a + 1].at[0] for a in range(len(parts_in))]
        first = reduce_scatter_steps(lambda dev, a: parts_in[a].at[dev], pieces, refs[:-4])
        yield from (x for _, x in zip(range(5), first))
        for a, out in enumerate(outs):
            out[me] = sums[a][...]
        yield from all_gather_steps(lambda a: sums[a], lambda dev, a: outs[a].at[dev], pieces, refs[-4:])
        for _ in first:
            pass

    ar_i = sum_all("ai", (v["di_in"], v["di_out"]), (0, 1), (di_in_out, di_out_out))
    next(ar_i)
    next(rs_dh)
    d_query = ((dz_col * targ_vec.astype(F32) + v["rsd.1"][0].T) * scale).astype(BF)
    q_pre = v["q_pre"]
    q_pre[...] = (v["q_slope"][...] * dot_nt(d_query, w2[...])).astype(BF)
    weight_grads(turn(tok_ref[...]), turn(d_query), q_pre, v["q_hid"], v["dq_in"], v["dq_out"])
    loss_part = v["loss"]
    loss_part[...] = jnp.zeros_like(loss_part)
    loss_part[0] = jnp.broadcast_to(loss, loss_part.shape[1:])
    ar_q = sum_all("aq", (v["dq_in"], v["dq_out"], loss_part), (1, 2, 0), (dq_in_out, dq_out_out, loss_out))
    drain(ar_q, ar_i, ag_rows, rs_dh)


def step(x, tokens, weights, q_all, cand, logq, targ, cid):
    parts, n_item, _ = x.shape
    n_tok = tokens.shape[0]
    n_cand = n_item - n_tok
    ff = weights[0].shape[1]
    dma = pltpu.SemaphoreType.DMA
    n_in, n_out = LANES // parts, ff // parts
    w_parts = [(n_in, ff, F32), (n_out, LANES, F32)]
    spec = grouped("rs", rs_scratch([(n_item, LANES, BF)], 3))
    spec += grouped("st", [pltpu.VMEM((3, 2, parts, n_tok), F32), pltpu.VMEM((2, 3, 2, parts, n_tok), F32), dma((2, 3)), dma((2, 3))])
    spec += grouped("rsd", rs_scratch([(LANES, n_tok, F32)], 3))
    spec += grouped("agr", ag_scratch(3))
    spec += grouped("ai", rs_scratch(w_parts, 2) + ag_scratch(2))
    spec += grouped("aq", rs_scratch(w_parts + [(8, LANES, F32)], 3) + ag_scratch(3))

    def add(name, shape, dtype=F32):
        spec.append((name, pltpu.VMEM(shape, dtype)))

    for n, pre in ((n_tok, "q"), (n_item, "i")):
        add(pre + "_slope", (n, ff))
        add(pre + "_hid", (n, ff), BF)
        add(pre + "_pre", (n, ff), BF)
        add(pre + "_vec", (n, LANES), BF)
        add("d" + pre + "_in", (parts, n_in, ff))
        add("d" + pre + "_out", (parts, n_out, LANES))
    add("i_grad", (n_item, LANES), BF)
    add("loss", (parts, 8, LANES))
    for name in ("lq", "ids", "d_acc"):
        add(name, (n_cand, LANES))
    add("z", (parts, n_cand, n_tok))
    for name in ("top", "den", "norm", "own"):
        add(name, (parts, n_tok))
    add("vec_t", (LANES, n_cand), BF)
    add("dz", (n_cand, n_tok), BF)
    add("dh", (parts, LANES, n_tok))
    sums = (jax.ShapeDtypeStruct((parts, n_in, ff), F32), jax.ShapeDtypeStruct((parts, n_out, LANES), F32))
    outs = (jax.ShapeDtypeStruct((parts, n_item, LANES), BF),) + sums + sums + (jax.ShapeDtypeStruct((parts, 8, LANES), F32),)
    return kernel_call(step_kernel, "softmax_step", cid, outs, spec, x, tokens, *weights, q_all, cand, logq, targ)


def solution(mesh):
    num_dev = mesh.shape["dp"]

    def local_step(tokens, w_one, w_two, wi_one, wi_two, table_loc, cand_ids, log_q, targ_loc):
        rows_loc, dim = table_loc.shape
        n_item = cand_ids.shape[0] // num_dev + tokens.shape[0]
        cand = cand_ids.reshape(-1, LANES)
        targ, q_all = start(tokens, w_one, w_two, targ_loc.reshape(-1, LANES), num_dev, 1)
        owned, plist, counts = gather(table_loc, cand, targ)
        back, *sums = step(owned.reshape(num_dev, n_item, dim), tokens, (w_one, w_two, wi_one, wi_two), q_all, cand, log_q.reshape(-1, LANES), targ, 2)
        d_table, di_in, di_out, dq_in, dq_out, loss = scatter(back.reshape(-1, dim), plist, counts, rows_loc, sums)
        shaped = [g.reshape(w.shape) for g, w in zip((dq_in, dq_out, di_in, di_out), (w_one, w_two, wi_one, wi_two))]
        return (loss[0, 0, 0], d_table) + tuple(shaped)

    return jax.shard_map(local_step, mesh=mesh, in_specs=(P("dp", None), P(), P(), P(), P(), P("dp", None), P(), P(), P("dp")), out_specs=(P(), P("dp", None), P(), P(), P(), P()), check_vma=False)
```

time: 177 us -> 157 us (0.89)
  local copies, waits for them, and re-layouts: 10.6 us -> 1.18 us
  Pallas kernels: 162 us -> 154 us
  other arithmetic: 2.19 us -> 0 us
  between operations: 2.5 us -> 0.66 us
    pallas_call x4, Pallas kernels: 162 us -> 154 us  [the longest x2 116 us: kernel_call(): pl.pallas_call(kernel, out_shape=out_shape, in_specs=[VM] * len(args), ou...]
    unnamed x5 -> x0, local copies, waits for them, and re-layouts: 3.04 us -> none
    broadcast_in_dim x2 -> x0, local copies, waits for them, and re-layouts: 1.99 us -> none  [the longest x1 1.01 us: local_step(): jnp.broadcast_to(my_ids[:, None], wide)]
where the time goes in v3:
time: 157 us; the launch traced here: 156 us
  Pallas kernels  154 us (98%)
    pallas_call x2, Pallas kernels, kernel_call(): pl.pallas_call(kernel, out_shape=out_shape, in_specs=[VM] * len(args), ou...  116 us
    pallas_call x1, Pallas kernels, scatter(): pl.pallas_call(functools.partial(scatter_kernel, chunks), out_shape=(jax....  22.2 us
    pallas_call x1, Pallas kernels, gather(): pl.pallas_call(functools.partial(gather_kernel, chunks), out_shape=(jax.S...  16 us

profile of v3, /device:TPU:0, one launch (start us, length us, event | category | flops | bytes accessed | tf_op | source)
XLA Modules:
  0.0 156.2 jit_solution(6075944023566986587)
XLA Ops:
  0.6 20.5 %start_step.1 = (s32[16,2,128]{2,1,0:T(2,128)}, bf16[16,256,128]{2,1,0:T(8,128)(2,1)}) custom-call(bf16[256,128]{1,0:T(8,128)(2,1)} %refs_1_.3, bf16[128,512]{1,0:T(8,128)(2,1)} %refs_2_.3, bf16[512,128]{1,0:T(8,128)(2,1)} %refs_3_.1, s32[2,128]{1,0:T(2,128)} %bitcast.15), custom_call_target="tpu_custom_call" | custom-call | tf_op jit(solution)/shard_map/start_step/pallas_call | solution.py:408
  21.2 16.0 %gather_rows.1 = (bf16[20480,128]{1,0:T(8,128)(2,1)}, s32[160,128]{1,0:T(8,128)}, s32[2]{0:T(128)}) custom-call(s32[128,128]{1,0:T(8,128)} %bitcast.12, s32[16,2,128]{2,1,0:T(2,128)} %get-tuple-element.23.targ_ref.refs_9_, bf16[32768,128]{1,0:T(8,128)(2,1)} %table_ref.1), custom_call_target="tpu_custom_call" | custom-call | tf_op jit(solution)/shard_map/gather_rows/pallas_call | solution.py:120
  37.2 95.7 %softmax_step.1 = (bf16[16,1280,128]{2,1,0:T(8,128)(2,1)}, f32[16,8,512]{2,1,0:T(8,128)}, f32[16,32,128]{2,1,0:T(8,128)}, f32[16,8,512]{2,1,0:T(8,128)}, f32[16,32,128]{2,1,0:T(8,128)}, /*index=5*/f32[16,8,128]{2,1,0:T(8,128)}) custom-call(bf16[16,1280,128]{2,1,0:T(8,128)(2,1)} %bitcast.11, bf16[256,128]{1,0:T(8,128)(2,1)} %refs_1_.3, ...), custom_call_target="tpu_custom_call" | custom-call | tf_op jit(solution)/shard_map/softmax_step/pallas_call | solution.py:408
  132.9 22.2 %scatter_rows.1 = (f32[32768,128]{1,0:T(8,128)}, f32[16,8,512]{2,1,0:T(8,128)}, f32[16,32,128]{2,1,0:T(8,128)}, f32[16,8,512]{2,1,0:T(8,128)}, f32[16,32,128]{2,1,0:T(8,128)}, /*index=5*/f32[16,8,128]{2,1,0:T(8,128)}) custom-call(s32[2]{0:T(128)} %get-tuple-element.24.cnt_ref, s32[160,128]{1,0:T(8,128)} %get-tuple-element.25.list_ref, ...), custom_call_target="tpu_custom_call" | custom-call | tf_op jit(solution)/shard_map/scatter_rows/pallas_call | solution.py:212
  155.1 1.2 slice.3

commit v4 on v3

--- a/solution.py
+++ b/solution.py
@@ -54,7 +54,7 @@
     return jnp.where(flat < total, val, nr * LANES * 32768), own, total
 
 
-def gather_kernel(chunks, cand_ref, targ_ref, table_ref, out_ref, list_ref, cnt_ref, ids_ref, stage, tab, dense, plist, sem, psem):
+def gather_kernel(chunks, cand_ref, targ_ref, table_ref, out_ref, list_ref, cnt_ref, ids_ref, stage, tab, dense, plist, packed_rows, sem, psem, osem):
     rows = tab.shape[0]
     npos = out_ref.shape[0]
     cr = rows // chunks
@@ -104,12 +104,17 @@
 
     lax.fori_loop(0, (total + LANES - 1) // LANES, pick, 0)
 
-    def pack(i, _):
-        s = pl.ds(pl.multiple_of(i * BLK, BLK), BLK)
-        out_ref[s, :] = dense[s, :].astype(BF)
-        return 0
-
-    lax.fori_loop(0, npos // BLK, pack, 0)
+    part = npos // parts
+
+    def leave(d):
+        s = pl.ds(d * part, part)
+        return pltpu.make_async_copy(packed_rows.at[s, :], out_ref.at[s, :], osem.at[d])
+
+    for d in range(parts):
+        packed_rows[pl.ds(d * part, part), :] = dense[pl.ds(d * part, part), :].astype(BF)
+        leave(d).start()
+    for d in range(parts):
+        leave(d).wait()
 
 
 def gather(table, cand, targ):
@@ -121,8 +126,8 @@
         functools.partial(gather_kernel, chunks),
         out_shape=(jax.ShapeDtypeStruct((npos, LANES), BF), jax.ShapeDtypeStruct((nr, LANES), I32), jax.ShapeDtypeStruct((2,), I32)),
         in_specs=[VM, VM, HB],
-        out_specs=(VM, VM, SM),
-        scratch_shapes=[pltpu.VMEM((nr, LANES), I32), pltpu.VMEM((rows, LANES), BF), pltpu.VMEM((rows, LANES), F32), pltpu.VMEM((npos + 8, LANES), F32), pltpu.SMEM((nr, LANES), I32), pltpu.SemaphoreType.DMA((chunks,)), pltpu.SemaphoreType.DMA],
+        out_specs=(HB, VM, SM),
+        scratch_shapes=[pltpu.VMEM((nr, LANES), I32), pltpu.VMEM((rows, LANES), BF), pltpu.VMEM((rows, LANES), F32), pltpu.VMEM((npos + 8, LANES), F32), pltpu.SMEM((nr, LANES), I32), pltpu.VMEM((npos, LANES), BF), pltpu.SemaphoreType.DMA((chunks,)), pltpu.SemaphoreType.DMA, pltpu.SemaphoreType.DMA((targ.shape[0],))],
         compiler_params=pltpu.CompilerParams(vmem_limit_bytes=VMEM_CAP),
         name="gather_rows",
     )(cand, targ, table)
@@ -132,8 +137,22 @@
 
 
 def scatter_kernel(chunks, cnt_ref, list_ref, grad_ref, *refs):
-    n = (len(refs) - 6) // 2
-    passed, (out_ref, *kept, acc, grad, plist, sem, psem) = refs[:n], refs[n:]
+    n = (len(refs) - 10) // 3
+    passed, (out_ref, *refs) = refs[:n], refs[n:]
+    kept, held, (acc, raw, grad, plist, sem, psem, gsem, isem, osem) = refs[:n], refs[n:2 * n], refs[2 * n:]
+    parts = gsem.shape[0]
+    part = grad_ref.shape[0] // parts
+
+    def arrive(d):
+        s = pl.ds(d * part, part)
+        return pltpu.make_async_copy(grad_ref.at[s, :], raw.at[s, :], gsem.at[d])
+
+    for d in range(parts):
+        arrive(d).start()
+    ins = [pltpu.make_async_copy(src, dst, isem.at[i]) for i, (src, dst) in enumerate(zip(passed, held))]
+    outs = [pltpu.make_async_copy(src, dst, osem.at[i]) for i, (src, dst) in enumerate(zip(held, kept))]
+    for c in ins:
+        c.start()
     rows = out_ref.shape[0]
     npos = grad_ref.shape[0]
     to_smem = pltpu.make_async_copy(list_ref, plist, psem)
@@ -145,12 +164,13 @@
 
     lax.fori_loop(0, rows // BLK, zero, 0)
 
-    def conv(i, _):
-        s = pl.ds(pl.multiple_of(i * BLK, BLK), BLK)
-        grad[s, :] = grad_ref[s, :].astype(F32)
-        return 0
-
-    lax.fori_loop(0, npos // BLK, conv, 0)
+    for d in range(parts):
+        arrive(d).wait()
+        s = pl.ds(d * part, part)
+        grad[s, :] = raw[s, :].astype(F32)
+    for i, o in zip(ins, outs):
+        i.wait()
+        o.start()
     grad[npos:, :] = jnp.zeros((8, LANES), F32)
     to_smem.wait()
     nhead = cnt_ref[0]
@@ -199,22 +219,25 @@
 
     for c in range(chunks):
         store(c).start()
-    for src, dst in zip(passed, kept):
-        dst[...] = src[...]
     for c in range(chunks):
         store(c).wait()
-
-
-def scatter(grads, plist, counts, rows, passed):
+    for o in outs:
+        o.wait()
+
+
+def scatter(grads, plist, counts, rows, passed, parts):
     nr = plist.shape[0]
     npos = nr * LANES
     chunks = 8
+    n = len(passed)
+    dma = pltpu.SemaphoreType.DMA
     return pl.pallas_call(
         functools.partial(scatter_kernel, chunks),
         out_shape=(jax.ShapeDtypeStruct((rows, LANES), F32),) + tuple(jax.ShapeDtypeStruct(p.shape, p.dtype) for p in passed),
-        in_specs=[SM, HB, VM] + [VM] * len(passed),
-        out_specs=(HB,) + (VM,) * len(passed),
-        scratch_shapes=[pltpu.VMEM((rows, LANES), F32), pltpu.VMEM((npos + 8, LANES), F32), pltpu.SMEM((nr, LANES), I32), pltpu.SemaphoreType.DMA((chunks,)), pltpu.SemaphoreType.DMA],
+        in_specs=[SM, HB, HB] + [HB] * n,
+        out_specs=(HB,) * (n + 1),
+        scratch_shapes=[pltpu.VMEM(p.shape, p.dtype) for p in passed]
+        + [pltpu.VMEM((rows, LANES), F32), pltpu.VMEM((npos, LANES), BF), pltpu.VMEM((npos + 8, LANES), F32), pltpu.SMEM((nr, LANES), I32), dma((chunks,)), dma, dma((parts,)), dma((n,)), dma((n,))],
         compiler_params=pltpu.CompilerParams(vmem_limit_bytes=VMEM_CAP),
         name="scatter_rows",
     )(counts, plist, grads, *passed)
@@ -242,10 +265,8 @@
     return chip
 
 
-def enter(extra=()):
-    me, core, chip, sign = place()
+def enter(peers):
     barrier = pltpu.get_barrier_semaphore()
-    peers = [me + 1 - 2 * core] + [2 * chip_at(chip, sign, d) + core for d in CHIP_DIMS] + list(extra)
     for peer in peers:
         pl.semaphore_signal(barrier, inc=1, device_id=(peer,), device_id_type=MESHID)
     pl.semaphore_wait(barrier, len(peers))
@@ -280,7 +301,7 @@
     return out + [dma((n, 8)), dma((n, 8)), dma((num, 7)), dma((num, 7))]
 
 
-def reduce_scatter_steps(get, pieces, scratch):
+def reduce_scatter_steps(get, pieces, scratch, mine=None, produce=None):
     csend_s, crecv_s, send_s, recv_s = scratch[-4:]
     me, core, chip, sign = place()
     other = me + 1 - 2 * core
@@ -302,18 +323,26 @@
         c.start()
         started.append(c)
 
-    for s in CORE_ORDER:
-        for a in arrays:
-            go(core_copy(s, a))
-    yield
-    for s in CORE_ORDER:
+    def absorb(s):
         for a in arrays:
             core_copy(s, a).wait_recv()
-            acc[a][s] = get(2 * chip_at(chip, sign, s) + core, a)[...] + crecv[a][s]
+            part = mine(s, a) if mine else get(2 * chip_at(chip, sign, s) + core, a)[...]
+            acc[a][s] = part + crecv[a][s]
         for k in range(num):
             for i, (src, dst) in enumerate(stage_slots(pieces[k][3], 0)):
                 if src == s:
                     go(ici_copy(k, 0, i, s))
+
+    for n, s in enumerate(CORE_ORDER):
+        if produce:
+            produce(s)
+        for a in arrays:
+            go(core_copy(s, a))
+        if produce and n:
+            absorb(CORE_ORDER[n - 1])
+    yield
+    for s in CORE_ORDER[-1:] if produce else CORE_ORDER:
+        absorb(s)
     yield
     for t in range(3):
         for i in reversed(range(4 >> t)):
@@ -336,7 +365,7 @@
     return [pltpu.SemaphoreType.DMA((num, 8))] * 4
 
 
-def all_gather_steps(own, out, pieces, scratch):
+def all_gather_steps(own, out, pieces, scratch, landed=None):
     csend_s, crecv_s, send_s, recv_s = scratch
     me, core, chip, sign = place()
     other = me + 1 - 2 * core
@@ -367,6 +396,8 @@
         there = ref(k, s, core)
         remote(there, there, send_s.at[k, s], recv_s.at[k, s], other).wait_recv()
         core_send(k, s)
+        if landed:
+            landed(k, s, 0)
 
     plan = (((), (0, 0)), ((), (1, 0)), ((1,), (1, 1)), ((), (2, 0)), ((), (2, 1)), ((2,), (2, 2)), ((3,), (2, 3)), ((4, 5, 6, 7), None))
     for i, (waits, sends) in enumerate(plan):
@@ -388,7 +419,59 @@
         for s in SLOTS:
             there = ref(k, s, 1 - core)
             remote(there, there, csend_s.at[k, s], crecv_s.at[k, s], other).wait_recv()
+            if landed:
+                landed(k, s, 1)
     for c in started:
+        c.wait_send()
+
+
+def direct_scratch(rows, width):
+    dma = pltpu.SemaphoreType.DMA
+    return [pltpu.VMEM((8, rows, width), F32)] * 3 + [pltpu.VMEM((rows, width), F32), dma, dma, dma((8,)), dma((8,)), dma((8,)), dma((8,)), dma((8,)), dma((8,))]
+
+
+def sum_direct_steps(src, out, scratch):
+    crecv, acc, recv, tot, cs, cr, s1, r1, s2, r2, s3, r3 = scratch
+    me, core, chip, sign = place()
+    other = me + 1 - 2 * core
+    first = remote(src.at[1 - core], crecv, cs, cr, other)
+    first.start()
+    yield
+    first.wait_recv()
+    acc[...] = src[core] + crecv[...]
+    far = (7, 3, 5, 6, 1, 2, 4)
+
+    def to(s):
+        return 2 * chip_at(chip, sign, s) + core
+
+    sends = [remote(acc.at[chip_at(chip, sign, s)], recv.at[s], s1.at[s], r1.at[s], to(s)) for s in far]
+    for c in sends:
+        c.start()
+    yield
+    for c in sends:
+        c.wait_recv()
+    total = acc[chip]
+    for s in far:
+        total = total + recv[s]
+    tot[...] = total
+    backs = [remote(tot, out.at[me], s2.at[s], r2.at[s], to(s)) for s in far]
+    for c in backs:
+        c.start()
+    pair = [remote(tot, out.at[me], s3.at[0], r3.at[0], other)]
+    pair[0].start()
+    out[me] = total
+    yield
+    for s in reversed(far):
+        there = out.at[to(s)]
+        remote(there, there, s2.at[s], r2.at[s], other).wait_recv()
+        c = remote(there, there, s3.at[s], r3.at[s], other)
+        c.start()
+        pair.append(c)
+    yield
+    for s in SLOTS:
+        there = out.at[2 * chip_at(chip, sign, s) + 1 - core]
+        remote(there, there, s3.at[s], r3.at[s], other).wait_recv()
+    for c in [first] + sends + backs + pair:
         c.wait_send()
 
 
@@ -398,7 +481,7 @@
         live = [g for g in live if next(g, StopIteration) is not StopIteration]
 
 
-def kernel_call(body, name, cid, out_shape, scratch, *args):
+def kernel_call(body, name, cid, out_shape, scratch, *args, in_hbm=(), out_hbm=()):
     names = tuple(n for n, _ in scratch)
 
     def kernel(*refs):
@@ -408,8 +491,8 @@
     return pl.pallas_call(
         kernel,
         out_shape=out_shape,
-        in_specs=[VM] * len(args),
-        out_specs=jax.tree.map(lambda _: VM, out_shape),
+        in_specs=[HB if i in in_hbm else VM for i in range(len(args))],
+        out_specs=tuple(HB if i in out_hbm else VM for i in range(len(out_shape))),
         scratch_shapes=[s for _, s in scratch],
         compiler_params=pltpu.CompilerParams(collective_id=cid, has_side_effects=True, vmem_limit_bytes=VMEM_CAP),
         name=name,
@@ -466,28 +549,48 @@
     row_blocks(rows, blk)
 
 
-def start_kernel(tok_ref, w1, w2, targ_ref, targ_out, q_out, v):
-    enter()
-    me = lax.axis_index("dp")
+def start_kernel(targ_ref, targ_out, v):
+    me, core, chip, sign = place()
+    peers = [2 * chip_at(chip, sign, s) + c for s in reversed(SLOTS) for c in ((core, 1 - core) if s else (1 - core,))]
+    enter(peers)
+    send_s, recv_s = v["sems.0"], v["sems.1"]
     targ_out[me] = targ_ref[...]
-    sub = targ_ref.shape[0]
-    n_tok = tok_ref.shape[0]
-    ag_t = all_gather_steps(lambda a: targ_ref, lambda dev, a: targ_out.at[dev], [(0, 0, sub, 0)], group(v, "agt"))
-    next(ag_t)
-    next(ag_t)
-    tower_into(n_tok, lambda s: tok_ref[s, :], w1, w2, v["slope"], v["hid"], v["vec"])
-    q_out[me] = v["vec"][...]
-    ag_q = all_gather_steps(lambda a: v["vec"], lambda dev, a: q_out.at[dev], thirds(n_tok, 16), group(v, "agq"))
-    drain(ag_t, ag_q)
-
-
-def start(tokens, w_one, w_two, targ, parts, cid):
-    n_tok = tokens.shape[0]
-    ff = w_one.shape[1]
-    scratch = grouped("agt", ag_scratch(1)) + grouped("agq", ag_scratch(3))
-    scratch += [("slope", pltpu.VMEM((n_tok, ff), F32)), ("hid", pltpu.VMEM((n_tok, ff), BF)), ("vec", pltpu.VMEM((n_tok, LANES), BF))]
-    outs = (jax.ShapeDtypeStruct((parts,) + targ.shape, I32), jax.ShapeDtypeStruct((parts, n_tok, LANES), BF))
-    return kernel_call(start_kernel, "start_step", cid, outs, scratch, tokens, w_one, w_two, targ)
+    copies = [remote(targ_ref, targ_out.at[me], send_s.at[i], recv_s.at[i], peer) for i, peer in enumerate(peers)]
+    for c in copies:
+        c.start()
+    for c in copies:
+        c.wait()
+
+
+def start(targ, parts, cid):
+    dma = pltpu.SemaphoreType.DMA
+    outs = (jax.ShapeDtypeStruct((parts,) + targ.shape, I32),)
+    return kernel_call(start_kernel, "start_step", cid, outs, grouped("sems", [dma((parts - 1,)), dma((parts - 1,))]), targ)[0]
+
+
+def packed_grads(row_t, grad_t, pre_ref, hid_ref, loss, sums_ref):
+    d_in = dot_nn(row_t, pre_ref[...])
+    d_out = dot_nn(grad_t, hid_ref[...]).T
+    parts = 2 * sums_ref.shape[1]
+    n_in, n_out = d_in.shape[0] // parts, d_out.shape[0] // parts
+    wide = d_in.shape[1] // LANES
+    for dev in range(parts):
+        part = sums_ref.at[dev % 2, dev // 2]
+        for c in range(wide):
+            part[c * n_in:(c + 1) * n_in, :] = d_in[dev * n_in:(dev + 1) * n_in, c * LANES:(c + 1) * LANES]
+        part[wide * n_in:wide * n_in + n_out, :] = d_out[dev * n_out:(dev + 1) * n_out, :]
+        part[wide * n_in + n_out:, :] = jnp.broadcast_to(loss if dev == 0 else 0.0 * loss, (8, LANES))
+
+
+def unpack_grads(sums_ref, in_ref, out_ref, loss_ref):
+    parts, n_in, width = in_ref.shape
+    n_out = out_ref.shape[1]
+    wide = width // LANES
+    for dev in range(parts):
+        for c in range(wide):
+            in_ref[dev, :, c * LANES:(c + 1) * LANES] = sums_ref[dev, c * n_in:(c + 1) * n_in, :]
+        out_ref[dev] = sums_ref[dev, wide * n_in:wide * n_in + n_out, :]
+    loss_ref[...] = sums_ref[0, wide * n_in + n_out:, :]
 
 
 def weight_grads(row_t, grad_t, pre_ref, hid_ref, in_ref, out_ref):
@@ -500,7 +603,7 @@
         out_ref[dev] = d_out[dev * n_out:(dev + 1) * n_out, :]
 
 
-def step_kernel(x_ref, tok_ref, w1, w2, wi1, wi2, q_all, cand_ref, logq_ref, targ_ref, rows_out, di_in_out, di_out_out, dq_in_out, dq_out_out, loss_out, v):
+def step_kernel(x_ref, tok_ref, w1, w2, wi1, wi2, cand_ref, logq_ref, targ_ref, rows_out, di_in_out, di_out_out, dq_in_out, dq_out_out, loss_out, v):
     parts, n_item, _ = x_ref.shape
     n_tok = tok_ref.shape[0]
     n_cand = n_item - n_tok
@@ -510,18 +613,34 @@
     x_chip = 2 * chip_at(chip, sign, 1)
     diag = 2 * chip_at(chip, sign, 6) + core
     rounds = ((me + 1 - 2 * core, x_chip + core, x_chip + 1 - core), (2 * chip_at(chip, sign, 2) + core, 2 * chip_at(chip, sign, 4) + core, diag))
-    enter((x_chip + 1 - core, diag))
-    rs_rows = reduce_scatter_steps(lambda dev, a: x_ref.at[dev], thirds(n_item, 16), group(v, "rs"))
+    enter([me + 1 - 2 * core, x_chip + 1 - core] + [2 * chip_at(chip, sign, s) + core for s in SLOTS[1:]])
+    x_mine, x_sem = v["x_mine"], v["x_sem"]
+
+    def fetch(s):
+        return pltpu.make_async_copy(x_ref.at[2 * chip_at(chip, sign, s) + core], x_mine.at[s], x_sem.at[s])
+
+    def own_part(s, a):
+        fetch(s).wait()
+        return x_mine[s]
+
+    rs_rows = reduce_scatter_steps(lambda dev, a: x_ref.at[dev], thirds(n_item, 16), group(v, "rs"), mine=own_part)
     next(rs_rows)
+    for s in CORE_ORDER:
+        fetch(s).start()
     tower_into(n_tok, lambda s: tok_ref[s, :], w1, w2, v["q_slope"], v["q_hid"], v["q_vec"])
+    q_all = v["q_all"]
+    q_all[me] = v["q_vec"][...]
+    ag_q = all_gather_steps(lambda a: v["q_vec"], lambda dev, a: q_all.at[dev], thirds(n_tok, 16), group(v, "agq"))
+    next(ag_q)
     next(rs_rows)
+    next(ag_q)
     n_sub = n_cand // LANES
     for r in range(n_sub):
         s = pl.ds(r * LANES, LANES)
         row = pl.ds(me * n_sub + r, 1)
         v["lq"][s, :] = jnp.broadcast_to(logq_ref[row, :] * LOG2E, (LANES, LANES)).T
         v["ids"][s, :] = jnp.broadcast_to(cand_ref[row, :].astype(F32), (LANES, LANES)).T
-    drain(rs_rows)
+    drain(rs_rows, ag_q)
     raw = v["rs.1"].at[0]
     tower_into(n_item, lambda s: raw[s, :], wi1, wi2, v["i_slope"], v["i_hid"], v["i_vec"])
     vec = v["i_vec"]
@@ -595,8 +714,10 @@
         dh[t] = dot_nn(vec_t[...], dz_s[...])
         return 0
 
-    lax.fori_loop(0, parts, pass_two, 0)
-    rs_dh = reduce_scatter_steps(lambda dev, a: dh.at[dev], thirds(LANES, 8), group(v, "rsd"))
+    def both(s):
+        lax.fori_loop(0, 2, lambda c, _: pass_two(2 * chip_at(chip, sign, s) + c, 0), 0)
+
+    rs_dh = reduce_scatter_steps(lambda dev, a: dh.at[dev], thirds(LANES, 8), group(v, "rsd"), produce=both)
     next(rs_dh)
     grad[pl.ds(0, n_cand), :] = (d_acc[...] * scale).astype(BF)
     i_pre, i_slope = v["i_pre"], v["i_slope"]
@@ -606,15 +727,24 @@
 
     row_blocks(n_item, pre_grad)
     next(rs_dh)
-    mine = rows_out.at[me]
+    rows_v, row_sem = v["rows"], v["row_sem"]
+    mine = rows_v.at[me]
+    row_cuts = thirds(n_item, 16)
+
+    def leave(k, s, other):
+        dev = 2 * chip_at(chip, sign, s) + (1 - core if other else core)
+        p = pl.ds(row_cuts[k][1], row_cuts[k][2])
+        return pltpu.make_async_copy(rows_v.at[dev, p, :], rows_out.at[dev, p, :], row_sem.at[k, s, other])
 
     def input_grad(s):
         mine[s, :] = dot_nt(i_pre[s, :], wi1[...]).astype(BF)
 
     row_blocks(n_item, input_grad)
     next(rs_dh)
-    ag_rows = all_gather_steps(lambda a: mine, lambda dev, a: rows_out.at[dev], thirds(n_item, 16), group(v, "agr"))
+    ag_rows = all_gather_steps(lambda a: mine, lambda dev, a: rows_v.at[dev], row_cuts, group(v, "agr"), landed=lambda k, s, o: leave(k, s, o).start())
     next(ag_rows)
+    for k in range(3):
+        leave(k, 0, 0).start()
     weight_grads(turn(raw[...]), turn(grad[...]), i_pre, v["i_hid"], v["di_in"], v["di_out"])
     next(rs_dh)
     next(ag_rows)
@@ -637,15 +767,17 @@
     d_query = ((dz_col * targ_vec.astype(F32) + v["rsd.1"][0].T) * scale).astype(BF)
     q_pre = v["q_pre"]
     q_pre[...] = (v["q_slope"][...] * dot_nt(d_query, w2[...])).astype(BF)
-    weight_grads(turn(tok_ref[...]), turn(d_query), q_pre, v["q_hid"], v["dq_in"], v["dq_out"])
-    loss_part = v["loss"]
-    loss_part[...] = jnp.zeros_like(loss_part)
-    loss_part[0] = jnp.broadcast_to(loss, loss_part.shape[1:])
-    ar_q = sum_all("aq", (v["dq_in"], v["dq_out"], loss_part), (1, 2, 0), (dq_in_out, dq_out_out, loss_out))
+    packed_grads(turn(tok_ref[...]), turn(d_query), q_pre, v["q_hid"], loss, v["q_part"])
+    ar_q = sum_direct_steps(v["q_part"], v["q_sum"], group(v, "aq"))
     drain(ar_q, ar_i, ag_rows, rs_dh)
-
-
-def step(x, tokens, weights, q_all, cand, logq, targ, cid):
+    unpack_grads(v["q_sum"], dq_in_out, dq_out_out, loss_out)
+    for k in range(3):
+        for s in SLOTS:
+            for other in range(2):
+                leave(k, s, other).wait()
+
+
+def step(x, tokens, weights, cand, logq, targ, cid):
     parts, n_item, _ = x.shape
     n_tok = tokens.shape[0]
     n_cand = n_item - n_tok
@@ -658,7 +790,10 @@
     spec += grouped("rsd", rs_scratch([(LANES, n_tok, F32)], 3))
     spec += grouped("agr", ag_scratch(3))
     spec += grouped("ai", rs_scratch(w_parts, 2) + ag_scratch(2))
-    spec += grouped("aq", rs_scratch(w_parts + [(8, LANES, F32)], 3) + ag_scratch(3))
+    q_rows = n_in * (ff // LANES) + n_out + 8
+    spec += grouped("aq", direct_scratch(q_rows, LANES))
+    spec += grouped("agq", ag_scratch(3))
+    spec += [("x_sem", dma((8,))), ("row_sem", dma((3, 8, 2)))]
 
     def add(name, shape, dtype=F32):
         spec.append((name, pltpu.VMEM(shape, dtype)))
@@ -668,10 +803,14 @@
         add(pre + "_hid", (n, ff), BF)
         add(pre + "_pre", (n, ff), BF)
         add(pre + "_vec", (n, LANES), BF)
-        add("d" + pre + "_in", (parts, n_in, ff))
-        add("d" + pre + "_out", (parts, n_out, LANES))
     add("i_grad", (n_item, LANES), BF)
-    add("loss", (parts, 8, LANES))
+    add("di_in", (parts, n_in, ff))
+    add("di_out", (parts, n_out, LANES))
+    add("q_part", (2, parts // 2, q_rows, LANES))
+    add("q_sum", (parts, q_rows, LANES))
+    add("x_mine", (8, n_item, LANES), BF)
+    add("rows", (parts, n_item, LANES), BF)
+    add("q_all", (parts, n_tok, LANES), BF)
     for name in ("lq", "ids", "d_acc"):
         add(name, (n_cand, LANES))
     add("z", (parts, n_cand, n_tok))
@@ -681,8 +820,8 @@
     add("dz", (n_cand, n_tok), BF)
     add("dh", (parts, LANES, n_tok))
     sums = (jax.ShapeDtypeStruct((parts, n_in, ff), F32), jax.ShapeDtypeStruct((parts, n_out, LANES), F32))
-    outs = (jax.ShapeDtypeStruct((parts, n_item, LANES), BF),) + sums + sums + (jax.ShapeDtypeStruct((parts, 8, LANES), F32),)
-    return kernel_call(step_kernel, "softmax_step", cid, outs, spec, x, tokens, *weights, q_all, cand, logq, targ)
+    outs = (jax.ShapeDtypeStruct((parts, n_item, LANES), BF),) + sums + sums + (jax.ShapeDtypeStruct((8, LANES), F32),)
+    return kernel_call(step_kernel, "softmax_step", cid, outs, spec, x, tokens, *weights, cand, logq, targ, in_hbm=(0,), out_hbm=(0,))
 
 
 def solution(mesh):
@@ -692,11 +831,11 @@
         rows_loc, dim = table_loc.shape
         n_item = cand_ids.shape[0] // num_dev + tokens.shape[0]
         cand = cand_ids.reshape(-1, LANES)
-        targ, q_all = start(tokens, w_one, w_two, targ_loc.reshape(-1, LANES), num_dev, 1)
+        targ = start(targ_loc.reshape(-1, LANES), num_dev, 1)
         owned, plist, counts = gather(table_loc, cand, targ)
-        back, *sums = step(owned.reshape(num_dev, n_item, dim), tokens, (w_one, w_two, wi_one, wi_two), q_all, cand, log_q.reshape(-1, LANES), targ, 2)
-        d_table, di_in, di_out, dq_in, dq_out, loss = scatter(back.reshape(-1, dim), plist, counts, rows_loc, sums)
+        back, *sums = step(owned.reshape(num_dev, n_item, dim), tokens, (w_one, w_two, wi_one, wi_two), cand, log_q.reshape(-1, LANES), targ, 2)
+        d_table, di_in, di_out, dq_in, dq_out, loss = scatter(back.reshape(-1, dim), plist, counts, rows_loc, sums, num_dev)
         shaped = [g.reshape(w.shape) for g, w in zip((dq_in, dq_out, di_in, di_out), (w_one, w_two, wi_one, wi_two))]
-        return (loss[0, 0, 0], d_table) + tuple(shaped)
+        return (loss[0, 0], d_table) + tuple(shaped)
 
     return jax.shard_map(local_step, mesh=mesh, in_specs=(P("dp", None), P(), P(), P(), P(), P("dp", None), P(), P(), P("dp")), out_specs=(P(), P("dp", None), P(), P(), P(), P()), check_vma=False)

time: 157 us -> 147 us (0.936)
  Pallas kernels: 154 us -> 144 us
    pallas_call x2, Pallas kernels: 116 us -> 109 us  [kernel_call(): pl.pallas_call(kernel, out_shape=out_shape, in_specs=[HB if i in in_hbm e...]
    pallas_call x1, Pallas kernels: 22.2 us -> 19.8 us  [scatter(): pl.pallas_call(functools.partial(scatter_kernel, chunks), out_shape=(jax....]
where the time goes in v4:
time: 147 us; the launch traced here: 146 us
  Pallas kernels  144 us (98%)
    pallas_call x2, Pallas kernels, kernel_call(): pl.pallas_call(kernel, out_shape=out_shape, in_specs=[HB if i in in_hbm e...  109 us
    pallas_call x1, Pallas kernels, scatter(): pl.pallas_call(functools.partial(scatter_kernel, chunks), out_shape=(jax....  19.8 us
    pallas_call x1, Pallas kernels, gather(): pl.pallas_call(functools.partial(gather_kernel, chunks), out_shape=(jax.S...  15.9 us

profile of v4, /device:TPU:0, one launch (start us, length us, event | category | flops | bytes accessed | tf_op | source)
XLA Modules:
  0.0 146.1 jit_solution(9031050227061111879)
XLA Ops:
  0.6 9.0 %start_step.1.targ_ref.refs_8_ = s32[16,2,128]{2,1,0:T(2,128)} custom-call(s32[2,128]{1,0:T(2,128)} %bitcast.15), custom_call_target="tpu_custom_call" | custom-call | tf_op jit(solution)/shard_map/start_step/pallas_call | solution.py:491
  9.6 15.9 %gather_rows.1 = (bf16[20480,128]{1,0:T(8,128)(2,1)}, s32[160,128]{1,0:T(8,128)}, s32[2]{0:T(128)}) custom-call(s32[128,128]{1,0:T(8,128)} %bitcast.12, s32[16,2,128]{2,1,0:T(2,128)} %start_step.1.targ_ref.refs_8_, bf16[32768,128]{1,0:T(8,128)(2,1)} %table_ref.1), custom_call_target="tpu_custom_call" | custom-call | tf_op jit(solution)/shard_map/gather_rows/pallas_call | solution.py:125
  25.5 99.7 %softmax_step.1 = (bf16[16,1280,128]{2,1,0:T(8,128)(2,1)}, f32[16,8,512]{2,1,0:T(8,128)}, f32[16,32,128]{2,1,0:T(8,128)}, f32[16,8,512]{2,1,0:T(8,128)}, f32[16,32,128]{2,1,0:T(8,128)}, /*index=5*/f32[8,128]{1,0:T(8,128)}) custom-call(bf16[16,1280,128]{2,1,0:T(8,128)(2,1)} %bitcast.11, bf16[256,128]{1,0:T(8,128)(2,1)} %refs_1_.1, bf16[128,512]{1,0:T(8,128)(2,1)} %refs_2_.1, ...), custom_call_target="tpu_custom_call" | custom-call | tf_op jit(solution)/shard_map/softmax_step/pallas_call | solution.py:491
  125.2 19.8 %scatter_rows.1 = (f32[32768,128]{1,0:T(8,128)}, f32[16,8,512]{2,1,0:T(8,128)}, f32[16,32,128]{2,1,0:T(8,128)}, f32[16,8,512]{2,1,0:T(8,128)}, f32[16,32,128]{2,1,0:T(8,128)}, /*index=5*/f32[8,128]{1,0:T(8,128)}) custom-call(s32[2]{0:T(128)} %get-tuple-element.21.cnt_ref, s32[160,128]{1,0:T(8,128)} %get-tuple-element.22.list_ref, ...), custom_call_target="tpu_custom_call" | custom-call | tf_op jit(solution)/shard_map/scatter_rows/pallas_call | solution.py:234
  144.9 1.2 slice.3

commit v5 on v4

--- a/solution.py
+++ b/solution.py
@@ -276,10 +276,10 @@
     return tuple(CHIP_DIMS[(k + i) % 3] for i in range(3))
 
 
-def thirds(rows, unit, a=0):
+def thirds(rows, unit, first=0):
     base = rows // unit
     cuts = [(base * i // 3) * unit for i in range(4)]
-    return [(a, cuts[i], cuts[i + 1] - cuts[i], i) for i in range(3)]
+    return [(0, first + cuts[i], cuts[i + 1] - cuts[i], i) for i in range(3)]
 
 
 def remote(src, dst, send, recv, peer):
@@ -399,7 +399,7 @@
         if landed:
             landed(k, s, 0)
 
-    plan = (((), (0, 0)), ((), (1, 0)), ((1,), (1, 1)), ((), (2, 0)), ((), (2, 1)), ((2,), (2, 2)), ((3,), (2, 3)), ((4, 5, 6, 7), None))
+    plan = (((), (0, 0)), ((), (1, 0)), ((), (2, 0)), ((1,), (1, 1)), ((), (2, 1)), ((2,), (2, 2)), ((3,), (2, 3)), ((4, 5, 6, 7), None))
     for i, (waits, sends) in enumerate(plan):
         for j in waits or (None,):
             for k in range(num):
@@ -630,19 +630,47 @@
     tower_into(n_tok, lambda s: tok_ref[s, :], w1, w2, v["q_slope"], v["q_hid"], v["q_vec"])
     q_all = v["q_all"]
     q_all[me] = v["q_vec"][...]
-    ag_q = all_gather_steps(lambda a: v["q_vec"], lambda dev, a: q_all.at[dev], thirds(n_tok, 16), group(v, "agq"))
-    next(ag_q)
+    q_send, q_recv, q_csend, q_crecv = group(v, "agq")
+    q_sent = []
+
+    def q_tile(s, c):
+        return q_all.at[2 * chip_at(chip, sign, s) + c]
+
+    def q_go(s, d):
+        src = v["q_vec"] if s == 0 else q_tile(s, core)
+        if d:
+            c = remote(src, q_tile(s, core), q_send.at[s ^ d], q_recv.at[s ^ d], 2 * chip_at(chip, sign, d) + core)
+        else:
+            c = remote(src, q_tile(s, core), q_csend.at[s], q_crecv.at[s], me + 1 - 2 * core)
+        c.start()
+        q_sent.append(c)
+
+    def q_have(s, onward):
+        remote(q_tile(s, core), q_tile(s, core), q_send.at[s], q_recv.at[s], me + 1 - 2 * core).wait_recv()
+        for d in onward:
+            q_go(s, d)
+        q_go(s, 0)
+
+    def q_other(s):
+        there = q_tile(s, 1 - core)
+        remote(there, there, q_csend.at[s], q_crecv.at[s], me + 1 - 2 * core).wait_recv()
+
+    for d in (1, 2, 4, 0):
+        q_go(0, d)
     next(rs_rows)
-    next(ag_q)
     n_sub = n_cand // LANES
     for r in range(n_sub):
         s = pl.ds(r * LANES, LANES)
         row = pl.ds(me * n_sub + r, 1)
         v["lq"][s, :] = jnp.broadcast_to(logq_ref[row, :] * LOG2E, (LANES, LANES)).T
         v["ids"][s, :] = jnp.broadcast_to(cand_ref[row, :].astype(F32), (LANES, LANES)).T
-    drain(rs_rows, ag_q)
+    drain(rs_rows)
     raw = v["rs.1"].at[0]
+    q_have(1, (2, 4))
+    q_have(2, (4,))
+    q_have(4, ())
     tower_into(n_item, lambda s: raw[s, :], wi1, wi2, v["i_slope"], v["i_hid"], v["i_vec"])
+    q_have(3, (4,))
     vec = v["i_vec"]
     z_ref, top_ref, den_ref, own_ref = v["z"], v["top"], v["den"], v["own"]
     own = pl.ds(me, 1)
@@ -653,7 +681,8 @@
     own_ref[...] = jnp.full(own_ref.shape, -jnp.inf, F32)
     own_ref[own, :] = z_own
 
-    def pass_one(t, _):
+    def pass_one(i, upper):
+        t = 2 * (chip + sign[1] * lax.rem(i // 2, 2) + 2 * sign[2] * (i // 4) + upper * 4 * sign[4]) + lax.rem(i, 2)
         q_t = q_all[t]
         targ = jnp.concatenate([targ_ref[t, pl.ds(i, 1), :] for i in range(n_tok // LANES)], axis=1).astype(F32)
         z_t = own_ref[pl.ds(t, 1), :]
@@ -673,9 +702,18 @@
             den8 = den8 + jnp.sum(e.reshape(COL_BLK // 8, 8, n_tok), axis=0)
         top_ref[pl.ds(t, 1), :] = top
         den_ref[pl.ds(t, 1), :] = jnp.sum(den8, axis=0, keepdims=True) + jnp.exp2(z_t - top)
-        return 0
-
-    lax.fori_loop(0, parts, pass_one, 0)
+        return upper
+
+    for s in (0, 1, 2, 3):
+        q_other(s)
+    lax.fori_loop(0, parts // 2, pass_one, 0)
+    for s in (5, 6, 7):
+        q_have(s, ())
+    for s in (4, 5, 6, 7):
+        q_other(s)
+    lax.fori_loop(0, parts // 2, pass_one, 1)
+    for c in q_sent:
+        c.wait_send()
     held, got, st_send, st_recv = group(v, "st")
     held[0, 0] = top_ref[...]
     held[0, 1] = den_ref[...]
@@ -700,54 +738,90 @@
     dz_col = jnp.sum(jnp.where(eye, dz_row, 0.0), axis=1, keepdims=True)
     grad = v["i_grad"]
     grad[pl.ds(n_cand, n_tok), :] = (scale * dz_col * q_own.astype(F32)).astype(BF)
+    i_pre, i_slope = v["i_pre"], v["i_slope"]
+    rows_v, row_sem = v["rows"], v["row_sem"]
+    mine = rows_v.at[me]
+
+    def item_back(first, rows):
+        for r in range(first, first + rows, ROW_BLK):
+            s = pl.ds(r, ROW_BLK)
+            i_pre[s, :] = (i_slope[s, :] * dot_nt(grad[s, :], wi2[...])).astype(BF)
+            mine[s, :] = dot_nt(i_pre[s, :], wi1[...]).astype(BF)
+
+    def send_back(n, first, rows):
+        cuts = thirds(rows, 16, first)
+
+        def leave(k, s, o):
+            dev = 2 * chip_at(chip, sign, s) + (1 - core if o else core)
+            p = pl.ds(cuts[k][1], cuts[k][2])
+            return pltpu.make_async_copy(rows_v.at[dev, p, :], rows_out.at[dev, p, :], row_sem.at[3 * n + k, s, o])
+
+        for k in range(3):
+            leave(k, 0, 0).start()
+        yield from all_gather_steps(lambda a: mine, lambda dev, a: rows_v.at[dev], cuts, group(v, f"agr{n}"), landed=lambda k, s, o: leave(k, s, o).start())
+        for k in range(3):
+            for s in SLOTS:
+                for o in range(2):
+                    leave(k, s, o).wait()
+
+    item_back(n_cand, n_tok)
+    back_t = send_back(0, n_cand, n_tok)
+    for _ in range(3):
+        next(back_t)
     vec_t = v["vec_t"]
     vec_t[...] = turn(vec[:n_cand, :])
     d_acc, dz_s, dh = v["d_acc"], v["dz"], v["dh"]
     d_acc[...] = jnp.zeros_like(d_acc)
-
-    def pass_two(t, _):
+    half = n_cand // 2
+
+    def pass_two(t, first):
         shift = norm[pl.ds(t, 1), :]
-        for j in range(n_cand // COL_BLK):
-            s = pl.ds(j * COL_BLK, COL_BLK)
-            dz_s[s, :] = jnp.exp2(z_ref[t, s, :] - shift).astype(BF)
-        d_acc[...] += dot_nn(dz_s[...], q_all[t])
-        dh[t] = dot_nn(vec_t[...], dz_s[...])
+        for j in range(half // COL_BLK):
+            dz_s[pl.ds(j * COL_BLK, COL_BLK), :] = jnp.exp2(z_ref[t, pl.ds(first + j * COL_BLK, COL_BLK), :] - shift).astype(BF)
+        d_acc[pl.ds(first, half), :] += dot_nn(dz_s[...], q_all[t])
+        part = dot_nn(vec_t[:, first:first + half], dz_s[...])
+        dh[t] = part if first == 0 else dh[t] + part
+
+    def upper_half(t, _):
+        pass_two(t, 0)
         return 0
 
+    def cand_back(first):
+        grad[pl.ds(first, half), :] = (d_acc[pl.ds(first, half), :] * scale).astype(BF)
+        item_back(first, half)
+
+    lax.fori_loop(0, parts // 2, upper_half, 0)
+    next(back_t)
+    next(back_t)
+    lax.fori_loop(parts // 2, parts, upper_half, 0)
+    next(back_t)
+    cand_back(0)
+    next(back_t)
+    back_a = send_back(1, 0, half)
+    for _ in range(3):
+        next(back_a)
+
     def both(s):
-        lax.fori_loop(0, 2, lambda c, _: pass_two(2 * chip_at(chip, sign, s) + c, 0), 0)
+        def one(c, _):
+            pass_two(2 * chip_at(chip, sign, s) + c, half)
+            return 0
+
+        lax.fori_loop(0, 2, one, 0)
 
     rs_dh = reduce_scatter_steps(lambda dev, a: dh.at[dev], thirds(LANES, 8), group(v, "rsd"), produce=both)
     next(rs_dh)
-    grad[pl.ds(0, n_cand), :] = (d_acc[...] * scale).astype(BF)
-    i_pre, i_slope = v["i_pre"], v["i_slope"]
-
-    def pre_grad(s):
-        i_pre[s, :] = (i_slope[s, :] * dot_nt(grad[s, :], wi2[...])).astype(BF)
-
-    row_blocks(n_item, pre_grad)
+    next(back_a)
     next(rs_dh)
-    rows_v, row_sem = v["rows"], v["row_sem"]
-    mine = rows_v.at[me]
-    row_cuts = thirds(n_item, 16)
-
-    def leave(k, s, other):
-        dev = 2 * chip_at(chip, sign, s) + (1 - core if other else core)
-        p = pl.ds(row_cuts[k][1], row_cuts[k][2])
-        return pltpu.make_async_copy(rows_v.at[dev, p, :], rows_out.at[dev, p, :], row_sem.at[k, s, other])
-
-    def input_grad(s):
-        mine[s, :] = dot_nt(i_pre[s, :], wi1[...]).astype(BF)
-
-    row_blocks(n_item, input_grad)
+    cand_back(half)
     next(rs_dh)
-    ag_rows = all_gather_steps(lambda a: mine, lambda dev, a: rows_v.at[dev], row_cuts, group(v, "agr"), landed=lambda k, s, o: leave(k, s, o).start())
-    next(ag_rows)
-    for k in range(3):
-        leave(k, 0, 0).start()
+    next(back_a)
+    next(back_t)
+    back_b = send_back(2, half, half)
+    next(back_b)
     weight_grads(turn(raw[...]), turn(grad[...]), i_pre, v["i_hid"], v["di_in"], v["di_out"])
     next(rs_dh)
-    next(ag_rows)
+    next(back_a)
+    next(back_b)
 
     def sum_all(name, parts_in, orders, outs):
         pieces = [(a, 0, r.shape[1], o) for a, (r, o) in enumerate(zip(parts_in, orders))]
@@ -769,12 +843,8 @@
     q_pre[...] = (v["q_slope"][...] * dot_nt(d_query, w2[...])).astype(BF)
     packed_grads(turn(tok_ref[...]), turn(d_query), q_pre, v["q_hid"], loss, v["q_part"])
     ar_q = sum_direct_steps(v["q_part"], v["q_sum"], group(v, "aq"))
-    drain(ar_q, ar_i, ag_rows, rs_dh)
+    drain(ar_q, ar_i, back_a, back_b, back_t, rs_dh)
     unpack_grads(v["q_sum"], dq_in_out, dq_out_out, loss_out)
-    for k in range(3):
-        for s in SLOTS:
-            for other in range(2):
-                leave(k, s, other).wait()
 
 
 def step(x, tokens, weights, cand, logq, targ, cid):
@@ -788,12 +858,13 @@
     spec = grouped("rs", rs_scratch([(n_item, LANES, BF)], 3))
     spec += grouped("st", [pltpu.VMEM((3, 2, parts, n_tok), F32), pltpu.VMEM((2, 3, 2, parts, n_tok), F32), dma((2, 3)), dma((2, 3))])
     spec += grouped("rsd", rs_scratch([(LANES, n_tok, F32)], 3))
-    spec += grouped("agr", ag_scratch(3))
+    for n in range(3):
+        spec += grouped(f"agr{n}", ag_scratch(3))
     spec += grouped("ai", rs_scratch(w_parts, 2) + ag_scratch(2))
     q_rows = n_in * (ff // LANES) + n_out + 8
     spec += grouped("aq", direct_scratch(q_rows, LANES))
-    spec += grouped("agq", ag_scratch(3))
-    spec += [("x_sem", dma((8,))), ("row_sem", dma((3, 8, 2)))]
+    spec += grouped("agq", [dma((8,))] * 4)
+    spec += [("x_sem", dma((8,))), ("row_sem", dma((9, 8, 2)))]
 
     def add(name, shape, dtype=F32):
         spec.append((name, pltpu.VMEM(shape, dtype)))
@@ -817,7 +888,7 @@
     for name in ("top", "den", "norm", "own"):
         add(name, (parts, n_tok))
     add("vec_t", (LANES, n_cand), BF)
-    add("dz", (n_cand, n_tok), BF)
+    add("dz", (n_cand // 2, n_tok), BF)
     add("dh", (parts, LANES, n_tok))
     sums = (jax.ShapeDtypeStruct((parts, n_in, ff), F32), jax.ShapeDtypeStruct((parts, n_out, LANES), F32))
     outs = (jax.ShapeDtypeStruct((parts, n_item, LANES), BF),) + sums + sums + (jax.ShapeDtypeStruct((8, LANES), F32),)

time: 147 us -> 147 us (level)
  no operation moved by 1% of the time
where the time goes in v5:
time: 147 us
  Pallas kernels  145 us (99%)
    pallas_call x2, Pallas kernels, kernel_call(): pl.pallas_call(kernel, out_shape=out_shape, in_specs=[HB if i in in_hbm e...  109 us
    pallas_call x1, Pallas kernels, scatter(): pl.pallas_call(functools.partial(scatter_kernel, chunks), out_shape=(jax....  20.2 us
    pallas_call x1, Pallas kernels, gather(): pl.pallas_call(functools.partial(gather_kernel, chunks), out_shape=(jax.S...  16.1 us

profile of v5, /device:TPU:0, one launch (start us, length us, event | category | flops | bytes accessed | tf_op | source)
XLA Modules:
  0.0 147.3 jit_solution(12814711654093446465)
XLA Ops:
  0.6 9.0 %start_step.1.targ_ref.refs_8_ = s32[16,2,128]{2,1,0:T(2,128)} custom-call(s32[2,128]{1,0:T(2,128)} %bitcast.15), custom_call_target="tpu_custom_call" | custom-call | tf_op jit(solution)/shard_map/start_step/pallas_call | solution.py:491
  9.6 16.1 %gather_rows.1 = (bf16[20480,128]{1,0:T(8,128)(2,1)}, s32[160,128]{1,0:T(8,128)}, s32[2]{0:T(128)}) custom-call(s32[128,128]{1,0:T(8,128)} %bitcast.12, s32[16,2,128]{2,1,0:T(2,128)} %start_step.1.targ_ref.refs_8_, bf16[32768,128]{1,0:T(8,128)(2,1)} %table_ref.1), custom_call_target="tpu_custom_call" | custom-call | tf_op jit(solution)/shard_map/gather_rows/pallas_call | solution.py:125
  25.7 100.3 %softmax_step.1 = (bf16[16,1280,128]{2,1,0:T(8,128)(2,1)}, f32[16,8,512]{2,1,0:T(8,128)}, f32[16,32,128]{2,1,0:T(8,128)}, f32[16,8,512]{2,1,0:T(8,128)}, f32[16,32,128]{2,1,0:T(8,128)}, /*index=5*/f32[8,128]{1,0:T(8,128)}) custom-call(bf16[16,1280,128]{2,1,0:T(8,128)(2,1)} %bitcast.11, bf16[256,128]{1,0:T(8,128)(2,1)} %refs_1_.1, bf16[128,512]{1,0:T(8,128)(2,1)} %refs_2_.1, ...), custom_call_target="tpu_custom_call" | custom-call | tf_op jit(solution)/shard_map/softmax_step/pallas_call | solution.py:491
  126.0 20.2 %scatter_rows.1 = (f32[32768,128]{1,0:T(8,128)}, f32[16,8,512]{2,1,0:T(8,128)}, f32[16,32,128]{2,1,0:T(8,128)}, f32[16,8,512]{2,1,0:T(8,128)}, f32[16,32,128]{2,1,0:T(8,128)}, /*index=5*/f32[8,128]{1,0:T(8,128)}) custom-call(s32[2]{0:T(128)} %get-tuple-element.21.cnt_ref, s32[160,128]{1,0:T(8,128)} %get-tuple-element.22.list_ref, ...), custom_call_target="tpu_custom_call" | custom-call | tf_op jit(solution)/shard_map/scatter_rows/pallas_call | solution.py:234
  146.1 1.2 slice.3

commit v6 on v5

--- a/solution.py
+++ b/solution.py
@@ -138,8 +138,8 @@
 
 def scatter_kernel(chunks, cnt_ref, list_ref, grad_ref, *refs):
     n = (len(refs) - 10) // 3
-    passed, (out_ref, *refs) = refs[:n], refs[n:]
-    kept, held, (acc, raw, grad, plist, sem, psem, gsem, isem, osem) = refs[:n], refs[n:2 * n], refs[2 * n:]
+    passed, (out_ref, loss_ref, *refs) = refs[:n], refs[n:]
+    kept, held, (acc, raw, grad, plist, sem, psem, gsem, isem, osem) = refs[:n - 1], refs[n - 1:2 * n - 1], refs[2 * n - 1:]
     parts = gsem.shape[0]
     part = grad_ref.shape[0] // parts
 
@@ -150,7 +150,7 @@
     for d in range(parts):
         arrive(d).start()
     ins = [pltpu.make_async_copy(src, dst, isem.at[i]) for i, (src, dst) in enumerate(zip(passed, held))]
-    outs = [pltpu.make_async_copy(src, dst, osem.at[i]) for i, (src, dst) in enumerate(zip(held, kept))]
+    outs = [pltpu.make_async_copy(src, dst, osem.at[i]) for i, (src, dst) in enumerate(zip(held[:-1], kept))]
     for c in ins:
         c.start()
     rows = out_ref.shape[0]
@@ -168,9 +168,11 @@
         arrive(d).wait()
         s = pl.ds(d * part, part)
         grad[s, :] = raw[s, :].astype(F32)
-    for i, o in zip(ins, outs):
+    for i in ins:
         i.wait()
+    for o in outs:
         o.start()
+    loss_ref[0] = jnp.sum(held[-1][0:1, 0:1])
     grad[npos:, :] = jnp.zeros((8, LANES), F32)
     to_smem.wait()
     nhead = cnt_ref[0]
@@ -233,9 +235,9 @@
     dma = pltpu.SemaphoreType.DMA
     return pl.pallas_call(
         functools.partial(scatter_kernel, chunks),
-        out_shape=(jax.ShapeDtypeStruct((rows, LANES), F32),) + tuple(jax.ShapeDtypeStruct(p.shape, p.dtype) for p in passed),
+        out_shape=(jax.ShapeDtypeStruct((rows, LANES), F32), jax.ShapeDtypeStruct((1,), F32)) + tuple(jax.ShapeDtypeStruct(p.shape, p.dtype) for p in passed[:-1]),
         in_specs=[SM, HB, HB] + [HB] * n,
-        out_specs=(HB,) * (n + 1),
+        out_specs=(HB, SM) + (HB,) * (n - 1),
         scratch_shapes=[pltpu.VMEM(p.shape, p.dtype) for p in passed]
         + [pltpu.VMEM((rows, LANES), F32), pltpu.VMEM((npos, LANES), BF), pltpu.VMEM((npos + 8, LANES), F32), pltpu.SMEM((nr, LANES), I32), dma((chunks,)), dma, dma((parts,)), dma((n,)), dma((n,))],
         compiler_params=pltpu.CompilerParams(vmem_limit_bytes=VMEM_CAP),
@@ -301,7 +303,7 @@
     return out + [dma((n, 8)), dma((n, 8)), dma((num, 7)), dma((num, 7))]
 
 
-def reduce_scatter_steps(get, pieces, scratch, mine=None, produce=None):
+def reduce_scatter_steps(get, pieces, scratch, mine=None, produce=None, fine=False):
     csend_s, crecv_s, send_s, recv_s = scratch[-4:]
     me, core, chip, sign = place()
     other = me + 1 - 2 * core
@@ -343,6 +345,8 @@
     yield
     for s in CORE_ORDER[-1:] if produce else CORE_ORDER:
         absorb(s)
+        if fine and s:
+            yield
     yield
     for t in range(3):
         for i in reversed(range(4 >> t)):
@@ -531,22 +535,17 @@
     return x.astype(F32).T.astype(BF)
 
 
-def row_blocks(rows, body):
+def tower_into(rows, load, w_in, w_out, slope_ref, hid_ref, out_ref, first=0):
     def blk(i, _):
-        body(pl.ds(pl.multiple_of(i * ROW_BLK, ROW_BLK), ROW_BLK))
-        return 0
-
-    lax.fori_loop(0, rows // ROW_BLK, blk, 0)
-
-
-def tower_into(rows, load, w_in, w_out, slope_ref, hid_ref, out_ref):
-    def blk(s):
-        act, slope = gelu_both(dot_nn(load(s), w_in[...]))
+        src = pl.ds(pl.multiple_of(i * ROW_BLK, ROW_BLK), ROW_BLK)
+        s = pl.ds(pl.multiple_of(first + i * ROW_BLK, ROW_BLK), ROW_BLK)
+        act, slope = gelu_both(dot_nn(load(src), w_in[...]))
         slope_ref[s, :] = slope
         hid_ref[s, :] = act.astype(BF)
         out_ref[s, :] = dot_nn(hid_ref[s, :], w_out[...]).astype(BF)
-
-    row_blocks(rows, blk)
+        return 0
+
+    lax.fori_loop(0, rows // ROW_BLK, blk, 0)
 
 
 def start_kernel(targ_ref, targ_out, v):
@@ -603,10 +602,18 @@
         out_ref[dev] = d_out[dev * n_out:(dev + 1) * n_out, :]
 
 
-def step_kernel(x_ref, tok_ref, w1, w2, wi1, wi2, cand_ref, logq_ref, targ_ref, rows_out, di_in_out, di_out_out, dq_in_out, dq_out_out, loss_out, v):
+def step_kernel(x_ref, *refs):
+    (rows_out, *outs), v = refs[8:-1], refs[-1]
+    ins = [pltpu.make_async_copy(src, v[f"in.{i}"], v["in_sem"].at[i]) for i, src in enumerate(refs[:8])]
+    for c in ins:
+        c.start()
+    tok_ref, w1, w2, wi1, wi2, cand_ref, logq_ref, targ_ref = group(v, "in")
+    di_in_out, di_out_out, dq_in_out, dq_out_out, loss_out = group(v, "out")
+    leaves = [pltpu.make_async_copy(v[f"out.{i}"], dst, v["out_sem"].at[i]) for i, dst in enumerate(outs)]
     parts, n_item, _ = x_ref.shape
     n_tok = tok_ref.shape[0]
     n_cand = n_item - n_tok
+    half = n_cand // 2
     total = float(n_tok * parts)
     scale = SCORE_GAIN / math.sqrt(LANES)
     me, core, chip, sign = place()
@@ -619,14 +626,28 @@
     def fetch(s):
         return pltpu.make_async_copy(x_ref.at[2 * chip_at(chip, sign, s) + core], x_mine.at[s], x_sem.at[s])
 
-    def own_part(s, a):
-        fetch(s).wait()
-        return x_mine[s]
-
-    rs_rows = reduce_scatter_steps(lambda dev, a: x_ref.at[dev], thirds(n_item, 16), group(v, "rs"), mine=own_part)
-    next(rs_rows)
+    fetched = set()
+
+    def own_part(first, rows):
+        def part(s, a):
+            if s not in fetched:
+                fetch(s).wait()
+                fetched.add(s)
+            return x_mine[s, pl.ds(first, rows), :]
+
+        return part
+
+    def row_sums(name, first, rows):
+        p = pl.ds(first, rows)
+        return reduce_scatter_steps(lambda dev, a: x_ref.at[dev, p, :], thirds(rows, 16), group(v, name), mine=own_part(first, rows), fine=True)
+
+    rs_a, rs_b = row_sums("rsa", 0, half), row_sums("rsb", half, n_item - half)
+    next(rs_a)
+    next(rs_b)
     for s in CORE_ORDER:
         fetch(s).start()
+    for c in ins[:3]:
+        c.wait()
     tower_into(n_tok, lambda s: tok_ref[s, :], w1, w2, v["q_slope"], v["q_hid"], v["q_vec"])
     q_all = v["q_all"]
     q_all[me] = v["q_vec"][...]
@@ -657,38 +678,48 @@
 
     for d in (1, 2, 4, 0):
         q_go(0, d)
-    next(rs_rows)
+    for _ in range(8):
+        next(rs_a)
+    q_have(1, (2, 4))
+    q_have(2, (4,))
+    q_have(4, ())
+    for c in ins[3:]:
+        c.wait()
     n_sub = n_cand // LANES
     for r in range(n_sub):
         s = pl.ds(r * LANES, LANES)
         row = pl.ds(me * n_sub + r, 1)
         v["lq"][s, :] = jnp.broadcast_to(logq_ref[row, :] * LOG2E, (LANES, LANES)).T
         v["ids"][s, :] = jnp.broadcast_to(cand_ref[row, :].astype(F32), (LANES, LANES)).T
-    drain(rs_rows)
-    raw = v["rs.1"].at[0]
-    q_have(1, (2, 4))
-    q_have(2, (4,))
-    q_have(4, ())
-    tower_into(n_item, lambda s: raw[s, :], wi1, wi2, v["i_slope"], v["i_hid"], v["i_vec"])
+    for _ in range(2):
+        next(rs_b)
+    next(rs_a)
+    for _ in range(6):
+        next(rs_b)
     q_have(3, (4,))
+    next(rs_a)
+    for s in (5, 6, 7):
+        q_have(s, ())
+    next(rs_b)
+    next(rs_a)
+    raw_a, raw_b = v["rsa.1"].at[0], v["rsb.1"].at[0]
+    tower_into(half, lambda s: raw_a[s, :], wi1, wi2, v["i_slope"], v["i_hid"], v["i_vec"])
+    for s in SLOTS:
+        q_other(s)
+    next(rs_b)
     vec = v["i_vec"]
     z_ref, top_ref, den_ref, own_ref = v["z"], v["top"], v["den"], v["own"]
-    own = pl.ds(me, 1)
-    targ_vec = vec[pl.ds(n_cand, n_tok), :]
-    q_own = v["q_vec"][...]
-    eye = lax.broadcasted_iota(I32, (n_tok, n_tok), 0) == lax.broadcasted_iota(I32, (n_tok, n_tok), 1)
-    z_own = jnp.sum(jnp.where(eye, dot_nt(targ_vec, q_own), 0.0), axis=0, keepdims=True) * (scale * LOG2E)
-    own_ref[...] = jnp.full(own_ref.shape, -jnp.inf, F32)
-    own_ref[own, :] = z_own
-
-    def pass_one(i, upper):
-        t = 2 * (chip + sign[1] * lax.rem(i // 2, 2) + 2 * sign[2] * (i // 4) + upper * 4 * sign[4]) + lax.rem(i, 2)
+    def pass_one(t, first):
         q_t = q_all[t]
+        row = pl.ds(t, 1)
         targ = jnp.concatenate([targ_ref[t, pl.ds(i, 1), :] for i in range(n_tok // LANES)], axis=1).astype(F32)
-        z_t = own_ref[pl.ds(t, 1), :]
-        top8 = jnp.broadcast_to(z_t, (8, n_tok))
-        for j in range(n_cand // COL_BLK):
-            s = pl.ds(j * COL_BLK, COL_BLK)
+        if first:
+            old_top, old_den, z_t = top_ref[row, :], den_ref[row, :], own_ref[row, :]
+            top8 = jnp.broadcast_to(jnp.maximum(old_top, z_t), (8, n_tok))
+        else:
+            top8 = jnp.full((8, n_tok), -jnp.inf, F32)
+        for j in range(half // COL_BLK):
+            s = pl.ds(first + j * COL_BLK, COL_BLK)
             lq = jnp.concatenate([v["lq"][s, :]] * (n_tok // LANES), axis=1)
             ids = jnp.concatenate([v["ids"][s, :]] * (n_tok // LANES), axis=1)
             z = dot_nt(vec[s, :], q_t) * (scale * LOG2E) - lq
@@ -697,21 +728,34 @@
             top8 = jnp.maximum(top8, jnp.max(z.reshape(COL_BLK // 8, 8, n_tok), axis=0))
         top = jnp.max(top8, axis=0, keepdims=True)
         den8 = jnp.zeros((8, n_tok), F32)
-        for j in range(n_cand // COL_BLK):
-            e = jnp.exp2(z_ref[t, pl.ds(j * COL_BLK, COL_BLK), :] - top)
+        for j in range(half // COL_BLK):
+            e = jnp.exp2(z_ref[t, pl.ds(first + j * COL_BLK, COL_BLK), :] - top)
             den8 = den8 + jnp.sum(e.reshape(COL_BLK // 8, 8, n_tok), axis=0)
-        top_ref[pl.ds(t, 1), :] = top
-        den_ref[pl.ds(t, 1), :] = jnp.sum(den8, axis=0, keepdims=True) + jnp.exp2(z_t - top)
-        return upper
-
-    for s in (0, 1, 2, 3):
-        q_other(s)
-    lax.fori_loop(0, parts // 2, pass_one, 0)
-    for s in (5, 6, 7):
-        q_have(s, ())
-    for s in (4, 5, 6, 7):
-        q_other(s)
-    lax.fori_loop(0, parts // 2, pass_one, 1)
+        den = jnp.sum(den8, axis=0, keepdims=True)
+        top_ref[row, :] = top
+        den_ref[row, :] = den + old_den * jnp.exp2(old_top - top) + jnp.exp2(z_t - top) if first else den
+
+    def lower(t, _):
+        pass_one(t, 0)
+        return 0
+
+    def higher(t, _):
+        pass_one(t, half)
+        return 0
+
+    lax.fori_loop(0, parts // 2, lower, 0)
+    next(rs_b)
+    lax.fori_loop(parts // 2, parts, lower, 0)
+    tower_into(n_item - half, lambda s: raw_b[s, :], wi1, wi2, v["i_slope"], v["i_hid"], v["i_vec"], half)
+    own = pl.ds(me, 1)
+    targ_vec = vec[pl.ds(n_cand, n_tok), :]
+    q_own = v["q_vec"][...]
+    eye = lax.broadcasted_iota(I32, (n_tok, n_tok), 0) == lax.broadcasted_iota(I32, (n_tok, n_tok), 1)
+    z_own = jnp.sum(jnp.where(eye, dot_nt(targ_vec, q_own), 0.0), axis=0, keepdims=True) * (scale * LOG2E)
+    own_ref[...] = jnp.full(own_ref.shape, -jnp.inf, F32)
+    own_ref[own, :] = z_own
+    lax.fori_loop(0, parts, higher, 0)
+    drain(rs_a, rs_b)
     for c in q_sent:
         c.wait_send()
     held, got, st_send, st_recv = group(v, "st")
@@ -772,8 +816,6 @@
     vec_t[...] = turn(vec[:n_cand, :])
     d_acc, dz_s, dh = v["d_acc"], v["dz"], v["dh"]
     d_acc[...] = jnp.zeros_like(d_acc)
-    half = n_cand // 2
-
     def pass_two(t, first):
         shift = norm[pl.ds(t, 1), :]
         for j in range(half // COL_BLK):
@@ -818,7 +860,7 @@
     next(back_t)
     back_b = send_back(2, half, half)
     next(back_b)
-    weight_grads(turn(raw[...]), turn(grad[...]), i_pre, v["i_hid"], v["di_in"], v["di_out"])
+    weight_grads(turn(jnp.concatenate([raw_a[...], raw_b[...]])), turn(grad[...]), i_pre, v["i_hid"], v["di_in"], v["di_out"])
     next(rs_dh)
     next(back_a)
     next(back_b)
@@ -844,7 +886,13 @@
     packed_grads(turn(tok_ref[...]), turn(d_query), q_pre, v["q_hid"], loss, v["q_part"])
     ar_q = sum_direct_steps(v["q_part"], v["q_sum"], group(v, "aq"))
     drain(ar_q, ar_i, back_a, back_b, back_t, rs_dh)
+    for c in leaves[:2]:
+        c.start()
     unpack_grads(v["q_sum"], dq_in_out, dq_out_out, loss_out)
+    for c in leaves[2:]:
+        c.start()
+    for c in leaves:
+        c.wait()
 
 
 def step(x, tokens, weights, cand, logq, targ, cid):
@@ -855,7 +903,8 @@
     dma = pltpu.SemaphoreType.DMA
     n_in, n_out = LANES // parts, ff // parts
     w_parts = [(n_in, ff, F32), (n_out, LANES, F32)]
-    spec = grouped("rs", rs_scratch([(n_item, LANES, BF)], 3))
+    half = n_cand // 2
+    spec = grouped("rsa", rs_scratch([(half, LANES, BF)], 3)) + grouped("rsb", rs_scratch([(n_item - half, LANES, BF)], 3))
     spec += grouped("st", [pltpu.VMEM((3, 2, parts, n_tok), F32), pltpu.VMEM((2, 3, 2, parts, n_tok), F32), dma((2, 3)), dma((2, 3))])
     spec += grouped("rsd", rs_scratch([(LANES, n_tok, F32)], 3))
     for n in range(3):
@@ -892,7 +941,10 @@
     add("dh", (parts, LANES, n_tok))
     sums = (jax.ShapeDtypeStruct((parts, n_in, ff), F32), jax.ShapeDtypeStruct((parts, n_out, LANES), F32))
     outs = (jax.ShapeDtypeStruct((parts, n_item, LANES), BF),) + sums + sums + (jax.ShapeDtypeStruct((8, LANES), F32),)
-    return kernel_call(step_kernel, "softmax_step", cid, outs, spec, x, tokens, *weights, cand, logq, targ, in_hbm=(0,), out_hbm=(0,))
+    args = (tokens, *weights, cand, logq, targ)
+    spec += grouped("in", [pltpu.VMEM(a.shape, a.dtype) for a in args]) + grouped("out", [pltpu.VMEM(o.shape, o.dtype) for o in outs[1:]])
+    spec += [("in_sem", dma((8,))), ("out_sem", dma((5,)))]
+    return kernel_call(step_kernel, "softmax_step", cid, outs, spec, x, *args, in_hbm=range(9), out_hbm=range(6))
 
 
 def solution(mesh):
@@ -905,8 +957,8 @@
         targ = start(targ_loc.reshape(-1, LANES), num_dev, 1)
         owned, plist, counts = gather(table_loc, cand, targ)
         back, *sums = step(owned.reshape(num_dev, n_item, dim), tokens, (w_one, w_two, wi_one, wi_two), cand, log_q.reshape(-1, LANES), targ, 2)
-        d_table, di_in, di_out, dq_in, dq_out, loss = scatter(back.reshape(-1, dim), plist, counts, rows_loc, sums, num_dev)
+        d_table, loss, di_in, di_out, dq_in, dq_out = scatter(back.reshape(-1, dim), plist, counts, rows_loc, sums, num_dev)
         shaped = [g.reshape(w.shape) for g, w in zip((dq_in, dq_out, di_in, di_out), (w_one, w_two, wi_one, wi_two))]
-        return (loss[0, 0], d_table) + tuple(shaped)
+        return (loss.reshape(()), d_table) + tuple(shaped)
 
     return jax.shard_map(local_step, mesh=mesh, in_specs=(P("dp", None), P(), P(), P(), P(), P("dp", None), P(), P(), P("dp")), out_specs=(P(), P("dp", None), P(), P(), P(), P()), check_vma=False)

time: 147 us -> 150 us (1.020)
  Pallas kernels: 145 us -> 149 us
    pallas_call x2, Pallas kernels: 109 us -> 113 us  [kernel_call(): pl.pallas_call(kernel, out_shape=out_shape, in_specs=[HB if i in in_hbm e...]
where the time goes in v6:
time: 150 us
  Pallas kernels  149 us (99%)
    pallas_call x2, Pallas kernels, kernel_call(): pl.pallas_call(kernel, out_shape=out_shape, in_specs=[HB if i in in_hbm e...  113 us
    pallas_call x1, Pallas kernels, scatter(): pl.pallas_call(functools.partial(scatter_kernel, chunks), out_shape=(jax....  20.5 us
    pallas_call x1, Pallas kernels, gather(): pl.pallas_call(functools.partial(gather_kernel, chunks), out_shape=(jax.S...  15.9 us

profile of v6, /device:TPU:0, one launch (start us, length us, event | category | flops | bytes accessed | tf_op | source)
XLA Modules:
  0.0 149.8 jit_solution(1193049466337036577)
XLA Ops:
  0.6 9.0 %start_step.1.targ_ref.refs_8_ = s32[16,2,128]{2,1,0:T(2,128)} custom-call(s32[2,128]{1,0:T(2,128)} %bitcast.15), custom_call_target="tpu_custom_call" | custom-call | tf_op jit(solution)/shard_map/start_step/pallas_call | solution.py:495
  9.6 15.9 %gather_rows.1 = (bf16[20480,128]{1,0:T(8,128)(2,1)}, s32[160,128]{1,0:T(8,128)}, s32[2]{0:T(128)}) custom-call(s32[128,128]{1,0:T(8,128)} %bitcast.12, s32[16,2,128]{2,1,0:T(2,128)} %start_step.1.targ_ref.refs_8_, bf16[32768,128]{1,0:T(8,128)(2,1)} %table_ref.1), custom_call_target="tpu_custom_call" | custom-call | tf_op jit(solution)/shard_map/gather_rows/pallas_call | solution.py:125
  25.5 103.7 %softmax_step.1 = (bf16[16,1280,128]{2,1,0:T(8,128)(2,1)}, f32[16,8,512]{2,1,0:T(8,128)}, f32[16,32,128]{2,1,0:T(8,128)}, f32[16,8,512]{2,1,0:T(8,128)}, f32[16,32,128]{2,1,0:T(8,128)}, /*index=5*/f32[8,128]{1,0:T(8,128)}) custom-call(bf16[16,1280,128]{2,1,0:T(8,128)(2,1)} %bitcast.11, bf16[256,128]{1,0:T(8,128)(2,1)} %refs_1_.1, bf16[128,512]{1,0:T(8,128)(2,1)} %refs_2_.1, ...), custom_call_target="tpu_custom_call" | custom-call | tf_op jit(solution)/shard_map/softmax_step/pallas_call | solution.py:495
  129.1 20.5 %scatter_rows.1 = (f32[32768,128]{1,0:T(8,128)}, f32[1]{0:T(128)}, f32[16,8,512]{2,1,0:T(8,128)}, f32[16,32,128]{2,1,0:T(8,128)}, f32[16,8,512]{2,1,0:T(8,128)}, /*index=5*/f32[16,32,128]{2,1,0:T(8,128)}) custom-call(s32[2]{0:T(128)} %get-tuple-element.21.cnt_ref, s32[160,128]{1,0:T(8,128)} %get-tuple-element.22.list_ref, bf16[20480,128]{1,0:T(8,128)(2,1)} %bitcast.10, ...), custom_call_target="tpu_custom_call" | custom-call | tf_op jit(solution)/shard_map/scatter_rows/pallas_call | solution.py:236

commit v7 on v5

--- a/solution.py
+++ b/solution.py
@@ -138,8 +138,8 @@
 
 def scatter_kernel(chunks, cnt_ref, list_ref, grad_ref, *refs):
     n = (len(refs) - 10) // 3
-    passed, (out_ref, *refs) = refs[:n], refs[n:]
-    kept, held, (acc, raw, grad, plist, sem, psem, gsem, isem, osem) = refs[:n], refs[n:2 * n], refs[2 * n:]
+    passed, (out_ref, loss_ref, *refs) = refs[:n], refs[n:]
+    kept, held, (acc, raw, grad, plist, sem, psem, gsem, isem, osem) = refs[:n - 1], refs[n - 1:2 * n - 1], refs[2 * n - 1:]
     parts = gsem.shape[0]
     part = grad_ref.shape[0] // parts
 
@@ -150,7 +150,7 @@
     for d in range(parts):
         arrive(d).start()
     ins = [pltpu.make_async_copy(src, dst, isem.at[i]) for i, (src, dst) in enumerate(zip(passed, held))]
-    outs = [pltpu.make_async_copy(src, dst, osem.at[i]) for i, (src, dst) in enumerate(zip(held, kept))]
+    outs = [pltpu.make_async_copy(src, dst, osem.at[i]) for i, (src, dst) in enumerate(zip(held[:-1], kept))]
     for c in ins:
         c.start()
     rows = out_ref.shape[0]
@@ -168,9 +168,11 @@
         arrive(d).wait()
         s = pl.ds(d * part, part)
         grad[s, :] = raw[s, :].astype(F32)
-    for i, o in zip(ins, outs):
+    for i in ins:
         i.wait()
+    for o in outs:
         o.start()
+    loss_ref[0] = jnp.sum(held[-1][0:1, 0:1])
     grad[npos:, :] = jnp.zeros((8, LANES), F32)
     to_smem.wait()
     nhead = cnt_ref[0]
@@ -233,9 +235,9 @@
     dma = pltpu.SemaphoreType.DMA
     return pl.pallas_call(
         functools.partial(scatter_kernel, chunks),
-        out_shape=(jax.ShapeDtypeStruct((rows, LANES), F32),) + tuple(jax.ShapeDtypeStruct(p.shape, p.dtype) for p in passed),
+        out_shape=(jax.ShapeDtypeStruct((rows, LANES), F32), jax.ShapeDtypeStruct((1,), F32)) + tuple(jax.ShapeDtypeStruct(p.shape, p.dtype) for p in passed[:-1]),
         in_specs=[SM, HB, HB] + [HB] * n,
-        out_specs=(HB,) * (n + 1),
+        out_specs=(HB, SM) + (HB,) * (n - 1),
         scratch_shapes=[pltpu.VMEM(p.shape, p.dtype) for p in passed]
         + [pltpu.VMEM((rows, LANES), F32), pltpu.VMEM((npos, LANES), BF), pltpu.VMEM((npos + 8, LANES), F32), pltpu.SMEM((nr, LANES), I32), dma((chunks,)), dma, dma((parts,)), dma((n,)), dma((n,))],
         compiler_params=pltpu.CompilerParams(vmem_limit_bytes=VMEM_CAP),
@@ -265,6 +267,11 @@
     return chip
 
 
+def locate():
+    me, core, chip, sign = place()
+    return me, core, 1 - core, chip, sign, lambda s, c: 2 * chip_at(chip, sign, s) + c
+
+
 def enter(peers):
     barrier = pltpu.get_barrier_semaphore()
     for peer in peers:
@@ -292,52 +299,40 @@
     return [(s, s ^ dims[t]) for s in live if s & dims[t]]
 
 
-def rs_scratch(arrays, num):
-    out = []
-    for rows, width, dtype in arrays:
-        out += [pltpu.VMEM((8, rows, width), dtype), pltpu.VMEM((8, rows, width), dtype), pltpu.VMEM((7, rows, width), dtype)]
-    n = len(arrays)
+def rs_scratch(rows, width, dtype):
     dma = pltpu.SemaphoreType.DMA
-    return out + [dma((n, 8)), dma((n, 8)), dma((num, 7)), dma((num, 7))]
+    return [pltpu.VMEM((8, rows, width), dtype), pltpu.VMEM((8, rows, width), dtype), pltpu.VMEM((7, rows, width), dtype), dma, dma((8,)), dma, dma((7,))]
 
 
 def reduce_scatter_steps(get, pieces, scratch, mine=None, produce=None):
-    csend_s, crecv_s, send_s, recv_s = scratch[-4:]
-    me, core, chip, sign = place()
-    other = me + 1 - 2 * core
-    num = len(pieces)
-    arrays = range((len(scratch) - 4) // 3)
-    crecv, acc, recv = ([scratch[3 * a + i] for a in arrays] for i in range(3))
-    started = []
-
-    def core_copy(s, a):
-        return remote(get(2 * chip_at(chip, sign, s) + 1 - core, a), crecv[a].at[s], csend_s.at[a, s], crecv_s.at[a, s], other)
-
-    def ici_copy(k, t, i, s):
-        a, off, ln, order = pieces[k]
+    crecv, acc, recv, csend_s, crecv_s, send_s, recv_s = scratch
+    me, core, away, chip, sign, at = locate()
+    other = at(0, away)
+
+    def core_copy(s):
+        return remote(get(at(s, away)), crecv.at[s], csend_s, crecv_s.at[s], other)
+
+    def send(k, t, i, s):
+        _, off, ln, order = pieces[k]
         slot = RS_BASE[t] + i
-        peer = 2 * chip_at(chip, sign, order_of(order)[t]) + core
-        return remote(acc[a].at[s, pl.ds(off, ln), :], recv[a].at[slot, pl.ds(off, ln), :], send_s.at[k, slot], recv_s.at[k, slot], peer)
-
-    def go(c):
-        c.start()
-        started.append(c)
+        peer = at(order_of(order)[t], core)
+        remote(acc.at[s, pl.ds(off, ln), :], recv.at[slot, pl.ds(off, ln), :], send_s, recv_s.at[slot], peer).start()
+
+    def forward(k, t, s):
+        for i, (src, _) in enumerate(stage_slots(pieces[k][3], t)):
+            if src == s:
+                send(k, t, i, s)
 
     def absorb(s):
-        for a in arrays:
-            core_copy(s, a).wait_recv()
-            part = mine(s, a) if mine else get(2 * chip_at(chip, sign, s) + core, a)[...]
-            acc[a][s] = part + crecv[a][s]
-        for k in range(num):
-            for i, (src, dst) in enumerate(stage_slots(pieces[k][3], 0)):
-                if src == s:
-                    go(ici_copy(k, 0, i, s))
+        core_copy(s).wait_recv()
+        acc[s] = (mine(s) if mine else get(at(s, core))[...]) + crecv[s]
+        for k in range(3):
+            forward(k, 0, s)
 
     for n, s in enumerate(CORE_ORDER):
         if produce:
             produce(s)
-        for a in arrays:
-            go(core_copy(s, a))
+        core_copy(s).start()
         if produce and n:
             absorb(CORE_ORDER[n - 1])
     yield
@@ -346,133 +341,115 @@
     yield
     for t in range(3):
         for i in reversed(range(4 >> t)):
-            for k in range(num):
-                a, off, ln, order = pieces[k]
-                src, dst = stage_slots(order, t)[i]
-                ici_copy(k, t, i, src).wait_recv()
+            slot = RS_BASE[t] + i
+            remote(recv.at[slot], recv.at[slot], send_s, recv_s.at[slot], other).wait_recv()
+            for k in range(3):
+                _, off, ln, order = pieces[k]
+                dst = stage_slots(order, t)[i][1]
                 p = pl.ds(off, ln)
-                acc[a][dst, p, :] = acc[a][dst, p, :] + recv[a][RS_BASE[t] + i, p, :]
+                acc[dst, p, :] = acc[dst, p, :] + recv[slot, p, :]
                 if t < 2:
-                    for i2, (src2, dst2) in enumerate(stage_slots(order, t + 1)):
-                        if src2 == dst:
-                            go(ici_copy(k, t + 1, i2, dst))
+                    forward(k, t + 1, dst)
         yield
-    for c in started:
-        c.wait_send()
-
-
-def ag_scratch(num):
-    return [pltpu.SemaphoreType.DMA((num, 8))] * 4
+    remote(crecv, crecv, csend_s, crecv_s.at[0], other).wait_send()
+    remote(recv, recv, send_s, recv_s.at[0], other).wait_send()
+
+
+def ag_scratch():
+    dma = pltpu.SemaphoreType.DMA
+    return [dma, dma, dma, dma((8,))]
 
 
 def all_gather_steps(own, out, pieces, scratch, landed=None):
     csend_s, crecv_s, send_s, recv_s = scratch
-    me, core, chip, sign = place()
-    other = me + 1 - 2 * core
-    num = len(pieces)
-    started = []
-
-    def ref(k, s, c):
-        a, off, ln, _ = pieces[k]
-        return out(2 * chip_at(chip, sign, s) + c, a).at[pl.ds(off, ln), :]
-
-    def source(k, s):
-        a, off, ln, _ = pieces[k]
-        return own(a).at[pl.ds(off, ln), :] if s == 0 else ref(k, s, core)
-
-    def go(c):
-        c.start()
-        started.append(c)
+    me, core, away, chip, sign, at = locate()
+    other = at(0, away)
+    begin = pieces[0][1]
+    whole = pl.ds(begin, sum(p[2] for p in pieces))
+
+    def device(s):
+        return at(s, core)
+
+    def slot(k, bits):
+        d = order_of(pieces[k][3])
+        return sum(d[b] for b in range(3) if bits >> b & 1)
+
+    def ends(k, s):
+        p = pl.ds(pieces[k][1], pieces[k][2])
+        there = out.at[device(s), p, :]
+        return (own.at[p, :] if s == 0 else there), there
 
     def core_send(k, s):
-        go(remote(source(k, s), ref(k, s, core), csend_s.at[k, s], crecv_s.at[k, s], other))
-
-    def send(k, t, s):
-        d = order_of(pieces[k][3])[t]
-        peer = 2 * chip_at(chip, sign, d) + core
-        go(remote(source(k, s), ref(k, s, core), send_s.at[k, s ^ d], recv_s.at[k, s ^ d], peer))
-
-    def arrive(k, s):
-        there = ref(k, s, core)
-        remote(there, there, send_s.at[k, s], recv_s.at[k, s], other).wait_recv()
-        core_send(k, s)
-        if landed:
-            landed(k, s, 0)
+        src, there = ends(k, s)
+        remote(src, there, csend_s, crecv_s, other).start()
+
+    def send(k, t, bits):
+        src, there = ends(k, slot(k, bits))
+        remote(src, there, send_s, recv_s.at[bits | 1 << t], at(order_of(pieces[k][3])[t], core)).start()
 
     plan = (((), (0, 0)), ((), (1, 0)), ((), (2, 0)), ((1,), (1, 1)), ((), (2, 1)), ((2,), (2, 2)), ((3,), (2, 3)), ((4, 5, 6, 7), None))
-    for i, (waits, sends) in enumerate(plan):
-        for j in waits or (None,):
-            for k in range(num):
-                d = order_of(pieces[k][3])
-
-                def slot(bits):
-                    return sum(d[b] for b in range(3) if bits >> b & 1)
-
-                if j is not None:
-                    arrive(k, slot(j))
-                if sends is not None:
-                    send(k, sends[0], slot(sends[1]))
-                if i == 0:
-                    core_send(k, 0)
+    for n, (waits, step) in enumerate(plan):
+        for bits in waits:
+            remote(out.at[me, whole, :], out.at[me, whole, :], send_s, recv_s.at[bits], other).wait_recv()
+            for k in range(len(pieces)):
+                core_send(k, slot(k, bits))
+                if landed:
+                    landed(device(slot(k, bits)), pieces[k][1], pieces[k][2])
+        for k in range(len(pieces)):
+            if step:
+                send(k, *step)
+            if n == 0:
+                core_send(k, 0)
         yield
-    for k in range(num):
+    half = out.at[pl.ds(0, 8), whole, :]
+    remote(half, half, csend_s, crecv_s, other).wait()
+    sent = out.at[pl.ds(0, 7), whole, :]
+    remote(sent, sent, send_s, recv_s.at[0], other).wait_send()
+    if landed:
         for s in SLOTS:
-            there = ref(k, s, 1 - core)
-            remote(there, there, csend_s.at[k, s], crecv_s.at[k, s], other).wait_recv()
-            if landed:
-                landed(k, s, 1)
-    for c in started:
-        c.wait_send()
+            landed(at(s, away), begin, whole.size)
 
 
 def direct_scratch(rows, width):
     dma = pltpu.SemaphoreType.DMA
-    return [pltpu.VMEM((8, rows, width), F32)] * 3 + [pltpu.VMEM((rows, width), F32), dma, dma, dma((8,)), dma((8,)), dma((8,)), dma((8,)), dma((8,)), dma((8,))]
+    return [pltpu.VMEM((8, rows, width), F32)] * 3 + [pltpu.VMEM((rows, width), F32)] + [dma] * 8
 
 
 def sum_direct_steps(src, out, scratch):
     crecv, acc, recv, tot, cs, cr, s1, r1, s2, r2, s3, r3 = scratch
-    me, core, chip, sign = place()
-    other = me + 1 - 2 * core
-    first = remote(src.at[1 - core], crecv, cs, cr, other)
+    me, core, away, chip, sign, at = locate()
+    other = at(0, away)
+    first = remote(src.at[away], crecv, cs, cr, other)
     first.start()
     yield
-    first.wait_recv()
+    first.wait()
     acc[...] = src[core] + crecv[...]
     far = (7, 3, 5, 6, 1, 2, 4)
 
     def to(s):
-        return 2 * chip_at(chip, sign, s) + core
-
-    sends = [remote(acc.at[chip_at(chip, sign, s)], recv.at[s], s1.at[s], r1.at[s], to(s)) for s in far]
-    for c in sends:
-        c.start()
+        return at(s, core)
+
+    for s in far:
+        remote(acc.at[chip_at(chip, sign, s)], recv.at[s], s1, r1, to(s)).start()
     yield
-    for c in sends:
-        c.wait_recv()
+    seven = recv.at[pl.ds(1, 7)]
+    remote(seven, seven, s1, r1, other).wait()
     total = acc[chip]
     for s in far:
         total = total + recv[s]
     tot[...] = total
-    backs = [remote(tot, out.at[me], s2.at[s], r2.at[s], to(s)) for s in far]
-    for c in backs:
-        c.start()
-    pair = [remote(tot, out.at[me], s3.at[0], r3.at[0], other)]
-    pair[0].start()
+    for s in far:
+        remote(tot, out.at[me], s2, r2, to(s)).start()
+    remote(tot, out.at[me], s3, r3, other).start()
     out[me] = total
     yield
-    for s in reversed(far):
-        there = out.at[to(s)]
-        remote(there, there, s2.at[s], r2.at[s], other).wait_recv()
-        c = remote(there, there, s3.at[s], r3.at[s], other)
-        c.start()
-        pair.append(c)
+    seven = out.at[pl.ds(0, 7)]
+    remote(seven, seven, s2, r2, other).wait()
+    for s in far:
+        remote(out.at[to(s)], out.at[to(s)], s3, r3, other).start()
     yield
-    for s in SLOTS:
-        there = out.at[2 * chip_at(chip, sign, s) + 1 - core]
-        remote(there, there, s3.at[s], r3.at[s], other).wait_recv()
-    for c in [first] + sends + backs + pair:
-        c.wait_send()
+    eight = out.at[pl.ds(0, 8)]
+    remote(eight, eight, s3, r3, other).wait()
 
 
 def drain(*steps):
@@ -531,55 +508,50 @@
     return x.astype(F32).T.astype(BF)
 
 
-def row_blocks(rows, body):
+def tower_into(rows, load, w_in, w_out, slope_ref, hid_ref, out_ref):
     def blk(i, _):
-        body(pl.ds(pl.multiple_of(i * ROW_BLK, ROW_BLK), ROW_BLK))
-        return 0
-
-    lax.fori_loop(0, rows // ROW_BLK, blk, 0)
-
-
-def tower_into(rows, load, w_in, w_out, slope_ref, hid_ref, out_ref):
-    def blk(s):
+        s = pl.ds(pl.multiple_of(i * ROW_BLK, ROW_BLK), ROW_BLK)
         act, slope = gelu_both(dot_nn(load(s), w_in[...]))
         slope_ref[s, :] = slope
         hid_ref[s, :] = act.astype(BF)
         out_ref[s, :] = dot_nn(hid_ref[s, :], w_out[...]).astype(BF)
 
-    row_blocks(rows, blk)
+        return 0
+
+    lax.fori_loop(0, rows // ROW_BLK, blk, 0)
 
 
 def start_kernel(targ_ref, targ_out, v):
-    me, core, chip, sign = place()
-    peers = [2 * chip_at(chip, sign, s) + c for s in reversed(SLOTS) for c in ((core, 1 - core) if s else (1 - core,))]
+    me, core, away, chip, sign, at = locate()
+    peers = [at(s, c) for s in reversed(SLOTS) for c in ((core, away) if s else (away,))]
     enter(peers)
     send_s, recv_s = v["sems.0"], v["sems.1"]
     targ_out[me] = targ_ref[...]
-    copies = [remote(targ_ref, targ_out.at[me], send_s.at[i], recv_s.at[i], peer) for i, peer in enumerate(peers)]
-    for c in copies:
-        c.start()
-    for c in copies:
-        c.wait()
+    for peer in peers:
+        remote(targ_ref, targ_out.at[me], send_s, recv_s, peer).start()
+    most = targ_out.at[pl.ds(0, len(peers))]
+    remote(most, most, send_s, recv_s, peers[-1]).wait()
 
 
 def start(targ, parts, cid):
     dma = pltpu.SemaphoreType.DMA
     outs = (jax.ShapeDtypeStruct((parts,) + targ.shape, I32),)
-    return kernel_call(start_kernel, "start_step", cid, outs, grouped("sems", [dma((parts - 1,)), dma((parts - 1,))]), targ)[0]
-
-
-def packed_grads(row_t, grad_t, pre_ref, hid_ref, loss, sums_ref):
+    return kernel_call(start_kernel, "start_step", cid, outs, grouped("sems", [dma, dma]), targ)[0]
+
+
+def packed_grads(row_t, grad_t, pre_ref, hid_ref, loss, part_of):
     d_in = dot_nn(row_t, pre_ref[...])
     d_out = dot_nn(grad_t, hid_ref[...]).T
-    parts = 2 * sums_ref.shape[1]
+    wide = d_in.shape[1] // LANES
+    parts = 16
     n_in, n_out = d_in.shape[0] // parts, d_out.shape[0] // parts
-    wide = d_in.shape[1] // LANES
     for dev in range(parts):
-        part = sums_ref.at[dev % 2, dev // 2]
+        part = part_of(dev)
         for c in range(wide):
             part[c * n_in:(c + 1) * n_in, :] = d_in[dev * n_in:(dev + 1) * n_in, c * LANES:(c + 1) * LANES]
         part[wide * n_in:wide * n_in + n_out, :] = d_out[dev * n_out:(dev + 1) * n_out, :]
-        part[wide * n_in + n_out:, :] = jnp.broadcast_to(loss if dev == 0 else 0.0 * loss, (8, LANES))
+        if loss is not None:
+            part[wide * n_in + n_out:, :] = jnp.broadcast_to(loss if dev == 0 else 0.0 * loss, (8, LANES))
 
 
 def unpack_grads(sums_ref, in_ref, out_ref, loss_ref):
@@ -590,74 +562,74 @@
         for c in range(wide):
             in_ref[dev, :, c * LANES:(c + 1) * LANES] = sums_ref[dev, c * n_in:(c + 1) * n_in, :]
         out_ref[dev] = sums_ref[dev, wide * n_in:wide * n_in + n_out, :]
-    loss_ref[...] = sums_ref[0, wide * n_in + n_out:, :]
-
-
-def weight_grads(row_t, grad_t, pre_ref, hid_ref, in_ref, out_ref):
-    parts, n_in, _ = in_ref.shape
-    n_out = out_ref.shape[1]
-    d_in = dot_nn(row_t, pre_ref[...])
-    d_out = dot_nn(grad_t, hid_ref[...]).T
-    for dev in range(parts):
-        in_ref[dev] = d_in[dev * n_in:(dev + 1) * n_in, :]
-        out_ref[dev] = d_out[dev * n_out:(dev + 1) * n_out, :]
-
-
-def step_kernel(x_ref, tok_ref, w1, w2, wi1, wi2, cand_ref, logq_ref, targ_ref, rows_out, di_in_out, di_out_out, dq_in_out, dq_out_out, loss_out, v):
+    if loss_ref is not None:
+        loss_ref[...] = sums_ref[0, wide * n_in + n_out:, :]
+
+
+def step_kernel(x_ref, *refs):
+    (rows_out, *outs), v = refs[8:-1], refs[-1]
+    ins = [pltpu.make_async_copy(src, v[f"in.{i}"], v["in_sem"].at[i]) for i, src in enumerate(refs[:8])]
+    for c in ins:
+        c.start()
+    tok_ref, w1, w2, wi1, wi2, cand_ref, logq_ref, targ_ref = group(v, "in")
+    di_in_out, di_out_out, dq_in_out, dq_out_out, loss_out = group(v, "out")
+    leaves = [pltpu.make_async_copy(v[f"out.{i}"], dst, v["out_sem"].at[i]) for i, dst in enumerate(outs)]
     parts, n_item, _ = x_ref.shape
     n_tok = tok_ref.shape[0]
     n_cand = n_item - n_tok
     total = float(n_tok * parts)
     scale = SCORE_GAIN / math.sqrt(LANES)
-    me, core, chip, sign = place()
-    x_chip = 2 * chip_at(chip, sign, 1)
-    diag = 2 * chip_at(chip, sign, 6) + core
-    rounds = ((me + 1 - 2 * core, x_chip + core, x_chip + 1 - core), (2 * chip_at(chip, sign, 2) + core, 2 * chip_at(chip, sign, 4) + core, diag))
-    enter([me + 1 - 2 * core, x_chip + 1 - core] + [2 * chip_at(chip, sign, s) + core for s in SLOTS[1:]])
+    me, core, away, chip, sign, at = locate()
+    other = at(0, away)
+    diag = at(6, core)
+    rounds = ((other, at(1, core), at(1, away)), (at(2, core), at(4, core), diag))
+    enter([other, at(1, away)] + [at(s, core) for s in SLOTS[1:]])
     x_mine, x_sem = v["x_mine"], v["x_sem"]
 
     def fetch(s):
-        return pltpu.make_async_copy(x_ref.at[2 * chip_at(chip, sign, s) + core], x_mine.at[s], x_sem.at[s])
-
-    def own_part(s, a):
+        return pltpu.make_async_copy(x_ref.at[at(s, core)], x_mine.at[s], x_sem.at[s])
+
+    def own_part(s):
         fetch(s).wait()
         return x_mine[s]
 
-    rs_rows = reduce_scatter_steps(lambda dev, a: x_ref.at[dev], thirds(n_item, 16), group(v, "rs"), mine=own_part)
+    rs_rows = reduce_scatter_steps(lambda dev: x_ref.at[dev], thirds(n_item, 16), group(v, "rs"), mine=own_part)
     next(rs_rows)
     for s in CORE_ORDER:
         fetch(s).start()
+    for c in ins[:3]:
+        c.wait()
     tower_into(n_tok, lambda s: tok_ref[s, :], w1, w2, v["q_slope"], v["q_hid"], v["q_vec"])
     q_all = v["q_all"]
     q_all[me] = v["q_vec"][...]
     q_send, q_recv, q_csend, q_crecv = group(v, "agq")
-    q_sent = []
 
     def q_tile(s, c):
-        return q_all.at[2 * chip_at(chip, sign, s) + c]
+        return q_all.at[at(s, c)]
 
     def q_go(s, d):
         src = v["q_vec"] if s == 0 else q_tile(s, core)
         if d:
-            c = remote(src, q_tile(s, core), q_send.at[s ^ d], q_recv.at[s ^ d], 2 * chip_at(chip, sign, d) + core)
+            c = remote(src, q_tile(s, core), q_send, q_recv.at[s ^ d], at(d, core))
         else:
-            c = remote(src, q_tile(s, core), q_csend.at[s], q_crecv.at[s], me + 1 - 2 * core)
+            c = remote(src, q_tile(s, core), q_csend, q_crecv.at[s // 4], other)
         c.start()
-        q_sent.append(c)
 
     def q_have(s, onward):
-        remote(q_tile(s, core), q_tile(s, core), q_send.at[s], q_recv.at[s], me + 1 - 2 * core).wait_recv()
+        remote(q_tile(s, core), q_tile(s, core), q_send, q_recv.at[s], other).wait_recv()
         for d in onward:
             q_go(s, d)
         q_go(s, 0)
 
-    def q_other(s):
-        there = q_tile(s, 1 - core)
-        remote(there, there, q_csend.at[s], q_crecv.at[s], me + 1 - 2 * core).wait_recv()
+    def q_other(upper):
+        four = q_all.at[pl.ds(0, 4)]
+        remote(four, four, q_csend, q_crecv.at[upper], other).wait_recv()
 
     for d in (1, 2, 4, 0):
         q_go(0, d)
     next(rs_rows)
+    for c in ins[3:]:
+        c.wait()
     n_sub = n_cand // LANES
     for r in range(n_sub):
         s = pl.ds(r * LANES, LANES)
@@ -704,25 +676,22 @@
         den_ref[pl.ds(t, 1), :] = jnp.sum(den8, axis=0, keepdims=True) + jnp.exp2(z_t - top)
         return upper
 
-    for s in (0, 1, 2, 3):
-        q_other(s)
+    q_other(0)
     lax.fori_loop(0, parts // 2, pass_one, 0)
     for s in (5, 6, 7):
         q_have(s, ())
-    for s in (4, 5, 6, 7):
-        q_other(s)
+    q_other(1)
     lax.fori_loop(0, parts // 2, pass_one, 1)
-    for c in q_sent:
-        c.wait_send()
+    for sem, tiles in ((q_send, 7), (q_csend, 8)):
+        some = q_all.at[pl.ds(0, tiles)]
+        remote(some, some, sem, q_recv.at[0], other).wait_send()
     held, got, st_send, st_recv = group(v, "st")
     held[0, 0] = top_ref[...]
     held[0, 1] = den_ref[...]
     for r, peers in enumerate(rounds):
-        copies = [remote(held.at[r], got.at[r, i], st_send.at[r, i], st_recv.at[r, i], peer) for i, peer in enumerate(peers)]
-        for c in copies:
-            c.start()
-        for c in copies:
-            c.wait()
+        for i, peer in enumerate(peers):
+            remote(held.at[r], got.at[r, i], st_send.at[r], st_recv.at[r], peer).start()
+        remote(got.at[r], got.at[r], st_send.at[r], st_recv.at[r], other).wait()
         tops = [held[r, 0]] + [got[r, i, 0] for i in range(3)]
         dens = [held[r, 1]] + [got[r, i, 1] for i in range(3)]
         top = jnp.maximum(jnp.maximum(tops[0], tops[1]), jnp.maximum(tops[2], tops[3]))
@@ -749,20 +718,15 @@
             mine[s, :] = dot_nt(i_pre[s, :], wi1[...]).astype(BF)
 
     def send_back(n, first, rows):
-        cuts = thirds(rows, 16, first)
-
-        def leave(k, s, o):
-            dev = 2 * chip_at(chip, sign, s) + (1 - core if o else core)
-            p = pl.ds(cuts[k][1], cuts[k][2])
-            return pltpu.make_async_copy(rows_v.at[dev, p, :], rows_out.at[dev, p, :], row_sem.at[3 * n + k, s, o])
-
-        for k in range(3):
-            leave(k, 0, 0).start()
-        yield from all_gather_steps(lambda a: mine, lambda dev, a: rows_v.at[dev], cuts, group(v, f"agr{n}"), landed=lambda k, s, o: leave(k, s, o).start())
-        for k in range(3):
-            for s in SLOTS:
-                for o in range(2):
-                    leave(k, s, o).wait()
+        p = pl.ds(first, rows)
+
+        def leave(dev, begin, num):
+            q = pl.ds(begin, num)
+            pltpu.make_async_copy(rows_v.at[dev, q, :], rows_out.at[dev, q, :], row_sem.at[n]).start()
+
+        leave(me, first, rows)
+        yield from all_gather_steps(mine, rows_v, thirds(rows, 16, first), group(v, f"agr{n}"), leave)
+        pltpu.make_async_copy(rows_v.at[:, p, :], rows_out.at[:, p, :], row_sem.at[n]).wait()
 
     item_back(n_cand, n_tok)
     back_t = send_back(0, n_cand, n_tok)
@@ -803,12 +767,12 @@
 
     def both(s):
         def one(c, _):
-            pass_two(2 * chip_at(chip, sign, s) + c, half)
+            pass_two(at(s, c), half)
             return 0
 
         lax.fori_loop(0, 2, one, 0)
 
-    rs_dh = reduce_scatter_steps(lambda dev, a: dh.at[dev], thirds(LANES, 8), group(v, "rsd"), produce=both)
+    rs_dh = reduce_scatter_steps(lambda dev: dh.at[dev], thirds(LANES, 8), group(v, "rsd"), produce=both)
     next(rs_dh)
     next(back_a)
     next(rs_dh)
@@ -818,33 +782,36 @@
     next(back_t)
     back_b = send_back(2, half, half)
     next(back_b)
-    weight_grads(turn(raw[...]), turn(grad[...]), i_pre, v["i_hid"], v["di_in"], v["di_out"])
+    packed_grads(turn(raw[...]), turn(grad[...]), i_pre, v["i_hid"], None, lambda dev: v["i_part"].at[dev])
     next(rs_dh)
     next(back_a)
     next(back_b)
 
-    def sum_all(name, parts_in, orders, outs):
-        pieces = [(a, 0, r.shape[1], o) for a, (r, o) in enumerate(zip(parts_in, orders))]
-        refs = group(v, name)
-        sums = [refs[3 * a + 1].at[0] for a in range(len(parts_in))]
-        first = reduce_scatter_steps(lambda dev, a: parts_in[a].at[dev], pieces, refs[:-4])
-        yield from (x for _, x in zip(range(5), first))
-        for a, out in enumerate(outs):
-            out[me] = sums[a][...]
-        yield from all_gather_steps(lambda a: sums[a], lambda dev, a: outs[a].at[dev], pieces, refs[-4:])
-        for _ in first:
-            pass
-
-    ar_i = sum_all("ai", (v["di_in"], v["di_out"]), (0, 1), (di_in_out, di_out_out))
+    def sum_items(part, out, refs):
+        first = reduce_scatter_steps(lambda dev: part.at[dev], thirds(part.shape[1], 8), refs[:-4])
+        for _ in range(5):
+            next(first)
+            yield
+        tot = refs[1].at[0]
+        out[me] = tot[...]
+        yield from all_gather_steps(tot, out, thirds(part.shape[1], 8), refs[-4:])
+        drain(first)
+
+    ar_i = sum_items(v["i_part"], v["i_sum"], group(v, "ai"))
     next(ar_i)
     next(rs_dh)
     d_query = ((dz_col * targ_vec.astype(F32) + v["rsd.1"][0].T) * scale).astype(BF)
     q_pre = v["q_pre"]
     q_pre[...] = (v["q_slope"][...] * dot_nt(d_query, w2[...])).astype(BF)
-    packed_grads(turn(tok_ref[...]), turn(d_query), q_pre, v["q_hid"], loss, v["q_part"])
+    packed_grads(turn(tok_ref[...]), turn(d_query), q_pre, v["q_hid"], loss, lambda dev: v["q_part"].at[dev % 2, dev // 2])
     ar_q = sum_direct_steps(v["q_part"], v["q_sum"], group(v, "aq"))
     drain(ar_q, ar_i, back_a, back_b, back_t, rs_dh)
+    unpack_grads(v["i_sum"], di_in_out, di_out_out, None)
     unpack_grads(v["q_sum"], dq_in_out, dq_out_out, loss_out)
+    for c in leaves:
+        c.start()
+    for c in leaves:
+        c.wait()
 
 
 def step(x, tokens, weights, cand, logq, targ, cid):
@@ -854,17 +821,17 @@
     ff = weights[0].shape[1]
     dma = pltpu.SemaphoreType.DMA
     n_in, n_out = LANES // parts, ff // parts
-    w_parts = [(n_in, ff, F32), (n_out, LANES, F32)]
-    spec = grouped("rs", rs_scratch([(n_item, LANES, BF)], 3))
-    spec += grouped("st", [pltpu.VMEM((3, 2, parts, n_tok), F32), pltpu.VMEM((2, 3, 2, parts, n_tok), F32), dma((2, 3)), dma((2, 3))])
-    spec += grouped("rsd", rs_scratch([(LANES, n_tok, F32)], 3))
+    spec = grouped("rs", rs_scratch(n_item, LANES, BF))
+    spec += grouped("st", [pltpu.VMEM((3, 2, parts, n_tok), F32), pltpu.VMEM((2, 3, 2, parts, n_tok), F32), dma((2,)), dma((2,))])
+    spec += grouped("rsd", rs_scratch(LANES, n_tok, F32))
     for n in range(3):
-        spec += grouped(f"agr{n}", ag_scratch(3))
-    spec += grouped("ai", rs_scratch(w_parts, 2) + ag_scratch(2))
-    q_rows = n_in * (ff // LANES) + n_out + 8
+        spec += grouped(f"agr{n}", ag_scratch())
+    i_rows = n_in * (ff // LANES) + n_out
+    q_rows = i_rows + 8
+    spec += grouped("ai", rs_scratch(i_rows, LANES, F32) + ag_scratch())
     spec += grouped("aq", direct_scratch(q_rows, LANES))
-    spec += grouped("agq", [dma((8,))] * 4)
-    spec += [("x_sem", dma((8,))), ("row_sem", dma((9, 8, 2)))]
+    spec += grouped("agq", [dma, dma((8,)), dma, dma((2,))])
+    spec += [("x_sem", dma((8,))), ("row_sem", dma((3,)))]
 
     def add(name, shape, dtype=F32):
         spec.append((name, pltpu.VMEM(shape, dtype)))
@@ -875,8 +842,8 @@
         add(pre + "_pre", (n, ff), BF)
         add(pre + "_vec", (n, LANES), BF)
     add("i_grad", (n_item, LANES), BF)
-    add("di_in", (parts, n_in, ff))
-    add("di_out", (parts, n_out, LANES))
+    add("i_part", (parts, i_rows, LANES))
+    add("i_sum", (parts, i_rows, LANES))
     add("q_part", (2, parts // 2, q_rows, LANES))
     add("q_sum", (parts, q_rows, LANES))
     add("x_mine", (8, n_item, LANES), BF)
@@ -892,7 +859,10 @@
     add("dh", (parts, LANES, n_tok))
     sums = (jax.ShapeDtypeStruct((parts, n_in, ff), F32), jax.ShapeDtypeStruct((parts, n_out, LANES), F32))
     outs = (jax.ShapeDtypeStruct((parts, n_item, LANES), BF),) + sums + sums + (jax.ShapeDtypeStruct((8, LANES), F32),)
-    return kernel_call(step_kernel, "softmax_step", cid, outs, spec, x, tokens, *weights, cand, logq, targ, in_hbm=(0,), out_hbm=(0,))
+    args = (tokens, *weights, cand, logq, targ)
+    spec += grouped("in", [pltpu.VMEM(a.shape, a.dtype) for a in args]) + grouped("out", [pltpu.VMEM(o.shape, o.dtype) for o in outs[1:]])
+    spec += [("in_sem", dma((8,))), ("out_sem", dma((5,)))]
+    return kernel_call(step_kernel, "softmax_step", cid, outs, spec, x, *args, in_hbm=range(9), out_hbm=range(6))
 
 
 def solution(mesh):
@@ -905,8 +875,8 @@
         targ = start(targ_loc.reshape(-1, LANES), num_dev, 1)
         owned, plist, counts = gather(table_loc, cand, targ)
         back, *sums = step(owned.reshape(num_dev, n_item, dim), tokens, (w_one, w_two, wi_one, wi_two), cand, log_q.reshape(-1, LANES), targ, 2)
-        d_table, di_in, di_out, dq_in, dq_out, loss = scatter(back.reshape(-1, dim), plist, counts, rows_loc, sums, num_dev)
+        d_table, loss, di_in, di_out, dq_in, dq_out = scatter(back.reshape(-1, dim), plist, counts, rows_loc, sums, num_dev)
         shaped = [g.reshape(w.shape) for g, w in zip((dq_in, dq_out, di_in, di_out), (w_one, w_two, wi_one, wi_two))]
-        return (loss[0, 0], d_table) + tuple(shaped)
+        return (loss.reshape(()), d_table) + tuple(shaped)
 
     return jax.shard_map(local_step, mesh=mesh, in_specs=(P("dp", None), P(), P(), P(), P(), P("dp", None), P(), P(), P("dp")), out_specs=(P(), P("dp", None), P(), P(), P(), P()), check_vma=False)

time: 147 us -> 139 us (0.946)
  Pallas kernels: 145 us -> 138 us
    pallas_call x2, Pallas kernels: 109 us -> 102 us  [kernel_call(): pl.pallas_call(kernel, out_shape=out_shape, in_specs=[HB if i in in_hbm e...]
where the time goes in v7:
time: 139 us
  Pallas kernels  138 us (99%)
    pallas_call x2, Pallas kernels, kernel_call(): pl.pallas_call(kernel, out_shape=out_shape, in_specs=[HB if i in in_hbm e...  102 us
    pallas_call x1, Pallas kernels, scatter(): pl.pallas_call(functools.partial(scatter_kernel, chunks), out_shape=(jax....  20.5 us
    pallas_call x1, Pallas kernels, gather(): pl.pallas_call(functools.partial(gather_kernel, chunks), out_shape=(jax.S...  15.9 us

profile of v7, /device:TPU:0, one launch (start us, length us, event | category | flops | bytes accessed | tf_op | source)
XLA Modules:
  0.0 139.1 jit_solution(12828292171430677281)
XLA Ops:
  0.6 8.7 %start_step.1.targ_ref.refs_8_ = s32[16,2,128]{2,1,0:T(2,128)} custom-call(s32[2,128]{1,0:T(2,128)} %bitcast.15), custom_call_target="tpu_custom_call" | custom-call | tf_op jit(solution)/shard_map/start_step/pallas_call | solution.py:468
  9.3 15.9 %gather_rows.1 = (bf16[20480,128]{1,0:T(8,128)(2,1)}, s32[160,128]{1,0:T(8,128)}, s32[2]{0:T(128)}) custom-call(s32[128,128]{1,0:T(8,128)} %bitcast.12, s32[16,2,128]{2,1,0:T(2,128)} %start_step.1.targ_ref.refs_8_, bf16[32768,128]{1,0:T(8,128)(2,1)} %table_ref.1), custom_call_target="tpu_custom_call" | custom-call | tf_op jit(solution)/shard_map/gather_rows/pallas_call | solution.py:125
  25.2 93.3 %softmax_step.1 = (bf16[16,1280,128]{2,1,0:T(8,128)(2,1)}, f32[16,8,512]{2,1,0:T(8,128)}, f32[16,32,128]{2,1,0:T(8,128)}, f32[16,8,512]{2,1,0:T(8,128)}, f32[16,32,128]{2,1,0:T(8,128)}, /*index=5*/f32[8,128]{1,0:T(8,128)}) custom-call(bf16[16,1280,128]{2,1,0:T(8,128)(2,1)} %bitcast.11, bf16[256,128]{1,0:T(8,128)(2,1)} %refs_1_.1, bf16[128,512]{1,0:T(8,128)(2,1)} %refs_2_.1, ...), custom_call_target="tpu_custom_call" | custom-call | tf_op jit(solution)/shard_map/softmax_step/pallas_call | solution.py:468
  118.5 20.5 %scatter_rows.1 = (f32[32768,128]{1,0:T(8,128)}, f32[1]{0:T(128)}, f32[16,8,512]{2,1,0:T(8,128)}, f32[16,32,128]{2,1,0:T(8,128)}, f32[16,8,512]{2,1,0:T(8,128)}, /*index=5*/f32[16,32,128]{2,1,0:T(8,128)}) custom-call(s32[2]{0:T(128)} %get-tuple-element.21.cnt_ref, s32[160,128]{1,0:T(8,128)} %get-tuple-element.22.list_ref, bf16[20480,128]{1,0:T(8,128)(2,1)} %bitcast.10, ...), custom_call_target="tpu_custom_call" | custom-call | tf_op jit(solution)/shard_map/scatter_rows/pallas_call | solution.py:236

commit v8 on v7

--- a/solution.py
+++ b/solution.py
@@ -686,24 +686,19 @@
         some = q_all.at[pl.ds(0, tiles)]
         remote(some, some, sem, q_recv.at[0], other).wait_send()
     held, got, st_send, st_recv = group(v, "st")
-    held[0, 0] = top_ref[...]
-    held[0, 1] = den_ref[...]
+    held[0] = top_ref[...] + jnp.log2(den_ref[...])
     for r, peers in enumerate(rounds):
         for i, peer in enumerate(peers):
             remote(held.at[r], got.at[r, i], st_send.at[r], st_recv.at[r], peer).start()
         remote(got.at[r], got.at[r], st_send.at[r], st_recv.at[r], other).wait()
-        tops = [held[r, 0]] + [got[r, i, 0] for i in range(3)]
-        dens = [held[r, 1]] + [got[r, i, 1] for i in range(3)]
-        top = jnp.maximum(jnp.maximum(tops[0], tops[1]), jnp.maximum(tops[2], tops[3]))
-        held[r + 1, 0] = top
-        held[r + 1, 1] = sum(d * jnp.exp2(m - top) for m, d in zip(tops, dens))
-    norm = v["norm"]
-    norm[...] = held[2, 0] + jnp.log2(held[2, 1] * total)
-    top_ref[...] = held[2, 0]
-    den_ref[...] = held[2, 1]
-    lse = top_ref[own, :] + jnp.log2(den_ref[own, :])
+        logs = [held[r]] + [got[r, i] for i in range(len(peers))]
+        top = functools.reduce(jnp.maximum, logs)
+        held[r + 1] = top + jnp.log2(sum(jnp.exp2(x - top) for x in logs))
+    lse_ref, norm = held.at[len(rounds)], v["norm"]
+    norm[...] = lse_ref[...] + math.log2(total)
+    lse = lse_ref[own, :]
     loss = jnp.sum(lse - z_own, axis=1, keepdims=True) * (1.0 / (LOG2E * total))
-    dz_row = ((jnp.exp2(z_own - top_ref[own, :]) / den_ref[own, :] - 1.0) * (1.0 / total)).astype(BF).astype(F32)
+    dz_row = ((jnp.exp2(z_own - lse) - 1.0) * (1.0 / total)).astype(BF).astype(F32)
     dz_col = jnp.sum(jnp.where(eye, dz_row, 0.0), axis=1, keepdims=True)
     grad = v["i_grad"]
     grad[pl.ds(n_cand, n_tok), :] = (scale * dz_col * q_own.astype(F32)).astype(BF)
@@ -736,76 +731,48 @@
     vec_t[...] = turn(vec[:n_cand, :])
     d_acc, dz_s, dh = v["d_acc"], v["dz"], v["dh"]
     d_acc[...] = jnp.zeros_like(d_acc)
-    half = n_cand // 2
-
-    def pass_two(t, first):
+
+    def pass_two(t):
         shift = norm[pl.ds(t, 1), :]
-        for j in range(half // COL_BLK):
-            dz_s[pl.ds(j * COL_BLK, COL_BLK), :] = jnp.exp2(z_ref[t, pl.ds(first + j * COL_BLK, COL_BLK), :] - shift).astype(BF)
-        d_acc[pl.ds(first, half), :] += dot_nn(dz_s[...], q_all[t])
-        part = dot_nn(vec_t[:, first:first + half], dz_s[...])
-        dh[t] = part if first == 0 else dh[t] + part
-
-    def upper_half(t, _):
-        pass_two(t, 0)
-        return 0
-
-    def cand_back(first):
-        grad[pl.ds(first, half), :] = (d_acc[pl.ds(first, half), :] * scale).astype(BF)
-        item_back(first, half)
-
-    lax.fori_loop(0, parts // 2, upper_half, 0)
-    next(back_t)
-    next(back_t)
-    lax.fori_loop(parts // 2, parts, upper_half, 0)
-    next(back_t)
-    cand_back(0)
-    next(back_t)
-    back_a = send_back(1, 0, half)
-    for _ in range(3):
-        next(back_a)
+        for j in range(n_cand // COL_BLK):
+            s = pl.ds(j * COL_BLK, COL_BLK)
+            dz_s[s, :] = jnp.exp2(z_ref[t, s, :] - shift).astype(BF)
+        d_acc[...] += dot_nn(dz_s[...], q_all[t])
+        dh[t] = dot_nn(vec_t[...], dz_s[...])
 
     def both(s):
         def one(c, _):
-            pass_two(at(s, c), half)
+            pass_two(at(s, c))
             return 0
 
         lax.fori_loop(0, 2, one, 0)
+        if s not in CORE_ORDER[:2]:
+            next(back_t, None)
 
     rs_dh = reduce_scatter_steps(lambda dev: dh.at[dev], thirds(LANES, 8), group(v, "rsd"), produce=both)
     next(rs_dh)
-    next(back_a)
     next(rs_dh)
-    cand_back(half)
+    grad[pl.ds(0, n_cand), :] = (d_acc[...] * scale).astype(BF)
+    item_back(0, n_cand)
     next(rs_dh)
-    next(back_a)
-    next(back_t)
-    back_b = send_back(2, half, half)
-    next(back_b)
-    packed_grads(turn(raw[...]), turn(grad[...]), i_pre, v["i_hid"], None, lambda dev: v["i_part"].at[dev])
+    back_c = send_back(1, 0, n_cand)
+    next(back_c)
+    packed_grads(turn(raw[...]), turn(grad[...]), i_pre, v["i_hid"], None, lambda dev: v["i_part"].at[dev % 2, dev // 2])
     next(rs_dh)
-    next(back_a)
-    next(back_b)
-
-    def sum_items(part, out, refs):
-        first = reduce_scatter_steps(lambda dev: part.at[dev], thirds(part.shape[1], 8), refs[:-4])
-        for _ in range(5):
-            next(first)
-            yield
-        tot = refs[1].at[0]
-        out[me] = tot[...]
-        yield from all_gather_steps(tot, out, thirds(part.shape[1], 8), refs[-4:])
-        drain(first)
-
-    ar_i = sum_items(v["i_part"], v["i_sum"], group(v, "ai"))
+    next(back_c)
+    ar_i = sum_direct_steps(v["i_part"], v["i_sum"], group(v, "ai"))
+    next(back_c)
     next(ar_i)
     next(rs_dh)
+    next(ar_i)
+    next(back_c)
+    next(back_c)
     d_query = ((dz_col * targ_vec.astype(F32) + v["rsd.1"][0].T) * scale).astype(BF)
     q_pre = v["q_pre"]
     q_pre[...] = (v["q_slope"][...] * dot_nt(d_query, w2[...])).astype(BF)
     packed_grads(turn(tok_ref[...]), turn(d_query), q_pre, v["q_hid"], loss, lambda dev: v["q_part"].at[dev % 2, dev // 2])
     ar_q = sum_direct_steps(v["q_part"], v["q_sum"], group(v, "aq"))
-    drain(ar_q, ar_i, back_a, back_b, back_t, rs_dh)
+    drain(ar_q, ar_i, back_c, back_t, rs_dh)
     unpack_grads(v["i_sum"], di_in_out, di_out_out, None)
     unpack_grads(v["q_sum"], dq_in_out, dq_out_out, loss_out)
     for c in leaves:
@@ -822,16 +789,16 @@
     dma = pltpu.SemaphoreType.DMA
     n_in, n_out = LANES // parts, ff // parts
     spec = grouped("rs", rs_scratch(n_item, LANES, BF))
-    spec += grouped("st", [pltpu.VMEM((3, 2, parts, n_tok), F32), pltpu.VMEM((2, 3, 2, parts, n_tok), F32), dma((2,)), dma((2,))])
+    spec += grouped("st", [pltpu.VMEM((3, parts, n_tok), F32), pltpu.VMEM((2, 3, parts, n_tok), F32), dma((2,)), dma((2,))])
     spec += grouped("rsd", rs_scratch(LANES, n_tok, F32))
-    for n in range(3):
+    for n in range(2):
         spec += grouped(f"agr{n}", ag_scratch())
     i_rows = n_in * (ff // LANES) + n_out
     q_rows = i_rows + 8
-    spec += grouped("ai", rs_scratch(i_rows, LANES, F32) + ag_scratch())
+    spec += grouped("ai", direct_scratch(i_rows, LANES))
     spec += grouped("aq", direct_scratch(q_rows, LANES))
     spec += grouped("agq", [dma, dma((8,)), dma, dma((2,))])
-    spec += [("x_sem", dma((8,))), ("row_sem", dma((3,)))]
+    spec += [("x_sem", dma((8,))), ("row_sem", dma((2,)))]
 
     def add(name, shape, dtype=F32):
         spec.append((name, pltpu.VMEM(shape, dtype)))
@@ -842,7 +809,7 @@
         add(pre + "_pre", (n, ff), BF)
         add(pre + "_vec", (n, LANES), BF)
     add("i_grad", (n_item, LANES), BF)
-    add("i_part", (parts, i_rows, LANES))
+    add("i_part", (2, parts // 2, i_rows, LANES))
     add("i_sum", (parts, i_rows, LANES))
     add("q_part", (2, parts // 2, q_rows, LANES))
     add("q_sum", (parts, q_rows, LANES))
@@ -855,7 +822,7 @@
     for name in ("top", "den", "norm", "own"):
         add(name, (parts, n_tok))
     add("vec_t", (LANES, n_cand), BF)
-    add("dz", (n_cand // 2, n_tok), BF)
+    add("dz", (n_cand, n_tok), BF)
     add("dh", (parts, LANES, n_tok))
     sums = (jax.ShapeDtypeStruct((parts, n_in, ff), F32), jax.ShapeDtypeStruct((parts, n_out, LANES), F32))
     outs = (jax.ShapeDtypeStruct((parts, n_item, LANES), BF),) + sums + sums + (jax.ShapeDtypeStruct((8, LANES), F32),)

time: 139 us -> 136 us (0.978)
  Pallas kernels: 138 us -> 135 us
    pallas_call x2, Pallas kernels: 102 us -> 98.2 us  [kernel_call(): pl.pallas_call(kernel, out_shape=out_shape, in_specs=[HB if i in in_hbm e...]
where the time goes in v8:
time: 136 us
  Pallas kernels  135 us (99%)
    pallas_call x2, Pallas kernels, kernel_call(): pl.pallas_call(kernel, out_shape=out_shape, in_specs=[HB if i in in_hbm e...  98.2 us
    pallas_call x1, Pallas kernels, scatter(): pl.pallas_call(functools.partial(scatter_kernel, chunks), out_shape=(jax....  20.7 us
    pallas_call x1, Pallas kernels, gather(): pl.pallas_call(functools.partial(gather_kernel, chunks), out_shape=(jax.S...  16.1 us

profile of v8, /device:TPU:0, one launch (start us, length us, event | category | flops | bytes accessed | tf_op | source)
XLA Modules:
  0.0 135.6 jit_solution(9893571070055672600)
XLA Ops:
  0.6 8.7 %start_step.1.targ_ref.refs_8_ = s32[16,2,128]{2,1,0:T(2,128)} custom-call(s32[2,128]{1,0:T(2,128)} %bitcast.15), custom_call_target="tpu_custom_call" | custom-call | tf_op jit(solution)/shard_map/start_step/pallas_call | solution.py:468
  9.3 16.1 %gather_rows.1 = (bf16[20480,128]{1,0:T(8,128)(2,1)}, s32[160,128]{1,0:T(8,128)}, s32[2]{0:T(128)}) custom-call(s32[128,128]{1,0:T(8,128)} %bitcast.12, s32[16,2,128]{2,1,0:T(2,128)} %start_step.1.targ_ref.refs_8_, bf16[32768,128]{1,0:T(8,128)(2,1)} %table_ref.1), custom_call_target="tpu_custom_call" | custom-call | tf_op jit(solution)/shard_map/gather_rows/pallas_call | solution.py:125
  25.4 89.5 %softmax_step.1 = (bf16[16,1280,128]{2,1,0:T(8,128)(2,1)}, f32[16,8,512]{2,1,0:T(8,128)}, f32[16,32,128]{2,1,0:T(8,128)}, f32[16,8,512]{2,1,0:T(8,128)}, f32[16,32,128]{2,1,0:T(8,128)}, /*index=5*/f32[8,128]{1,0:T(8,128)}) custom-call(bf16[16,1280,128]{2,1,0:T(8,128)(2,1)} %bitcast.11, bf16[256,128]{1,0:T(8,128)(2,1)} %refs_1_.1, bf16[128,512]{1,0:T(8,128)(2,1)} %refs_2_.1, ...), custom_call_target="tpu_custom_call" | custom-call | tf_op jit(solution)/shard_map/softmax_step/pallas_call | solution.py:468
  114.9 20.7 %scatter_rows.1 = (f32[32768,128]{1,0:T(8,128)}, f32[1]{0:T(128)}, f32[16,8,512]{2,1,0:T(8,128)}, f32[16,32,128]{2,1,0:T(8,128)}, f32[16,8,512]{2,1,0:T(8,128)}, /*index=5*/f32[16,32,128]{2,1,0:T(8,128)}) custom-call(s32[2]{0:T(128)} %get-tuple-element.21.cnt_ref, s32[160,128]{1,0:T(8,128)} %get-tuple-element.22.list_ref, bf16[20480,128]{1,0:T(8,128)(2,1)} %bitcast.10, ...), custom_call_target="tpu_custom_call" | custom-call | tf_op jit(solution)/shard_map/scatter_rows/pallas_call | solution.py:236

commit v9 on v8

--- a/solution.py
+++ b/solution.py
@@ -54,7 +54,7 @@
     return jnp.where(flat < total, val, nr * LANES * 32768), own, total
 
 
-def gather_kernel(chunks, cand_ref, targ_ref, table_ref, out_ref, list_ref, cnt_ref, ids_ref, stage, tab, dense, plist, packed_rows, sem, psem, osem):
+def gather_kernel(chunks, cand_ref, targ_ref, table_ref, out_ref, list_out, cnt_ref, list_ref, ids_ref, stage, tab, dense, plist, packed_rows, sem, psem, osem, lsem):
     rows = tab.shape[0]
     npos = out_ref.shape[0]
     cr = rows // chunks
@@ -76,6 +76,8 @@
     cnt_ref[1] = total
     to_smem = pltpu.make_async_copy(list_ref, plist, psem)
     to_smem.start()
+    to_hbm = pltpu.make_async_copy(list_ref, list_out, lsem)
+    to_hbm.start()
 
     def zero(i, _):
         dense[pl.ds(pl.multiple_of(i * BLK, BLK), BLK), :] = jnp.zeros((BLK, LANES), F32)
@@ -115,6 +117,7 @@
         leave(d).start()
     for d in range(parts):
         leave(d).wait()
+    to_hbm.wait()
 
 
 def gather(table, cand, targ):
@@ -126,8 +129,8 @@
         functools.partial(gather_kernel, chunks),
         out_shape=(jax.ShapeDtypeStruct((npos, LANES), BF), jax.ShapeDtypeStruct((nr, LANES), I32), jax.ShapeDtypeStruct((2,), I32)),
         in_specs=[VM, VM, HB],
-        out_specs=(HB, VM, SM),
-        scratch_shapes=[pltpu.VMEM((nr, LANES), I32), pltpu.VMEM((rows, LANES), BF), pltpu.VMEM((rows, LANES), F32), pltpu.VMEM((npos + 8, LANES), F32), pltpu.SMEM((nr, LANES), I32), pltpu.VMEM((npos, LANES), BF), pltpu.SemaphoreType.DMA((chunks,)), pltpu.SemaphoreType.DMA, pltpu.SemaphoreType.DMA((targ.shape[0],))],
+        out_specs=(HB, HB, SM),
+        scratch_shapes=[pltpu.VMEM((nr, LANES), I32), pltpu.VMEM((nr, LANES), I32), pltpu.VMEM((rows, LANES), BF), pltpu.VMEM((rows, LANES), F32), pltpu.VMEM((npos + 8, LANES), F32), pltpu.SMEM((nr, LANES), I32), pltpu.VMEM((npos, LANES), BF), pltpu.SemaphoreType.DMA((chunks,)), pltpu.SemaphoreType.DMA, pltpu.SemaphoreType.DMA((targ.shape[0],)), pltpu.SemaphoreType.DMA],
         compiler_params=pltpu.CompilerParams(vmem_limit_bytes=VMEM_CAP),
         name="gather_rows",
     )(cand, targ, table)
@@ -486,7 +489,7 @@
 GELU_C = math.sqrt(2.0 / math.pi)
 GELU_A = 0.044715
 ROW_BLK = 256
-COL_BLK = 128
+COL_BLK = 256
 
 
 def gelu_both(x):
@@ -772,11 +775,18 @@
     q_pre[...] = (v["q_slope"][...] * dot_nt(d_query, w2[...])).astype(BF)
     packed_grads(turn(tok_ref[...]), turn(d_query), q_pre, v["q_hid"], loss, lambda dev: v["q_part"].at[dev % 2, dev // 2])
     ar_q = sum_direct_steps(v["q_part"], v["q_sum"], group(v, "aq"))
-    drain(ar_q, ar_i, back_c, back_t, rs_dh)
+    for _ in range(4):
+        for g in (ar_q, ar_i, back_c):
+            next(g, None)
+    drain(ar_i)
     unpack_grads(v["i_sum"], di_in_out, di_out_out, None)
+    for c in leaves[:2]:
+        c.start()
+    drain(ar_q)
     unpack_grads(v["q_sum"], dq_in_out, dq_out_out, loss_out)
-    for c in leaves:
+    for c in leaves[2:]:
         c.start()
+    drain(back_c, back_t, rs_dh)
     for c in leaves:
         c.wait()
 

time: 136 us -> 135 us (level)
  no operation moved by 1% of the time
where the time goes in v9:
time: 135 us
  Pallas kernels  134 us (99%)
    pallas_call x2, Pallas kernels, kernel_call(): pl.pallas_call(kernel, out_shape=out_shape, in_specs=[HB if i in in_hbm e...  98.2 us
    pallas_call x1, Pallas kernels, scatter(): pl.pallas_call(functools.partial(scatter_kernel, chunks), out_shape=(jax....  20.5 us
    pallas_call x1, Pallas kernels, gather(): pl.pallas_call(functools.partial(gather_kernel, chunks), out_shape=(jax.S...  15.8 us

profile of v9, /device:TPU:0, one launch (start us, length us, event | category | flops | bytes accessed | tf_op | source)
XLA Modules:
  0.0 135.1 jit_solution(8856378029841339693)
XLA Ops:
  0.6 8.7 %start_step.1.targ_ref.refs_8_ = s32[16,2,128]{2,1,0:T(2,128)} custom-call(s32[2,128]{1,0:T(2,128)} %bitcast.15), custom_call_target="tpu_custom_call" | custom-call | tf_op jit(solution)/shard_map/start_step/pallas_call | solution.py:471
  9.3 15.8 %gather_rows.1 = (bf16[20480,128]{1,0:T(8,128)(2,1)}, s32[160,128]{1,0:T(8,128)}, s32[2]{0:T(128)}) custom-call(s32[128,128]{1,0:T(8,128)} %bitcast.12, s32[16,2,128]{2,1,0:T(2,128)} %start_step.1.targ_ref.refs_8_, bf16[32768,128]{1,0:T(8,128)(2,1)} %table_ref.1), custom_call_target="tpu_custom_call" | custom-call | tf_op jit(solution)/shard_map/gather_rows/pallas_call | solution.py:128
  25.1 89.5 %softmax_step.1 = (bf16[16,1280,128]{2,1,0:T(8,128)(2,1)}, f32[16,8,512]{2,1,0:T(8,128)}, f32[16,32,128]{2,1,0:T(8,128)}, f32[16,8,512]{2,1,0:T(8,128)}, f32[16,32,128]{2,1,0:T(8,128)}, /*index=5*/f32[8,128]{1,0:T(8,128)}) custom-call(bf16[16,1280,128]{2,1,0:T(8,128)(2,1)} %bitcast.11, bf16[256,128]{1,0:T(8,128)(2,1)} %refs_1_.1, bf16[128,512]{1,0:T(8,128)(2,1)} %refs_2_.1, ...), custom_call_target="tpu_custom_call" | custom-call | tf_op jit(solution)/shard_map/softmax_step/pallas_call | solution.py:471
  114.6 20.5 %scatter_rows.1 = (f32[32768,128]{1,0:T(8,128)}, f32[1]{0:T(128)}, f32[16,8,512]{2,1,0:T(8,128)}, f32[16,32,128]{2,1,0:T(8,128)}, f32[16,8,512]{2,1,0:T(8,128)}, /*index=5*/f32[16,32,128]{2,1,0:T(8,128)}) custom-call(s32[2]{0:T(128)} %get-tuple-element.21.cnt_ref, s32[160,128]{1,0:T(8,128)} %get-tuple-element.22.list_ref, bf16[20480,128]{1,0:T(8,128)(2,1)} %bitcast.10, ...), custom_call_target="tpu_custom_call" | custom-call | tf_op jit(solution)/shard_map/scatter_rows/pallas_call | solution.py:239
